TPU v7x, 768 devices: a whole 4x8x12 slice. The times are simulated.
768 devices in a mesh: replica: 8 (over x, core), fsdp: 24 (over y_lo, z), tensor: 4 (over y_hi).
Axes of the slice: x: 4, y: 8 (y_hi: 4, y_lo: 2; y = y_hi * 2 + y_lo), z: 12, core: 2. Of those that a mesh axis runs over, the one named last changes fastest.
Arguments:
- pseudo_grad: bfloat16 [8, 3072, 18432], P('replica', 'fsdp', 'tensor'), may hold values from -6 to 6
- compensation: float32 [8, 3072, 18432], P('replica', 'fsdp', 'tensor'), may hold values from -6 to 6
- params: float32 [3072, 18432], P(('fsdp', 'replica'), 'tensor'), may hold values from -6 to 6
- momentum: float32 [3072, 18432], P(('fsdp', 'replica'), 'tensor'), may hold values from -6 to 6
- probe: bfloat16 [1536, 18432], P('fsdp', 'tensor'), may hold values from -0.046875 to 0.046875
Outputs:
- new_params: float32 [3072, 18432], P(('fsdp', 'replica'), 'tensor')
- new_momentum: float32 [3072, 18432], P(('fsdp', 'replica'), 'tensor')
- probe_out: bfloat16 [1536, 3072], P('tensor', 'fsdp')
All inputs are finite; a program needn't handle non-finite values.
Results may differ from a plain program's by a relative error of at most 0.014.
Values may be sent and summed in bfloat16 or wider, within the bound.
A program may use at most 64 MiB of HBM per device.

v0:
```python
import jax
import jax.numpy as jnp
from jax import lax
from jax.sharding import PartitionSpec as P

outer_rate = 0.7
nesterov = 0.9


def split_up(x, dim, size):
    shape = x.shape
    tiles = x.reshape(*shape[:dim], size, shape[dim] // size, *shape[dim + 1 :])
    return jnp.moveaxis(tiles, dim, 0)


def summed_on_arrival(x, axis, dim):
    tiles = split_up(x, dim, lax.axis_size(axis))
    arrived = lax.all_to_all(tiles, axis, split_axis=0, concat_axis=0, tiled=True)
    return arrived.astype(jnp.float32).sum(axis=0)


def sent_to_all(x, axis):
    copies = jnp.broadcast_to(x, (lax.axis_size(axis), *x.shape))
    return lax.all_to_all(copies, axis, split_axis=0, concat_axis=0, tiled=True)


def in_order(tiles, dim):
    shape = list(tiles.shape[1:])
    shape[dim] *= tiles.shape[0]
    return jnp.moveaxis(tiles, 0, dim).reshape(shape)


def gathered_copies(x, axis, dim):
    tiles = sent_to_all(x, axis)
    return in_order(tiles, dim)


def per_device(pseudo_grad, compensation, params, momentum, probe):
    outgoing = (pseudo_grad[0].astype(jnp.float32) + compensation[0]).astype(jnp.bfloat16)
    summed = summed_on_arrival(outgoing, "replica", 0)
    average = summed / lax.axis_size("replica")
    new_momentum = nesterov * momentum + average
    new_params = params - outer_rate * (average + nesterov * new_momentum)
    weights = new_params.astype(jnp.bfloat16)
    local_weights = gathered_copies(weights, "replica", 0)
    workers = lax.axis_size("replica")
    strided = probe.reshape(probe.shape[0] // workers, workers, probe.shape[1])
    picked = lax.dynamic_slice_in_dim(strided, lax.axis_index("replica"), 1, 1)
    source_rows = picked.reshape(probe.shape[0] // workers, probe.shape[1])
    partial_value = lax.dot_general(
        lax.all_gather(source_rows, "fsdp", axis=0, tiled=True),
        local_weights,
        (((1,), (1,)), ((), ())),
        preferred_element_type=jnp.float32,
    )
    chosen_part = summed_on_arrival(partial_value.astype(jnp.bfloat16), "tensor", 0).astype(
        jnp.bfloat16
    )
    joined = gathered_copies(chosen_part, "replica", 0)
    block_rows = chosen_part.shape[0]
    width = chosen_part.shape[1]
    probe_out = (
        joined.reshape(workers, block_rows, width)
        .transpose(1, 0, 2)
        .reshape(workers * block_rows, width)
    )
    return (new_params, new_momentum, probe_out)


def solution(mesh):
    in_specs = (
        P("replica", "fsdp", "tensor"),
        P("replica", "fsdp", "tensor"),
        P(("fsdp", "replica"), "tensor"),
        P(("fsdp", "replica"), "tensor"),
        P("fsdp", "tensor"),
    )
    out_specs = (
        P(("fsdp", "replica"), "tensor"),
        P(("fsdp", "replica"), "tensor"),
        P("tensor", "fsdp"),
    )
    return jax.shard_map(
        per_device, mesh=mesh, in_specs=in_specs, out_specs=out_specs, check_vma=False
    )
```

profile of v0, /device:TPU:1, one launch (start us, length us, event | category | flops | bytes accessed | tf_op | source)
XLA Modules:
  0.0 165.9 jit_solution(863678869579234715)
XLA Ops:
  7.2 0.0 copy-start
  7.2 3.2 %add_convert_fusion = bf16[1,128,4608]{2,1,0:T(8,128)(2,1)} fusion(f32[1,128,4608]{2,1,0:T(8,128)} %param.6, bf16[1,128,4608]{2,1,0:T(8,128)(2,1)} %param.5), kind=kLoop, calls=%fused_computation.1 | loop fusion | flops 1769472 | bytes 4718592 | tf_op jit(solution)/shard_map/convert_element_type | solution.py:39
  10.4 13.9 %all-to-all-start = ((bf16[8,16,4608]{2,1,0:T(8,128)(2,1)}), bf16[8,16,4608]{2,1,0:T(8,128)(2,1)S(1)}, u32[]{:S(2)}, u32[]{:S(2)}) async-start(bf16[8,16,4608]{2,1,0:T(8,128)(2,1)} %bitcast), calls=%async_computation | async-start | bytes 2359296 | tf_op jit(solution)/shard_map/all_to_all | solution.py:18
  24.4 0.0 copy-start.1
  24.4 0.0 copy-start.2
  24.4 0.0 all-gather.3.cloned.1.call-start
  24.4 0.0 copy-done
  24.4 0.2 constant_dynamic-slice_fusion
  24.6 0.6 copy.9
  25.2 0.0 all-gather.3.cloned.1.call-update
  25.3 15.5 %all-to-all-done = bf16[8,16,4608]{2,1,0:T(8,128)(2,1)S(1)} async-done(((bf16[8,16,4608]{2,1,0:T(8,128)(2,1)}), bf16[8,16,4608]{2,1,0:T(8,128)(2,1)S(1)}, u32[]{:S(2)}, u32[]{:S(2)}) %all-to-all-start) | async-done | bytes 1179680 | tf_op jit(solution)/shard_map/all_to_all | solution.py:18
  40.8 0.2 convert_reduce_fusion
  40.9 0.0 copy-done.1
  40.9 0.0 copy-done.2
  40.9 0.9 fusion.5
  41.8 0.1 broadcast_in_dim.6
  41.9 19.9 %all_to_all.20 = bf16[8,16,4608]{2,1,0:T(8,128)(2,1)S(1)} all-to-all(bf16[8,16,4608]{2,1,0:T(8,128)(2,1)S(1)} %broadcast_in_dim.6), channel_id=1, replica_groups=mesh['replica'=8,'fsdp'=24,'tensor'=4] {'replica'}, dimensions={0} | all-to-all | bytes 2359296 | tf_op jit(solution)/shard_map/all_to_all | solution.py:24
  61.8 54.6 %all-gather.3.cloned.1.call-done = bf16[192,1,4608]{2,0,1:T(8,128)(2,1)} async-done(((bf16[8,1,4608]{2,0,1:T(8,128)(2,1)}), bf16[192,1,4608]{2,0,1:T(8,128)(2,1)}) %all-gather.3.cloned.1.call-update) | async-done | bytes 1769488 | tf_op jit(solution)/shard_map/all_gather | solution.py:51
  116.4 2.1 %fusion.2 = bf16[192,128]{1,0:T(8,128)(2,1)S(1)} fusion(bf16[128,4608]{1,0:T(8,128)(2,1)S(1)} %bitcast.16, bf16[192,1,4608]{2,0,1:T(8,128)(2,1)} %all-gather.3.cloned.1.call-done), kind=kOutput, calls=%fused_computation.4 | convolution fusion | flops 226516992 | bytes 2998272 | tf_op jit(solution)/shard_map/dot_general | solution.py:50
  118.5 12.5 %all_to_all.21 = bf16[4,48,128]{2,1,0:T(8,128)(2,1)S(1)} all-to-all(bf16[4,48,128]{2,1,0:T(8,128)(2,1)S(1)} %bitcast.17), channel_id=1, replica_groups=mesh['replica'=8,'fsdp'=24,'tensor'=4] {'tensor'}, dimensions={0} | all-to-all | bytes 98304 | tf_op jit(solution)/shard_map/all_to_all | solution.py:18
  131.0 27.3 %all_to_all.22 = bf16[8,48,128]{2,1,0:T(8,128)(2,1)S(1)} all-to-all(bf16[8,48,128]{2,1,0:T(8,128)(2,1)S(1)} %broadcast_in_dim.7), channel_id=1, replica_groups=mesh['replica'=8,'fsdp'=24,'tensor'=4] {'replica'}, dimensions={0} | all-to-all | bytes 196608 | tf_op jit(solution)/shard_map/all_to_all | solution.py:24
  158.4 0.7 copy.12
  (2 shorter events, 0.0 us)
Async XLA Ops:
  7.2 17.3 %copy-start = (bf16[64,4608]{1,0:T(8,128)(2,1)S(1)}, bf16[64,4608]{1,0:T(8,128)(2,1)}, u32[]{:S(2)}) copy-start(bf16[64,4608]{1,0:T(8,128)(2,1)} %param.9) | copy-start | bytes 1769476
  10.4 30.3 %all-to-all-start = ((bf16[8,16,4608]{2,1,0:T(8,128)(2,1)}), bf16[8,16,4608]{2,1,0:T(8,128)(2,1)S(1)}, u32[]{:S(2)}, u32[]{:S(2)}) async-start(bf16[8,16,4608]{2,1,0:T(8,128)(2,1)} %bitcast), calls=%async_computation | async-start | bytes 2359296 | tf_op jit(solution)/shard_map/all_to_all | solution.py:18
  24.4 16.6 %copy-start.1 = (f32[16,4608]{1,0:T(8,128)S(1)}, f32[16,4608]{1,0:T(8,128)}, u32[]{:S(2)}) copy-start(f32[16,4608]{1,0:T(8,128)} %param.7) | copy-start | bytes 884740
  24.4 16.6 %copy-start.2 = (f32[16,4608]{1,0:T(8,128)S(1)}, f32[16,4608]{1,0:T(8,128)}, u32[]{:S(2)}) copy-start(f32[16,4608]{1,0:T(8,128)} %param.8) | copy-start | bytes 884740
  24.4 92.0 %all-gather.3.cloned.1.call-start = ((), (), s32[]{:S(2)}) async-start(), calls=%async_computation.4 | async-start | bytes 1843200 | tf_op jit(solution)/shard_map/all_gather | solution.py:51
Sparse Core Ops, SparseCore 0:
  28.1 88.2 all-gather.2
where the time goes:
time: 166 us
  waiting for transfers between devices  70.1 us (42%)
  blocking collectives  59.7 us (36%)
  between operations  14.1 us (8%)
  starting transfers between devices  14 us (8%)
  other arithmetic  4.3 us (3%)
  matrix products  2.09 us (1%)
    all_gather x1, waiting for transfers between devices, per_device(): lax.all_gather(source_rows, 'fsdp', axis=0, tiled=True)  54.6 us
    all_to_all x2, blocking collectives, sent_to_all(): return lax.all_to_all(copies, axis, split_axis=0, concat_axis=0, tiled=True)  47.2 us
    all_to_all x1, waiting for transfers between devices, summed_on_arrival(): lax.all_to_all(tiles, axis, split_axis=0, concat_axis=0, tiled=True)  15.5 us
    all_to_all x1, starting transfers between devices, summed_on_arrival(): lax.all_to_all(tiles, axis, split_axis=0, concat_axis=0, tiled=True)  13.9 us
    all_to_all x1, blocking collectives, summed_on_arrival(): lax.all_to_all(tiles, axis, split_axis=0, concat_axis=0, tiled=True)  12.5 us
  transfers between devices with their start and end apart: 2, of which 2 were waited for; matrix products, arithmetic and copies ran while one was open for 1% of the time, Pallas kernels for 0%

commit v1 on v0

v1 whole, which is shorter than its diff:
```python
import jax
import jax.numpy as jnp
from jax import lax
from jax.experimental import pallas as pl
from jax.experimental.pallas import tpu as pltpu
from jax.sharding import PartitionSpec as P

MESH = pl.DeviceIdType.MESH
RATE = 0.7
NEST = 0.9
F32, BF16 = jnp.float32, jnp.bfloat16

NX, NY, NZ = 4, 8, 12
K = 4608
KC = K // 4
ORDER = (("O", 0), ("P", 0), ("P", 1), ("O", 1))
N_SEM = 192


class Keys:
    def __init__(self):
        self.at = {}

    def __call__(self, *key):
        return self.at.setdefault(key, len(self.at))


def kernel(
    pg_hbm, comp_hbm, prm_hbm, mom_hbm, probe_hbm,
    new_prm_hbm, new_mom_hbm, out_hbm,
    v_pg, v_comp, out_s, cs, r_opp, r_fin, t_acc, prm, mom, q_s, sum_s,
    w, wy, pb, b_send, part, y_in, outb, n_prm, n_mom,
    send_sem, recv_sem, loc_sem,
):
    rep = lax.axis_index("replica")
    fs = lax.axis_index("fsdp")
    t = lax.axis_index("tensor")
    x, core = rep // 2, rep % 2
    lo, z = fs // NZ, fs % NZ
    y = t * 2 + lo

    def dev(x_, core_, y_, z_):
        return (x_ * 2 + core_, (y_ % 2) * NZ + z_, y_ // 2)

    def xat(d):
        return lax.rem(x + d + NX, NX)

    def yat(d):
        return lax.rem(y + d + NY, NY)

    def zat(d):
        return lax.rem(z + d + NZ, NZ)

    rk, sk, lk = Keys(), Keys(), Keys()
    pending = []

    def send(src, dst, key, to, n=0):
        cp = pltpu.make_async_remote_copy(
            src_ref=src, dst_ref=dst, send_sem=send_sem.at[sk(key, to_name(key), n)],
            recv_sem=recv_sem.at[rk(key)], device_id=to, device_id_type=MESH,
        )
        cp.start()
        pending.append(cp)

    def to_name(key):
        return key

    def arrived(dst, key):
        pltpu.make_async_remote_copy(
            src_ref=dst, dst_ref=dst, send_sem=send_sem.at[0], recv_sem=recv_sem.at[rk(key)],
            device_id=dev(x, core, y, z), device_id_type=MESH,
        ).wait_recv()

    def local(src, dst, key):
        cp = pltpu.make_async_copy(src, dst, loc_sem.at[lk(key)])
        cp.start()
        return cp

    def koff(kind, kc):
        half = lo if kind == "O" else 1 - lo
        return pl.multiple_of((half * 2 + kc) * KC, KC)

    loads = []
    for i, (kind, kc) in enumerate(ORDER):
        at = pl.ds(koff(kind, kc), KC)
        loads.append(
            (
                local(pg_hbm.at[:, :, at], v_pg.at[i], ("pg", i)),
                local(comp_hbm.at[:, :, at], v_comp.at[i], ("comp", i)),
            )
        )
    load_prm = local(prm_hbm, prm, "prm")
    load_mom = local(mom_hbm, mom, "mom")

    barrier = pltpu.get_barrier_semaphore()

    def greet(devices):
        for d in devices:
            pl.semaphore_signal(barrier, inc=1, device_id=d, device_id_type=MESH)

    @pl.when(core == 0)
    def _():
        pending.clear()
        load_b = [
            local(probe_hbm.at[x, :, pl.ds(koff(kind, kc), KC)],
                  pb.at[lo, z, kc] if kind == "O" else b_send.at[kc], ("probe", kind, kc))
            for kind in "OP" for kc in (0, 1)
        ]
        peers = [dev(x, 1, y, z), dev(x, 0, y + 1 - 2 * lo, z)]
        peers += [dev(x, 0, y, zat(d)) for d in (1, -1, 2, -2)]
        peers += [dev(xat(d), 1, y, z) for d in (1, 2, 3)]
        greet(peers)

        def outgoing(i):
            for cp in loads[i]:
                cp.wait()
            out_s[i] = (v_pg[i].astype(F32) + v_comp[i]).astype(BF16)

        outgoing(0)
        for cp in load_b:
            cp.wait()
        pl.semaphore_wait(barrier, len(peers))

        def hop(slot, typ, at, sign, kc, step):
            d = at + step
            ref = pb.at[slot[0], slot[1], kc]
            send(ref, ref, ("z", typ, sign * d, kc), dev(x, 0, y, zat(sign * step)), 0)

        own = {"A": lo, "B": 1 - lo}

        def spread(typ, at, kc):
            for sign in (1, -1):
                src = zat(-sign * at)
                if at < 4:
                    hop((own[typ], src), typ, at, sign, kc, 2)
                    hop((own[typ], src), typ, at, sign, kc, 1)
                else:
                    hop((own[typ], src), typ, at, sign, kc, 1)
                    if (kc == 0) == (sign == 1):
                        hop((own[typ], src), typ, at, sign, kc, 2)

        def wait_z(typ, d, kc):
            arrived(pb.at[own[typ], zat(-d), kc], ("z", typ, d, kc))

        def forward(typ, d):
            ref = pb.at[own[typ], zat(-d)]
            send(ref, ref, ("fw", typ, d), dev(x, 1, y, z))

        for kc in (0, 1):
            ref = pb.at[lo, z, kc]
            send(b_send.at[kc], ref, ("bx", kc), dev(x, 0, y + 1 - 2 * lo, z))
        for kc in (0, 1):
            spread("A", 0, kc)

        def push(i):
            send(out_s.at[i], out_s.at[i], ("push", i), dev(x, 1, y, z))

        push(0)
        for i in (1, 2, 3):
            outgoing(i)
            push(i)
        load_prm.wait()
        load_mom.wait()
        q_s[...] = prm[...] - (RATE * NEST * NEST) * mom[...]
        send(q_s, q_s, ("q",), dev(x, 1, y, z))
        forward("A", 0)

        for kc in (0, 1):
            arrived(pb.at[1 - lo, z, kc], ("bx", kc))
            spread("B", 0, kc)
        forward("B", 0)
        for kc in (0, 1):
            for sign in (1, -1):
                wait_z("A", 2 * sign, kc)
            spread("A", 2, kc)
        for d in (1, -1):
            for kc in (0, 1):
                wait_z("A", d, kc)
            forward("A", d)
        forward("A", 2)
        forward("A", -2)
        for kc in (0, 1):
            for sign in (1, -1):
                wait_z("B", 2 * sign, kc)
            spread("B", 2, kc)
        for d in (1, -1):
            for kc in (0, 1):
                wait_z("B", d, kc)
            forward("B", d)
        forward("B", 2)
        forward("B", -2)
        for typ in "AB":
            for kc in (0, 1):
                for sign in (1, -1):
                    wait_z(typ, 4 * sign, kc)
                spread(typ, 4, kc)
            for d in (3, -3):
                for kc in (0, 1):
                    wait_z(typ, d, kc)
                forward(typ, d)
            forward(typ, 4)
            forward(typ, -4)
        for typ in "AB":
            for d in (5, -5):
                for kc in (0, 1):
                    wait_z(typ, d, kc)
                forward(typ, d)
            wait_z(typ, 6, 0)
            wait_z(typ, -6, 1)
            forward(typ, 6)

        stores = []
        for i, (kind, kc) in enumerate(ORDER):
            at = pl.ds(koff(kind, kc), KC)
            arrived(sum_s.at[i], ("sum", i))
            average = sum_s[i]
            m = NEST * mom[:, at] + average
            n_mom[i] = m
            n_prm[i] = prm[:, at] - RATE * (average + NEST * m)
            stores.append(local(n_mom.at[i], new_mom_hbm.at[:, at], ("nm", i)))
            stores.append(local(n_prm.at[i], new_prm_hbm.at[:, at], ("np", i)))
        for d in (0, 1, 2, 3):
            arrived(outb.at[:, xat(-d)], ("out", 0, d))
        stores.append(local(outb, out_hbm, "out"))
        for cp in stores:
            cp.wait()
        for cp in pending:
            cp.wait_send()

    @pl.when(core == 1)
    def _():
        pending.clear()
        right, left = xat(1), xat(-1)
        twin = dev(x, 1, y + 1 - 2 * lo, z)
        peers = [dev(x, 0, y, z)] + [dev(xat(d), 1, y, z) for d in (1, 2, 3)]
        peers += [dev(x, 1, yat(d), z) for d in range(1, NY)]
        peers += [dev(xat(d), 0, y, z) for d in (1, 2, 3)]
        greet(peers)
        pl.semaphore_wait(barrier, len(peers))
        rdev, ldev = dev(right, 1, y, z), dev(left, 1, y, z)
        far = xat(2)

        def chip_sum(i, s):
            return v_pg[i, s].astype(F32) + v_comp[i, s] + out_s[i, s].astype(F32)

        for i in range(4):
            for cp in loads[i]:
                cp.wait()
            arrived(out_s.at[i], ("push", i))
            for side, to in ((1, rdev), (0, ldev)):
                s = far * 2 + side
                cs[i, s] = chip_sum(i, s).astype(BF16)
                send(cs.at[i, s], r_opp.at[i, side], ("opp", i, side), to)
            for side, to, xx in ((0, rdev, right), (1, ldev, left)):
                s = xx * 2 + side
                cs[i, s] = chip_sum(i, s).astype(BF16)
                send(cs.at[i, s], r_fin.at[i, side, 0], ("dir", i, side), to)

        for i in range(4):
            for side, to, xx in ((1, rdev, right), (0, ldev, left)):
                arrived(r_opp.at[i, side], ("opp", i, side))
                s = xx * 2 + side
                t_acc[i, side] = (chip_sum(i, s) + r_opp[i, side].astype(F32)).astype(BF16)
                send(t_acc.at[i, side], r_fin.at[i, side, 1], ("acc", i, side), to)

        load_prm.wait()
        load_mom.wait()
        arrived(q_s, ("q",))
        stores = []

        def gather(kc, f):
            for side, to in ((1, rdev), (0, ldev), (0, rdev), (1, ldev)):
                ref = w.at[kc, f, x, side]
                sign = "r" if to is rdev else "l"
                rel = 0 if f is lo else 1
                send(ref, ref, ("ag", kc, rel, side, sign), to)

        def relay(kc, f):
            rel = 0 if f is lo else 1
            for side, to, xx, sign in ((1, rdev, left, "r"), (0, ldev, right, "l")):
                ref = w.at[kc, f, xx, side]
                arrived(ref, ("ag", kc, rel, side, sign))
                send(ref, ref, ("ag2", kc, rel, side), to)

        for i, (kind, kc) in enumerate(ORDER):
            at = pl.ds(koff(kind, kc), KC)
            for side in (1, 0):
                for j, tag in enumerate(("dir", "acc")):
                    arrived(r_fin.at[i, side, j], (tag, i, side))
                average = (
                    chip_sum(i, x * 2 + side)
                    + r_fin[i, side, 0].astype(F32)
                    + r_fin[i, side, 1].astype(F32)
                ) * 0.125
                if side == 1:
                    m = NEST * mom[:, at] + average
                    new = prm[:, at] - RATE * (average + NEST * m)
                    n_mom[i] = m
                    n_prm[i] = new
                else:
                    sum_s[i] = average
                    new = q_s[:, at] - (RATE * (1 + NEST)) * average
                if kind == "O":
                    w[kc, lo, x, side] = new.astype(BF16)
                else:
                    wy[kc, side] = new.astype(BF16)
            if kind == "O":
                gather(kc, lo)
            else:
                send(wy.at[kc], w.at[kc, lo, x], ("wy", kc), twin)
            send(sum_s.at[i], sum_s.at[i], ("sum", i), dev(x, 0, y, z))
            stores.append(local(n_mom.at[i], new_mom_hbm.at[:, at], ("nm", i)))
            stores.append(local(n_prm.at[i], new_prm_hbm.at[:, at], ("np", i)))

        other = 1 - lo
        relay(0, lo)
        for kc in (0, 1):
            arrived(w.at[kc, other, x], ("wy", kc))
            gather(kc, other)
        relay(1, lo)
        for kc in (0, 1):
            relay(kc, other)
        for kc in (0, 1):
            for rel, f in ((0, lo), (1, other)):
                arrived(w.at[kc, f, left, 0], ("ag", kc, rel, 0, "r"))
                arrived(w.at[kc, f, right, 1], ("ag", kc, rel, 1, "l"))
                for side in (0, 1):
                    arrived(w.at[kc, f, far, side], ("ag2", kc, rel, side))
        for typ, f in (("A", lo), ("B", other)):
            for d in range(-5, 7):
                arrived(pb.at[f, zat(-d)], ("fw", typ, d))

        for lp in (0, 1):
            rows = [pb[lp, :, kc].reshape(NZ * 16, KC) for kc in (0, 1)]
            for lw in (0, 1):
                acc = jnp.zeros((NZ * 16, 128), F32)
                for kc in (0, 1):
                    acc += lax.dot_general(
                        rows[kc], w[kc, lw].reshape(128, KC), (((1,), (1,)), ((), ())),
                        preferred_element_type=F32,
                    )
                part[lw, lp] = acc.astype(BF16).reshape(2, 6, 16, 128)

        for d in (4, 3, 5, 2, 6, 1, 7):
            yy = yat(d)
            tt, ll = yy // 2, yy % 2
            send(part.at[ll, tt // 2, tt % 2], y_in.at[d], ("y", d), dev(x, 1, yy, z))
        total = part[lo, t // 2, t % 2].astype(F32)
        for d in (1, 7, 2, 6, 3, 5, 4):
            arrived(y_in.at[d], ("y", d))
            total += y_in[d].astype(F32)
        outb[:, x] = total.astype(BF16)
        for d in (2, 1, 3):
            for cc in (1, 0):
                send(outb.at[:, x], outb.at[:, x], ("out", cc, d), dev(xat(d), cc, y, z))
        send(outb.at[:, x], outb.at[:, x], ("out", 0, 0), dev(x, 0, y, z))
        for d in (1, 3, 2):
            arrived(outb.at[:, xat(-d)], ("out", 1, d))
        stores.append(local(outb, out_hbm, "out"))
        for cp in stores:
            cp.wait()
        for cp in pending:
            cp.wait_send()

    assert max(len(k.at) for k in (rk, sk, lk)) <= N_SEM


def per_device(pseudo_grad, compensation, params, momentum, probe):
    any_space = pl.BlockSpec(memory_space=pl.ANY)
    new_params, new_momentum, out = pl.pallas_call(
        kernel,
        out_shape=(
            jax.ShapeDtypeStruct((16, K), F32),
            jax.ShapeDtypeStruct((16, K), F32),
            jax.ShapeDtypeStruct((6, NX, 16, 128), BF16),
        ),
        in_specs=[any_space] * 5,
        out_specs=[any_space] * 3,
        scratch_shapes=[
            pltpu.VMEM((4, 8, 16, KC), BF16),
            pltpu.VMEM((4, 8, 16, KC), F32),
            pltpu.VMEM((4, 8, 16, KC), BF16),
            pltpu.VMEM((4, 8, 16, KC), BF16),
            pltpu.VMEM((4, 2, 16, KC), BF16),
            pltpu.VMEM((4, 2, 2, 16, KC), BF16),
            pltpu.VMEM((4, 2, 16, KC), BF16),
            pltpu.VMEM((16, K), F32),
            pltpu.VMEM((16, K), F32),
            pltpu.VMEM((16, K), F32),
            pltpu.VMEM((4, 16, KC), F32),
            pltpu.VMEM((2, 2, NX, 2, 16, KC), BF16),
            pltpu.VMEM((2, 2, 16, KC), BF16),
            pltpu.VMEM((2, NZ, 2, 16, KC), BF16),
            pltpu.VMEM((2, 16, KC), BF16),
            pltpu.VMEM((2, 2, 2, 6, 16, 128), BF16),
            pltpu.VMEM((NY, 6, 16, 128), BF16),
            pltpu.VMEM((6, NX, 16, 128), BF16),
            pltpu.VMEM((4, 16, KC), F32),
            pltpu.VMEM((4, 16, KC), F32),
            pltpu.SemaphoreType.DMA((N_SEM,)),
            pltpu.SemaphoreType.DMA((N_SEM,)),
            pltpu.SemaphoreType.DMA((N_SEM,)),
        ],
        compiler_params=pltpu.CompilerParams(
            collective_id=0, has_side_effects=True, vmem_limit_bytes=40 * 2**20
        ),
    )(
        pseudo_grad.reshape(8, 16, K),
        compensation.reshape(8, 16, K),
        params,
        momentum,
        probe.reshape(NX, 16, K),
    )
    return new_params, new_momentum, out.reshape(384, 128)


def solution(mesh):
    in_specs = (
        P("replica", "fsdp", "tensor"),
        P("replica", "fsdp", "tensor"),
        P(("fsdp", "replica"), "tensor"),
        P(("fsdp", "replica"), "tensor"),
        P("fsdp", "tensor"),
    )
    out_specs = (
        P(("fsdp", "replica"), "tensor"),
        P(("fsdp", "replica"), "tensor"),
        P("tensor", "fsdp"),
    )
    return jax.shard_map(
        per_device, mesh=mesh, in_specs=in_specs, out_specs=out_specs, check_vma=False
    )
```

time: 166 us -> 59.4 us (0.36)
  waiting for transfers between devices: 70.1 us -> 0 us
  blocking collectives: 59.7 us -> 0 us
  Pallas kernels: 0 us -> 50.5 us
  starting transfers between devices: 14 us -> 0 us
  between operations: 14.1 us -> 0.65 us
  local copies, waits for them, and re-layouts: 1.58 us -> 7.98 us
  other arithmetic: 4.3 us -> 0 us
  matrix products: 2.09 us -> 0 us
    all_to_all x3 -> x0, blocking collectives: 59.7 us -> none  [the longest x2 47.2 us: sent_to_all(): return lax.all_to_all(copies, axis, split_axis=0, concat_axis=0, tiled=True)]
    all_gather x1 -> x0, waiting for transfers between devices: 54.6 us -> none  [per_device(): lax.all_gather(source_rows, 'fsdp', axis=0, tiled=True)]
    pallas_call x0 -> x1, Pallas kernels: none -> 50.5 us  [per_device(): pl.pallas_call(kernel, out_shape=(jax.ShapeDtypeStruct((16, K), F32), jax...]
    all_to_all x1 -> x0, waiting for transfers between devices: 15.5 us -> none  [summed_on_arrival(): lax.all_to_all(tiles, axis, split_axis=0, concat_axis=0, tiled=True)]
    all_to_all x1 -> x0, starting transfers between devices: 13.9 us -> none  [summed_on_arrival(): lax.all_to_all(tiles, axis, split_axis=0, concat_axis=0, tiled=True)]
    unnamed x6 -> x13, local copies, waits for them, and re-layouts: 0.02 us -> 7.98 us
    convert_element_type x2 -> x0, other arithmetic: 4.13 us -> none  [the longest x1 3.24 us: per_device(): (pseudo_grad[0].astype(jnp.float32) + compensation[0]).astype(jnp.bfloat16)]
    dot_general x1 -> x0, matrix products: 2.09 us -> none  [per_device(): lax.dot_general(lax.all_gather(source_rows, 'fsdp', axis=0, tiled=True),...]
  transfers between devices with their start and end apart: 2 -> 0, of which waited for: 2 -> 0; matrix products, arithmetic and copies ran while one was open for 1% -> 0% of each run, Pallas kernels for 0% -> 0%
where the time goes in v1:
time: 59.4 us; the launch traced here: 59.1 us
  Pallas kernels  50.5 us (85%)
  local copies, waits for them, and re-layouts  7.98 us (13%)
  between operations  0.65 us (1%)
    pallas_call x1, Pallas kernels, per_device(): pl.pallas_call(kernel, out_shape=(jax.ShapeDtypeStruct((16, K), F32), jax...  50.5 us
    unnamed x13, local copies, waits for them, and re-layouts  7.98 us

profile of v1, /device:TPU:1, one launch (start us, length us, event | category | flops | bytes accessed | tf_op | source)
XLA Modules:
  0.0 59.1 jit_solution(8475209634237674473)
XLA Ops:
  0.6 0.0 copy-start
  0.6 1.7 %copy-done = f32[1,128,4608]{2,1,0:T(8,128)S(1)} copy-done((f32[1,128,4608]{2,1,0:T(8,128)S(1)}, f32[1,128,4608]{2,1,0:T(8,128)}, u32[]{:S(2)}) %copy-start) | copy-done | bytes 2359320
  2.3 0.0 copy-start.1
  2.3 1.3 %copy-done.1 = bf16[1,128,4608]{2,1,0:T(8,128)(2,1)S(1)} copy-done((bf16[1,128,4608]{2,1,0:T(8,128)(2,1)S(1)}, bf16[1,128,4608]{2,1,0:T(8,128)(2,1)}, u32[]{:S(2)}) %copy-start.1) | copy-done | bytes 1179672
  3.6 0.0 copy-start.2
  3.6 1.1 %copy-done.2 = bf16[64,4608]{1,0:T(8,128)(2,1)S(1)} copy-done((bf16[64,4608]{1,0:T(8,128)(2,1)S(1)}, bf16[64,4608]{1,0:T(8,128)(2,1)}, u32[]{:S(2)}) %copy-start.2) | copy-done | bytes 589848
  4.6 0.0 copy-start.3
  4.6 1.0 %copy-done.3 = f32[16,4608]{1,0:T(8,128)S(1)} copy-done((f32[16,4608]{1,0:T(8,128)S(1)}, f32[16,4608]{1,0:T(8,128)}, u32[]{:S(2)}) %copy-start.3) | copy-done | bytes 294936
  5.6 0.0 copy-start.4
  5.6 1.0 %copy-done.4 = f32[16,4608]{1,0:T(8,128)S(1)} copy-done((f32[16,4608]{1,0:T(8,128)S(1)}, f32[16,4608]{1,0:T(8,128)}, u32[]{:S(2)}) %copy-start.4) | copy-done | bytes 294936
  6.6 50.5 %shard_map.76 = (f32[16,4608]{1,0:T(8,128)S(1)}, f32[16,4608]{1,0:T(8,128)S(1)}, bf16[6,4,16,128]{3,2,1,0:T(8,128)(2,1)S(1)}) custom-call(bf16[8,16,4608]{2,1,0:T(8,128)(2,1)S(1)} %bitcast.5, f32[8,16,4608]{2,1,0:T(8,128)S(1)} %bitcast.4, f32[16,4608]{1,0:T(8,128)S(1)} %copy-done.3, f32[16,4608]{1,0:T(8,128)S(1)} %copy-done.4, bf16[4,16,4608]{2,1,0:T(8,128)(2,1)S(1)} %bitcast.6), custom_call_target="tpu_custom_call" | custom-call | tf_op jit(solution)/shard_map/pallas_call | solution.py:370
  57.0 0.7 %copy.11 = f32[16,4608]{1,0:T(8,128)} copy(f32[16,4608]{1,0:T(8,128)S(1)} %get-tuple-element.12) | data formatting | bytes 589824
  57.8 0.7 %copy.12 = f32[16,4608]{1,0:T(8,128)} copy(f32[16,4608]{1,0:T(8,128)S(1)} %get-tuple-element.13) | data formatting | bytes 589824
  58.5 0.6 %copy.13 = bf16[384,128]{1,0:T(8,128)(2,1)} copy(bf16[384,128]{1,0:T(8,128)(2,1)S(1)} %bitcast.7) | data formatting | bytes 196608
Async XLA Ops:
  0.6 1.7 %copy-start = (f32[1,128,4608]{2,1,0:T(8,128)S(1)}, f32[1,128,4608]{2,1,0:T(8,128)}, u32[]{:S(2)}) copy-start(f32[1,128,4608]{2,1,0:T(8,128)} %param.6) | copy-start | bytes 7077892
  2.3 1.3 %copy-start.1 = (bf16[1,128,4608]{2,1,0:T(8,128)(2,1)S(1)}, bf16[1,128,4608]{2,1,0:T(8,128)(2,1)}, u32[]{:S(2)}) copy-start(bf16[1,128,4608]{2,1,0:T(8,128)(2,1)} %param.5) | copy-start | bytes 3538948
  3.6 1.1 %copy-start.2 = (bf16[64,4608]{1,0:T(8,128)(2,1)S(1)}, bf16[64,4608]{1,0:T(8,128)(2,1)}, u32[]{:S(2)}) copy-start(bf16[64,4608]{1,0:T(8,128)(2,1)} %param.9) | copy-start | bytes 1769476
  4.6 1.0 %copy-start.3 = (f32[16,4608]{1,0:T(8,128)S(1)}, f32[16,4608]{1,0:T(8,128)}, u32[]{:S(2)}) copy-start(f32[16,4608]{1,0:T(8,128)} %prm_hbm.1) | copy-start | bytes 884740
  5.6 1.0 %copy-start.4 = (f32[16,4608]{1,0:T(8,128)S(1)}, f32[16,4608]{1,0:T(8,128)}, u32[]{:S(2)}) copy-start(f32[16,4608]{1,0:T(8,128)} %mom_hbm.1) | copy-start | bytes 884740

commit v2 on v1

--- a/solution.py
+++ b/solution.py
@@ -30,7 +30,7 @@
     new_prm_hbm, new_mom_hbm, out_hbm,
     v_pg, v_comp, out_s, cs, r_opp, r_fin, t_acc, prm, mom, q_s, sum_s,
     w, wy, pb, b_send, part, y_in, outb, n_prm, n_mom,
-    send_sem, recv_sem, loc_sem,
+    send_sem, recv_sem, loc_sem, go,
 ):
     rep = lax.axis_index("replica")
     fs = lax.axis_index("fsdp")
@@ -98,145 +98,16 @@
         for d in devices:
             pl.semaphore_signal(barrier, inc=1, device_id=d, device_id_type=MESH)
 
-    @pl.when(core == 0)
-    def _():
-        pending.clear()
-        load_b = [
-            local(probe_hbm.at[x, :, pl.ds(koff(kind, kc), KC)],
-                  pb.at[lo, z, kc] if kind == "O" else b_send.at[kc], ("probe", kind, kc))
-            for kind in "OP" for kc in (0, 1)
-        ]
-        peers = [dev(x, 1, y, z), dev(x, 0, y + 1 - 2 * lo, z)]
-        peers += [dev(x, 0, y, zat(d)) for d in (1, -1, 2, -2)]
-        peers += [dev(xat(d), 1, y, z) for d in (1, 2, 3)]
-        greet(peers)
-
-        def outgoing(i):
-            for cp in loads[i]:
-                cp.wait()
-            out_s[i] = (v_pg[i].astype(F32) + v_comp[i]).astype(BF16)
-
-        outgoing(0)
-        for cp in load_b:
-            cp.wait()
-        pl.semaphore_wait(barrier, len(peers))
-
-        def hop(slot, typ, at, sign, kc, step):
-            d = at + step
-            ref = pb.at[slot[0], slot[1], kc]
-            send(ref, ref, ("z", typ, sign * d, kc), dev(x, 0, y, zat(sign * step)), 0)
-
-        own = {"A": lo, "B": 1 - lo}
-
-        def spread(typ, at, kc):
-            for sign in (1, -1):
-                src = zat(-sign * at)
-                if at < 4:
-                    hop((own[typ], src), typ, at, sign, kc, 2)
-                    hop((own[typ], src), typ, at, sign, kc, 1)
-                else:
-                    hop((own[typ], src), typ, at, sign, kc, 1)
-                    if (kc == 0) == (sign == 1):
-                        hop((own[typ], src), typ, at, sign, kc, 2)
-
-        def wait_z(typ, d, kc):
-            arrived(pb.at[own[typ], zat(-d), kc], ("z", typ, d, kc))
-
-        def forward(typ, d):
-            ref = pb.at[own[typ], zat(-d)]
-            send(ref, ref, ("fw", typ, d), dev(x, 1, y, z))
-
-        for kc in (0, 1):
-            ref = pb.at[lo, z, kc]
-            send(b_send.at[kc], ref, ("bx", kc), dev(x, 0, y + 1 - 2 * lo, z))
-        for kc in (0, 1):
-            spread("A", 0, kc)
-
-        def push(i):
-            send(out_s.at[i], out_s.at[i], ("push", i), dev(x, 1, y, z))
-
-        push(0)
-        for i in (1, 2, 3):
-            outgoing(i)
-            push(i)
-        load_prm.wait()
-        load_mom.wait()
-        q_s[...] = prm[...] - (RATE * NEST * NEST) * mom[...]
-        send(q_s, q_s, ("q",), dev(x, 1, y, z))
-        forward("A", 0)
-
-        for kc in (0, 1):
-            arrived(pb.at[1 - lo, z, kc], ("bx", kc))
-            spread("B", 0, kc)
-        forward("B", 0)
-        for kc in (0, 1):
-            for sign in (1, -1):
-                wait_z("A", 2 * sign, kc)
-            spread("A", 2, kc)
-        for d in (1, -1):
-            for kc in (0, 1):
-                wait_z("A", d, kc)
-            forward("A", d)
-        forward("A", 2)
-        forward("A", -2)
-        for kc in (0, 1):
-            for sign in (1, -1):
-                wait_z("B", 2 * sign, kc)
-            spread("B", 2, kc)
-        for d in (1, -1):
-            for kc in (0, 1):
-                wait_z("B", d, kc)
-            forward("B", d)
-        forward("B", 2)
-        forward("B", -2)
-        for typ in "AB":
-            for kc in (0, 1):
-                for sign in (1, -1):
-                    wait_z(typ, 4 * sign, kc)
-                spread(typ, 4, kc)
-            for d in (3, -3):
-                for kc in (0, 1):
-                    wait_z(typ, d, kc)
-                forward(typ, d)
-            forward(typ, 4)
-            forward(typ, -4)
-        for typ in "AB":
-            for d in (5, -5):
-                for kc in (0, 1):
-                    wait_z(typ, d, kc)
-                forward(typ, d)
-            wait_z(typ, 6, 0)
-            wait_z(typ, -6, 1)
-            forward(typ, 6)
-
-        stores = []
-        for i, (kind, kc) in enumerate(ORDER):
-            at = pl.ds(koff(kind, kc), KC)
-            arrived(sum_s.at[i], ("sum", i))
-            average = sum_s[i]
-            m = NEST * mom[:, at] + average
-            n_mom[i] = m
-            n_prm[i] = prm[:, at] - RATE * (average + NEST * m)
-            stores.append(local(n_mom.at[i], new_mom_hbm.at[:, at], ("nm", i)))
-            stores.append(local(n_prm.at[i], new_prm_hbm.at[:, at], ("np", i)))
-        for d in (0, 1, 2, 3):
-            arrived(outb.at[:, xat(-d)], ("out", 0, d))
-        stores.append(local(outb, out_hbm, "out"))
-        for cp in stores:
-            cp.wait()
-        for cp in pending:
-            cp.wait_send()
-
     @pl.when(core == 1)
     def _():
         pending.clear()
         right, left = xat(1), xat(-1)
         twin = dev(x, 1, y + 1 - 2 * lo, z)
-        peers = [dev(x, 0, y, z)] + [dev(xat(d), 1, y, z) for d in (1, 2, 3)]
+        peers = [dev(xat(d), 1, y, z) for d in (1, 2, 3)]
         peers += [dev(x, 1, yat(d), z) for d in range(1, NY)]
-        peers += [dev(xat(d), 0, y, z) for d in (1, 2, 3)]
         greet(peers)
-        pl.semaphore_wait(barrier, len(peers))
+        pl.semaphore_wait(barrier, len(peers) + 4)
+        pl.semaphore_signal(go, inc=1, device_id=dev(x, 0, y, z), device_id_type=MESH)
         rdev, ldev = dev(right, 1, y, z), dev(left, 1, y, z)
         far = xat(2)
 
@@ -356,6 +227,135 @@
         send(outb.at[:, x], outb.at[:, x], ("out", 0, 0), dev(x, 0, y, z))
         for d in (1, 3, 2):
             arrived(outb.at[:, xat(-d)], ("out", 1, d))
+        stores.append(local(outb, out_hbm, "out"))
+        for cp in stores:
+            cp.wait()
+        for cp in pending:
+            cp.wait_send()
+
+    @pl.when(core == 0)
+    def _():
+        pending.clear()
+        load_b = [
+            local(probe_hbm.at[x, :, pl.ds(koff(kind, kc), KC)],
+                  pb.at[lo, z, kc] if kind == "O" else b_send.at[kc], ("probe", kind, kc))
+            for kind in "OP" for kc in (0, 1)
+        ]
+        mate = y + 1 - 2 * lo
+        greet([dev(xat(d), 1, y, z) for d in (0, 1, 2, 3)])
+        peers = [dev(x, 0, mate, z)]
+        peers += [dev(x, 0, yy, zat(d)) for d in (1, -1, 2, -2) for yy in (y, mate)]
+        greet(peers)
+
+        def outgoing(i):
+            for cp in loads[i]:
+                cp.wait()
+            out_s[i] = (v_pg[i].astype(F32) + v_comp[i]).astype(BF16)
+
+        def push(i):
+            send(out_s.at[i], out_s.at[i], ("push", i), dev(x, 1, y, z))
+
+        outgoing(0)
+        pl.semaphore_wait(go, 1)
+        push(0)
+        for i in (1, 2, 3):
+            outgoing(i)
+            push(i)
+        load_prm.wait()
+        load_mom.wait()
+        q_s[...] = prm[...] - (RATE * NEST * NEST) * mom[...]
+        send(q_s, q_s, ("q",), dev(x, 1, y, z))
+        for cp in load_b:
+            cp.wait()
+        pl.semaphore_wait(barrier, len(peers))
+
+        def hop(slot, typ, at, sign, kc, step):
+            d = at + step
+            ref = pb.at[slot[0], slot[1], kc]
+            send(ref, ref, ("z", typ, sign * d, kc), dev(x, 0, y, zat(sign * step)), 0)
+
+        own = {"A": lo, "B": 1 - lo}
+
+        def spread(typ, at, kc):
+            for sign in (1, -1):
+                src = zat(-sign * at)
+                if at < 4:
+                    hop((own[typ], src), typ, at, sign, kc, 2)
+                    hop((own[typ], src), typ, at, sign, kc, 1)
+                else:
+                    hop((own[typ], src), typ, at, sign, kc, 1)
+                    if (kc == 0) == (sign == 1):
+                        hop((own[typ], src), typ, at, sign, kc, 2)
+
+        def wait_z(typ, d, kc):
+            arrived(pb.at[own[typ], zat(-d), kc], ("z", typ, d, kc))
+
+        def forward(typ, d):
+            ref = pb.at[own[typ], zat(-d)]
+            send(ref, ref, ("fw", typ, d), dev(x, 1, y, z))
+
+        for kc in (0, 1):
+            ref = pb.at[lo, z, kc]
+            for d in (2, -2, 1, -1):
+                send(ref, ref, ("z", "A", d, kc), dev(x, 0, y, zat(d)))
+            for d in (2, -2, 1, -1, 0):
+                send(b_send.at[kc], ref, ("z", "B", d, kc), dev(x, 0, mate, zat(d)))
+        forward("A", 0)
+        for kc in (0, 1):
+            wait_z("B", 0, kc)
+        forward("B", 0)
+        for kc in (0, 1):
+            for sign in (1, -1):
+                wait_z("A", 2 * sign, kc)
+            spread("A", 2, kc)
+        for d in (1, -1):
+            for kc in (0, 1):
+                wait_z("A", d, kc)
+            forward("A", d)
+        forward("A", 2)
+        forward("A", -2)
+        for kc in (0, 1):
+            for sign in (1, -1):
+                wait_z("B", 2 * sign, kc)
+            spread("B", 2, kc)
+        for d in (1, -1):
+            for kc in (0, 1):
+                wait_z("B", d, kc)
+            forward("B", d)
+        forward("B", 2)
+        forward("B", -2)
+        for typ in "AB":
+            for kc in (0, 1):
+                for sign in (1, -1):
+                    wait_z(typ, 4 * sign, kc)
+                spread(typ, 4, kc)
+            for d in (3, -3):
+                for kc in (0, 1):
+                    wait_z(typ, d, kc)
+                forward(typ, d)
+            forward(typ, 4)
+            forward(typ, -4)
+        for typ in "AB":
+            for d in (5, -5):
+                for kc in (0, 1):
+                    wait_z(typ, d, kc)
+                forward(typ, d)
+            wait_z(typ, 6, 0)
+            wait_z(typ, -6, 1)
+            forward(typ, 6)
+
+        stores = []
+        for i, (kind, kc) in enumerate(ORDER):
+            at = pl.ds(koff(kind, kc), KC)
+            arrived(sum_s.at[i], ("sum", i))
+            average = sum_s[i]
+            m = NEST * mom[:, at] + average
+            n_mom[i] = m
+            n_prm[i] = prm[:, at] - RATE * (average + NEST * m)
+            stores.append(local(n_mom.at[i], new_mom_hbm.at[:, at], ("nm", i)))
+            stores.append(local(n_prm.at[i], new_prm_hbm.at[:, at], ("np", i)))
+        for d in (0, 1, 2, 3):
+            arrived(outb.at[:, xat(-d)], ("out", 0, d))
         stores.append(local(outb, out_hbm, "out"))
         for cp in stores:
             cp.wait()
@@ -400,9 +400,10 @@
             pltpu.SemaphoreType.DMA((N_SEM,)),
             pltpu.SemaphoreType.DMA((N_SEM,)),
             pltpu.SemaphoreType.DMA((N_SEM,)),
+            pltpu.SemaphoreType.REGULAR,
         ],
         compiler_params=pltpu.CompilerParams(
-            collective_id=0, has_side_effects=True, vmem_limit_bytes=40 * 2**20
+            collective_id=0, has_side_effects=True, vmem_limit_bytes=60 * 2**20
         ),
     )(
         pseudo_grad.reshape(8, 16, K),

time: 59.4 us -> 57.2 us (0.963)
  local copies, waits for them, and re-layouts: 7.98 us -> 4.93 us
  Pallas kernels: 50.5 us -> 51.4 us
    unnamed x13 -> x3, local copies, waits for them, and re-layouts: 7.98 us -> 4.93 us
    pallas_call x1, Pallas kernels: 50.5 us -> 51.4 us  [per_device(): pl.pallas_call(kernel, out_shape=(jax.ShapeDtypeStruct((16, K), F32), jax...]
where the time goes in v2:
time: 57.2 us; the launch traced here: 57 us
  Pallas kernels  51.4 us (90%)
  local copies, waits for them, and re-layouts  4.93 us (9%)
  between operations  0.64 us (1%)
    pallas_call x1, Pallas kernels, per_device(): pl.pallas_call(kernel, out_shape=(jax.ShapeDtypeStruct((16, K), F32), jax...  51.4 us
    unnamed x3, local copies, waits for them, and re-layouts  4.93 us

profile of v2, /device:TPU:1, one launch (start us, length us, event | category | flops | bytes accessed | tf_op | source)
XLA Modules:
  0.0 57.0 jit_solution(1173831780642940833)
XLA Ops:
  0.6 51.4 %shard_map.76 = (f32[16,4608]{1,0:T(8,128)}, f32[16,4608]{1,0:T(8,128)}, bf16[6,4,16,128]{3,2,1,0:T(8,128)(2,1)}) custom-call(bf16[8,16,4608]{2,1,0:T(8,128)(2,1)} %bitcast.5, f32[8,16,4608]{2,1,0:T(8,128)} %bitcast.4, f32[16,4608]{1,0:T(8,128)} %prm_hbm.1, f32[16,4608]{1,0:T(8,128)} %mom_hbm.1, bf16[4,16,4608]{2,1,0:T(8,128)(2,1)} %bitcast.6), custom_call_target="tpu_custom_call" | custom-call | tf_op jit(solution)/shard_map/pallas_call | solution.py:370
  52.1 1.7 %copy.11 = f32[16,4608]{1,0:T(8,128)} copy(f32[16,4608]{1,0:T(8,128)} %get-tuple-element.12) | data formatting | bytes 589824
  53.8 1.7 %copy.12 = f32[16,4608]{1,0:T(8,128)} copy(f32[16,4608]{1,0:T(8,128)} %get-tuple-element.13) | data formatting | bytes 589824
  55.5 1.5 %copy.13 = bf16[384,128]{1,0:T(8,128)(2,1)} copy(bf16[384,128]{1,0:T(8,128)(2,1)} %bitcast.7) | data formatting | bytes 196608

commit v3 on v0

v3 whole, which is shorter than its diff:
```python
import jax
import jax.numpy as jnp
from jax import lax
from jax.experimental import pallas as pl
from jax.experimental.pallas import tpu as pltpu
from jax.sharding import PartitionSpec as P

MESH = pl.DeviceIdType.MESH
RATE = 0.7
NEST = 0.9
F32, BF16 = jnp.float32, jnp.bfloat16

NX, NY, NZ = 4, 8, 12
K = 4608
KC = K // 4
HALF = NZ // 2
FIRST = 6
EARLY = 6
ORDER = (("P", 0), ("P", 1), ("O", 0), ("O", 1))
SPREAD = {0: (-3, 1, -1), 1: (1,), 2: (1,), 3: (1,), 4: (1,), -1: (-1,), -3: (-1, -3), -4: (-1,)}
LEAVES = (5, -2, -5, -6)
INNER = (1, -1, -3, 2, -4, 3, 4)
N_RECV, N_SEND, N_LOCAL = 88, 12, 10


class Keys:
    def __init__(self):
        self.at = {}

    def __call__(self, *key):
        return self.at.setdefault(key, len(self.at))


def kernel(
    pg_hbm, comp_hbm, prm_hbm, mom_hbm, probe_hbm,
    n_prm, n_mom, outb,
    v_pg, v_comp, out_s, cs, r_opp, r_fin, t_acc, prm, mom, q_s, sum_s,
    w, wy, pb, b_send, part, y_in,
    send_sem, recv_sem, loc_sem, go,
):
    rep = lax.axis_index("replica")
    fs = lax.axis_index("fsdp")
    t = lax.axis_index("tensor")
    x, core = rep // 2, rep % 2
    lo, z = fs // NZ, fs % NZ
    other = 1 - lo
    y = t * 2 + lo
    mate = t * 2 + other

    def dev(x_, core_, y_, z_):
        return (x_ * 2 + core_, (y_ % 2) * NZ + z_, y_ // 2)

    def xat(d):
        return lax.rem(x + d + NX, NX)

    def yat(d):
        return lax.rem(y + d + NY, NY)

    def zat(d):
        return lax.rem(z + d + NZ, NZ)

    def w_core(z_):
        return jnp.where(z_ < FIRST, 1, 0)

    wc = w_core(z)
    hc = 1 - wc
    w_dev, h_dev, me = dev(x, wc, y, z), dev(x, hc, y, z), dev(x, core, y, z)

    rk, sk, lk = Keys(), Keys(), Keys()

    def rsem(*key):
        return recv_sem.at[rk(*key)]

    def ssem(group):
        return send_sem.at[sk(group)]

    def send(src, dst, key, to, group):
        pltpu.make_async_remote_copy(
            src_ref=src, dst_ref=dst, send_sem=ssem(group), recv_sem=rsem(*key),
            device_id=to, device_id_type=MESH,
        ).start()

    def arrived(like, *key):
        pltpu.make_async_remote_copy(
            src_ref=like, dst_ref=like, send_sem=send_sem.at[0], recv_sem=rsem(*key),
            device_id=me, device_id_type=MESH,
        ).wait_recv()

    def sent(like, group):
        pltpu.make_async_remote_copy(
            src_ref=like, dst_ref=like, send_sem=ssem(group), recv_sem=recv_sem.at[0],
            device_id=me, device_id_type=MESH,
        ).wait_send()

    def load(src, dst, key):
        pltpu.make_async_copy(src, dst, loc_sem.at[lk(key)]).start()

    def loaded(like, key):
        pltpu.make_async_remote_copy(
            src_ref=like, dst_ref=like, send_sem=send_sem.at[0], recv_sem=loc_sem.at[lk(key)],
            device_id=me, device_id_type=MESH,
        ).wait_recv()

    def columns(kind, kc):
        half = lo if kind == "O" else other
        return pl.ds(pl.multiple_of((half * 2 + kc) * KC, KC), KC)

    for i, (kind, kc) in enumerate(ORDER):
        at = columns(kind, kc)
        load(pg_hbm.at[:, :, at], v_pg.at[i], ("in", i))
        load(comp_hbm.at[:, :, at], v_comp.at[i], ("in", i))

    barrier = pltpu.get_barrier_semaphore()

    def greet(to):
        pl.semaphore_signal(barrier, inc=1, device_id=to, device_id_type=MESH)

    for d in (1, 2, 3):
        greet(dev(xat(d), wc, y, z))
    for d in range(1, NY):
        greet(dev(x, wc, yat(d), z))

    def p_dev(y_, d):
        return dev(x, 1 - w_core(zat(d)), y_, zat(d))

    @pl.when(core == hc)
    def _():
        greet(w_dev)
        for kc in (0, 1):
            load(probe_hbm.at[x, :, columns("O", kc)], pb.at[lo, z, kc], "own")
            load(probe_hbm.at[x, :, columns("P", kc)], b_send.at[kc], "own")
        for yy in (y, mate):
            for d in (1, -1, 3):
                greet(p_dev(yy, d))
        greet(p_dev(mate, 0))

    @pl.when(core == wc)
    def _():
        @pl.when(wc == 1)
        def _():
            for d in (1, -1, 3):
                greet(p_dev(y, d))

        @pl.when(z >= EARLY)
        def _():
            greet(h_dev)

    load(prm_hbm, prm, "state")
    load(mom_hbm, mom, "state")

    @pl.when(core == wc)
    def _():
        right, left, far = xat(1), xat(-1), xat(2)
        rdev, ldev = dev(right, wc, y, z), dev(left, wc, y, z)
        pl.semaphore_wait(barrier, 7 + 14)

        @pl.when(z < EARLY)
        def _():
            pl.semaphore_signal(go, inc=1, device_id=h_dev, device_id_type=MESH)

        def chip_sum(i, s):
            return v_pg[i, s].astype(F32) + v_comp[i, s] + out_s[i, s].astype(F32)

        def opposite(i):
            loaded(pb.at[0], ("in", i))
            arrived(out_s.at[i], "push", i)
            for side, to in ((1, rdev), (0, ldev)):
                s = far * 2 + side
                cs[i, s] = chip_sum(i, s).astype(BF16)
                send(cs.at[i, s], r_opp.at[i, side], ("opp", i, side), to, "rs")

        def direct(i):
            for side, to, xx in ((0, rdev, right), (1, ldev, left)):
                s = xx * 2 + side
                cs[i, s] = chip_sum(i, s).astype(BF16)
                send(cs.at[i, s], r_fin.at[i, side, 0], ("fin", i), to, "rs")

        def on_the_way(i):
            for side, to, xx in ((1, rdev, right), (0, ldev, left)):
                s = xx * 2 + side
                arrived(r_opp.at[i, side], "opp", i, side)
                t_acc[i, side] = (chip_sum(i, s) + r_opp[i, side].astype(F32)).astype(BF16)
                send(t_acc.at[i, side], r_fin.at[i, side, 1], ("fin", i), to, "rs")

        opposite(0)
        opposite(1)
        direct(0)
        direct(1)
        opposite(2)
        opposite(3)
        on_the_way(0)
        on_the_way(1)
        direct(2)
        direct(3)
        on_the_way(2)
        on_the_way(3)

        loaded(v_comp.at[0], "state")
        arrived(q_s, "q")

        def gather(kc, f, rel):
            for side, to, first in ((1, rdev, True), (0, ldev, True), (0, rdev, False), (1, ldev, False)):
                ref = w.at[kc, f, x, side]
                send(ref, ref, ("ag", kc, rel, side) if first else ("rest", kc, rel), to, "ag")

        def relay(kc, f, rel):
            for side, to, xx in ((1, rdev, left), (0, ldev, right)):
                ref = w.at[kc, f, xx, side]
                arrived(ref, "ag", kc, rel, side)
                send(ref, ref, ("rest", kc, rel), to, "ag")

        for i, (kind, kc) in enumerate(ORDER):
            at = columns(kind, kc)
            arrived(r_fin.at[i], "fin", i)

            def average(side):
                return (
                    chip_sum(i, x * 2 + side)
                    + r_fin[i, side, 0].astype(F32)
                    + r_fin[i, side, 1].astype(F32)
                ) * 0.125

            avg = average(wc)
            m = NEST * mom[:, at] + avg
            new = prm[:, at] - RATE * (avg + NEST * m)
            n_mom[:, at] = m
            n_prm[:, at] = new
            avg = average(hc)
            sum_s[i] = avg
            new_h = q_s[:, at] - (RATE * (1 + NEST)) * avg
            if kind == "O":
                w[kc, lo, x, wc] = new.astype(BF16)
                w[kc, lo, x, hc] = new_h.astype(BF16)
                gather(kc, lo, 0)
            else:
                wy[kc, wc] = new.astype(BF16)
                wy[kc, hc] = new_h.astype(BF16)
                for side in (1, 0):
                    send(wy.at[kc, side], w.at[kc, lo, x, side], ("wy", kc), dev(x, wc, mate, z), "ag")
            send(sum_s.at[i], sum_s.at[i], ("sum",), h_dev, "sum")

        for kc in (0, 1):
            arrived(w.at[kc, other, x], "wy", kc)
            gather(kc, other, 1)
        for rel, f in ((0, lo), (1, other)):
            for kc in (0, 1):
                relay(kc, f, rel)
        for rel, f in ((0, lo), (1, other)):
            for kc in (0, 1):
                arrived(w.at[kc, f, 0:2], "rest", kc, rel)

                @pl.when(wc == 0)
                def _():
                    send(w.at[kc, f], w.at[kc, f], ("wf",), h_dev, "wf")

    @pl.when(core == hc)
    def _():
        def pushes():
            for i in range(4):
                loaded(pb.at[0], ("in", i))
                out_s[i] = (v_pg[i].astype(F32) + v_comp[i]).astype(BF16)
                send(out_s.at[i], out_s.at[i], ("push", i), w_dev, "push")
            loaded(v_comp.at[0], "state")
            q_s[...] = prm[...] - (RATE * NEST * NEST) * mom[...]
            send(q_s, q_s, ("q",), w_dev, "q")

        early = jnp.where(z < EARLY, 1, 0)
        greeted = 8 - early
        for d in (1, -1, -3):
            greeted += w_core(zat(d))

        @pl.when(early == 1)
        def _():
            pl.semaphore_wait(go, 1)
            pushes()

        loaded(pb.at[0, 0:2], "own")
        pl.semaphore_wait(barrier, greeted)
        own = {"A": lo, "B": other}

        def place(typ, d, step):
            zz = zat(step)
            if d in LEAVES:
                return dev(x, 1, y, zz), ("leaf", typ, d)
            return dev(x, 1 - w_core(zz), y, zz), None

        def spread(typ, at, kc):
            ref = pb.at[own[typ], zat(-at), kc]
            for step in SPREAD[at]:
                d = at + step
                to, key = place(typ, d, step)
                send(ref, ref, key or ("z", typ, d, kc), to, "relay" if at else "own")

        for kc in (0, 1):
            spread("A", 0, kc)
            for step in (*SPREAD[0], 0):
                ref = pb.at[lo, z, kc]
                send(b_send.at[kc], ref, ("z", "B", step, kc), p_dev(mate, step), "own")

        @pl.when(early == 0)
        def _():
            pushes()

        def wait_z(typ, d, kc):
            arrived(pb.at[own[typ], zat(-d), kc], "z", typ, d, kc)

        def forward(d):
            @pl.when(hc == 0)
            def _():
                for typ in "AB":
                    ref = pb.at[own[typ], zat(-d)]
                    send(ref, ref, ("fw", d), w_dev, "fw")

        for kc in (0, 1):
            wait_z("B", 0, kc)
        forward(0)
        for level in ((1, -1, -3), (2, -4), (3,), (4,)):
            for kc in (0, 1):
                for typ in "AB":
                    for d in level:
                        wait_z(typ, d, kc)
                        spread(typ, d, kc)
            for d in level:
                forward(d)

    @pl.when(core == 1)
    def _():
        near = z // HALF

        @pl.when(wc == 0)
        def _():
            arrived(w, "wf")

        def wait_blocks(want_near):
            for d in (0, *INNER, *LEAVES):
                is_near = zat(-d) // HALF == near
                for typ in "AB" if d in LEAVES else "A":
                    cond = is_near if want_near else jnp.logical_not(is_near)
                    if d in LEAVES:
                        key, like = ("leaf", typ, d), pb.at[0, 0]
                    else:
                        key, like = ("fw", d), pb.at[0, 0:2]
                        cond = jnp.logical_and(cond, wc == 1)

                    @pl.when(cond)
                    def _():
                        arrived(like, *key)

        for phase in (0, 1):
            h = near if phase == 0 else 1 - near
            wait_blocks(phase == 0)
            acc = jnp.zeros((2 * HALF * 16, 256), F32)
            for kc in (0, 1):
                rows = pb[:, pl.ds(h * HALF, HALF), kc].reshape(2 * HALF * 16, KC)
                acc += lax.dot_general(
                    rows, w[kc].reshape(256, KC), (((1,), (1,)), ((), ())),
                    preferred_element_type=F32,
                )
            for lp in (0, 1):
                for lw in (0, 1):
                    piece = acc[lp * 96 : lp * 96 + 96, lw * 128 : lw * 128 + 128]
                    part[phase, lp, lw] = piece.astype(BF16).reshape(HALF, 16, 128)
            for lp in (0, 1):
                for lw in (0, 1):
                    to = 4 * lp + 2 * h + lw

                    @pl.when(to != y)
                    def _():
                        send(part.at[phase, lp, lw], y_in.at[y], ("y",), dev(x, 1, to, z), "y")

                    @pl.when(to == y)
                    def _():
                        y_in[y] = part[phase, lp, lw]

        arrived(y_in.at[0:7], "y")
        total = y_in[0].astype(F32)
        for i in range(1, NY):
            total += y_in[i].astype(F32)
        outb[:, x] = total.astype(BF16)
        mine = outb.at[:, x]
        for d in (2, 1, 3):
            for cc in (1, 0):
                send(mine, mine, ("out",), dev(xat(d), cc, y, z), "out")
        send(mine, mine, ("out",), dev(x, 0, y, z), "out")

    @pl.when(core == hc)
    def _():
        arrived(sum_s, "sum")
        for i, (kind, kc) in enumerate(ORDER):
            at = columns(kind, kc)
            avg = sum_s[i]
            m = NEST * mom[:, at] + avg
            n_mom[:, at] = m
            n_prm[:, at] = prm[:, at] - RATE * (avg + NEST * m)
        sent(out_s, "push")
        sent(q_s, "q")
        sent(pb.at[0, 0:7], "own")
        sent(pb.at[:, 0:8], "relay")

        @pl.when(hc == 0)
        def _():
            sent(pb.at[:, 0:8], "fw")

    @pl.when(core == wc)
    def _():
        sent(pb.at[0], "rs")
        sent(pb.at[:, 0:7], "ag")
        sent(sum_s, "sum")

        @pl.when(wc == 0)
        def _():
            sent(w, "wf")

    @pl.when(core == 1)
    def _():
        sent(y_in.at[0:7], "y")
        sent(y_in.at[0:7], "out")
        arrived(y_in.at[0:3], "out")

    @pl.when(core == 0)
    def _():
        arrived(y_in.at[0:4], "out")

    assert len(rk.at) <= N_RECV and len(sk.at) <= N_SEND and len(lk.at) <= N_LOCAL


def store(a, b, c, a_out, b_out, c_out, sem):
    copies = [
        pltpu.make_async_copy(src, dst, sem.at[i])
        for i, (src, dst) in enumerate(((a, a_out), (b, b_out), (c, c_out)))
    ]
    for cp in copies:
        cp.start()
    for cp in copies:
        cp.wait()


def per_device(pseudo_grad, compensation, params, momentum, probe):
    any_space = pl.BlockSpec(memory_space=pl.ANY)
    vmem = pl.BlockSpec(memory_space=pltpu.VMEM)
    shapes = (
        jax.ShapeDtypeStruct((16, K), F32),
        jax.ShapeDtypeStruct((16, K), F32),
        jax.ShapeDtypeStruct((6, NX, 16, 128), BF16),
    )
    outs = pl.pallas_call(
        kernel,
        out_shape=tuple(pltpu.VMEM(s.shape, s.dtype) for s in shapes),
        in_specs=[any_space] * 5,
        out_specs=[vmem] * 3,
        scratch_shapes=[
            pltpu.VMEM((4, 8, 16, KC), BF16),
            pltpu.VMEM((4, 8, 16, KC), F32),
            pltpu.VMEM((4, 8, 16, KC), BF16),
            pltpu.VMEM((4, 8, 16, KC), BF16),
            pltpu.VMEM((4, 2, 16, KC), BF16),
            pltpu.VMEM((4, 2, 2, 16, KC), BF16),
            pltpu.VMEM((4, 2, 16, KC), BF16),
            pltpu.VMEM((16, K), F32),
            pltpu.VMEM((16, K), F32),
            pltpu.VMEM((16, K), F32),
            pltpu.VMEM((4, 16, KC), F32),
            pltpu.VMEM((2, 2, NX, 2, 16, KC), BF16),
            pltpu.VMEM((2, 2, 16, KC), BF16),
            pltpu.VMEM((2, NZ, 2, 16, KC), BF16),
            pltpu.VMEM((2, 16, KC), BF16),
            pltpu.VMEM((2, 2, 2, HALF, 16, 128), BF16),
            pltpu.VMEM((NY, HALF, 16, 128), BF16),
            pltpu.SemaphoreType.DMA((N_SEND,)),
            pltpu.SemaphoreType.DMA((N_RECV,)),
            pltpu.SemaphoreType.DMA((N_LOCAL,)),
            pltpu.SemaphoreType.REGULAR,
        ],
        compiler_params=pltpu.CompilerParams(
            collective_id=0, has_side_effects=True, vmem_limit_bytes=60 * 2**20
        ),
    )(
        pseudo_grad.reshape(8, 16, K),
        compensation.reshape(8, 16, K),
        params,
        momentum,
        probe.reshape(NX, 16, K),
    )
    new_params, new_momentum, out = pl.pallas_call(
        store,
        out_shape=shapes,
        in_specs=[any_space] * 3,
        out_specs=[any_space] * 3,
        scratch_shapes=[pltpu.SemaphoreType.DMA((3,))],
        compiler_params=pltpu.CompilerParams(vmem_limit_bytes=2**20),
    )(*outs)
    return new_params, new_momentum, out.reshape(384, 128)


def solution(mesh):
    in_specs = (
        P("replica", "fsdp", "tensor"),
        P("replica", "fsdp", "tensor"),
        P(("fsdp", "replica"), "tensor"),
        P(("fsdp", "replica"), "tensor"),
        P("fsdp", "tensor"),
    )
    out_specs = (
        P(("fsdp", "replica"), "tensor"),
        P(("fsdp", "replica"), "tensor"),
        P("tensor", "fsdp"),
    )
    return jax.shard_map(
        per_device, mesh=mesh, in_specs=in_specs, out_specs=out_specs, check_vma=False
    )
```

time: 166 us -> 49.2 us (0.30)
  the two profiles are of different devices: /device:TPU:1 before, /device:TPU:80 now
where the time goes in v3:
time: 49.2 us; the launch traced here: 49.1 us
  Pallas kernels  48.4 us (98%)
  between operations  0.64 us (1%)
    pallas_call x1, Pallas kernels, per_device(): pl.pallas_call(kernel, out_shape=tuple((pltpu.VMEM(s.shape, s.dtype) for...  47.6 us

profile of v3, /device:TPU:80, one launch (start us, length us, event | category | flops | bytes accessed | tf_op | source)
XLA Modules:
  0.0 49.1 jit_solution(10323934600138441878)
XLA Ops:
  0.6 47.6 %shard_map.76 = (f32[16,4608]{1,0:T(8,128)S(1)}, f32[16,4608]{1,0:T(8,128)S(1)}, bf16[6,4,16,128]{3,2,1,0:T(8,128)(2,1)S(1)}) custom-call(bf16[8,16,4608]{2,1,0:T(8,128)(2,1)} %bitcast.5, f32[8,16,4608]{2,1,0:T(8,128)} %bitcast.4, f32[16,4608]{1,0:T(8,128)} %prm_hbm.1, f32[16,4608]{1,0:T(8,128)} %mom_hbm.1, bf16[4,16,4608]{2,1,0:T(8,128)(2,1)} %bitcast.6), custom_call_target="tpu_custom_call" | custom-call | tf_op jit(solution)/shard_map/pallas_call | solution.py:446
  48.2 0.9 %shard_map.77 = (f32[16,4608]{1,0:T(8,128)}, f32[16,4608]{1,0:T(8,128)}, bf16[6,4,16,128]{3,2,1,0:T(8,128)(2,1)}) custom-call(f32[16,4608]{1,0:T(8,128)S(1)} %get-tuple-element.9.a, f32[16,4608]{1,0:T(8,128)S(1)} %get-tuple-element.10.b, bf16[6,4,16,128]{3,2,1,0:T(8,128)(2,1)S(1)} %get-tuple-element.11.c), custom_call_target="tpu_custom_call" | custom-call | tf_op jit(solution)/shard_map/pallas_call | solution.py:484

commit v4 on v3

v4 whole, which is shorter than its diff:
```python
import jax
import jax.numpy as jnp
from jax import lax
from jax.experimental import pallas as pl
from jax.experimental.pallas import tpu as pltpu
from jax.sharding import PartitionSpec as P

MESH = pl.DeviceIdType.MESH
RATE = 0.7
NEST = 0.9
F32, BF16 = jnp.float32, jnp.bfloat16

NX, NY, NZ = 4, 8, 12
K = 4608
KC = K // 4
HALF = NZ // 2
FIRST = 1
EARLY = 6
ORDER = (("P", 0), ("P", 1), ("O", 0), ("O", 1))
TREE = {
    0: {0: (1, 11,), 1: (2,), 2: (3,), 3: (4,), 4: (5,), 5: (6,), 8: (9, 7,), 10: (8,), 11: (10,)},
    1: {0: (11,), 1: (2, 0,), 2: (3,), 3: (4,), 4: (5,), 5: (6,), 6: (7,), 9: (8, 10,), 11: (9,)},
    2: {0: (11,), 1: (0,), 2: (1, 3,), 3: (4,), 4: (5,), 5: (6,), 6: (7,), 7: (8,), 10: (9,), 11: (10,)},
    3: {0: (11,), 1: (0,), 2: (1,), 3: (2, 4,), 4: (5,), 5: (6,), 6: (7,), 7: (8,), 10: (9,), 11: (10,)},
    4: {0: (11,), 1: (0,), 2: (1,), 3: (2,), 4: (3, 5,), 5: (6,), 6: (7,), 7: (8,), 8: (9,), 9: (10,)},
    5: {1: (0,), 2: (1,), 3: (2,), 4: (3,), 5: (4, 6,), 6: (7,), 7: (8,), 8: (11, 9,), 9: (10,)},
    6: {1: (0, 2,), 2: (3,), 4: (5,), 6: (4, 8, 7, 1,), 8: (9,), 9: (10,), 10: (11,)},
    7: {2: (1,), 3: (2, 4,), 4: (5,), 6: (3,), 7: (8, 6,), 8: (9, 10,), 10: (11, 0,)},
    8: {0: (1, 11,), 3: (2,), 4: (5, 3,), 5: (6,), 7: (4,), 8: (7, 9,), 9: (0,), 11: (10,)},
    9: {0: (11, 1,), 1: (2,), 4: (3, 5,), 6: (4,), 7: (6, 8,), 9: (7, 0,), 11: (10,)},
    10: {0: (1,), 1: (2,), 4: (3,), 6: (5,), 7: (6,), 8: (7,), 9: (4,), 10: (9, 8, 11,), 11: (0,)},
    11: {1: (0, 2,), 2: (3,), 3: (4,), 6: (5, 7,), 9: (8,), 10: (9, 6,), 11: (1, 10,)},
}
WAITS = (
    (4, 6, 5, 7, 8, 10, 9, 11, -1, 12, 14, 13, 15, 36, 40, 16, 38, 37, 42, 18, 41, 32, 17, 39, 43, 34, 19, 33, 35),
    (0, 8, 2, 1, 10, 9, 3, 11, 12, 14, 13, 15, 16, 44, 18, 46, 45, 17, 24, 47, 19, 25, 26, 20, 22, 27, 36, 21, 40, 23, 38, 37, 42, 41, 39, 43),
    (4, 6, 5, 12, 7, 0, 14, 2, 13, 1, 15, 3, 16, 18, 17, 19, 20, 22, 21, 44, 23, 46, 45, 24, 47, 28, 30, 25, 26, 29, 31, 27),
    (8, 10, 9, 11, 4, 16, 6, 5, 18, 17, 7, 0, 19, 2, 1, 3, 20, 22, 21, 23, 28, 30, 29, 31, 44, 32, 46, 34, 45, 33, 47, 35),
    (12, 14, 13, 8, 15, 10, 20, 9, 22, 11, 21, 4, 23, 24, 6, 5, 7, 0, 25, 26, 2, 1, 27, 3, 32, 34, 33, 35, 28, 40, 30, 36, 29, 41, 42, 31, 38, 37, 39, 43),
    (16, 18, 17, 12, -1, 19, 14, 13, 8, 15, 10, 9, 11, 4, 6, 5, 0, 7, 2, 1, 32, 3, 34, 33, 35),
    (28, 30, 20, 29, 22, 31, 21, 16, 23, 18, 17, 12, 19, 36, 14, 13, 8, 38, 15, 37, 10, 9, 39, 4, 11, 40, 6, 44, 5, 46, 7, 41, 42, 45, 47, 43),
    (32, 34, 33, 36, 35, 38, 37, 20, 39, 22, 21, 16, 40, 23, 18, 17, 41, 12, 42, 19, 14, 13, 8, 43, 15, 10, 9, 11),
    (28, 30, 29, 24, 31, 26, 25, 40, 27, 41, 42, 43, 20, 22, 21, 16, 23, 18, 17, 0, 19, 2, 1, 3),
    (32, 40, 34, 33, 35, 41, 42, 43, 24, 44, 46, 45, 26, 25, 47, 27, 4, 20, 6, 22, 5, 21, 7, 16, 23, 18, 17, 19),
    (44, 46, 45, 47, 28, 30, 0, 29, 2, 31, 1, 24, 3, 8, 26, 10, 25, 9, 27, 11, 12, 14, 13, 15),
    (40, 42, 41, 43, 0, 2, 1, 3, 4, 6, 8, 5, 7, 10, 9, 11, 12, 14, 13, 15, 36, 38, 37, 32, 39, 34, 33, 35),
)
LINKS = {0: NZ - 1, EARLY - 1: EARLY}
SHARED = 50
N_RECV, N_SEND, N_LOCAL = SHARED + 16, 12, 6


class Keys:
    def __init__(self):
        self.at = {}

    def __call__(self, *key):
        return self.at.setdefault(key, len(self.at))


def kernel(
    pg_hbm, comp_hbm, prm_hbm, mom_hbm, probe_hbm,
    n_prm, n_mom, outb,
    v_pg, v_comp, out_s, cs, r_opp, r_fin, t_acc, prm, mom, q_s, sum_s,
    w, w_t, wy, pb, b_send, part, y_in,
    send_sem, recv_sem, loc_sem, go, go_late,
):
    rep = lax.axis_index("replica")
    fs = lax.axis_index("fsdp")
    t = lax.axis_index("tensor")
    x, core = rep // 2, rep % 2
    lo, z = fs // NZ, fs % NZ
    other = 1 - lo
    y = t * 2 + lo
    mate = t * 2 + other

    def dev(x_, core_, y_, z_):
        return (x_ * 2 + core_, (y_ % 2) * NZ + z_, y_ // 2)

    def xat(d):
        return lax.rem(x + d + NX, NX)

    def yat(d):
        return lax.rem(y + d + NY, NY)

    def zat(d):
        return lax.rem(z + d + NZ, NZ)

    def w_core(z_):
        return jnp.where(z_ < FIRST, 1, 0)

    wc = w_core(z)
    hc = 1 - wc
    w_dev, h_dev, me = dev(x, wc, y, z), dev(x, hc, y, z), dev(x, core, y, z)

    keys, sk, lk = {group: Keys() for group in "wpt"}, Keys(), Keys()

    def rsem(group, *key):
        at = keys[group](*key)
        return recv_sem.at[SHARED + at if group == "t" else at]

    def ssem(group):
        return send_sem.at[sk(group)]

    def send(src, dst, key, to, group):
        pltpu.make_async_remote_copy(
            src_ref=src, dst_ref=dst, send_sem=ssem(group), recv_sem=rsem(*key),
            device_id=to, device_id_type=MESH,
        ).start()

    def arrived(like, *key):
        pltpu.make_async_remote_copy(
            src_ref=like, dst_ref=like, send_sem=send_sem.at[0], recv_sem=rsem(*key),
            device_id=me, device_id_type=MESH,
        ).wait_recv()

    def sent(like, group):
        pltpu.make_async_remote_copy(
            src_ref=like, dst_ref=like, send_sem=ssem(group), recv_sem=recv_sem.at[0],
            device_id=me, device_id_type=MESH,
        ).wait_send()

    def load(src, dst, key):
        pltpu.make_async_copy(src, dst, loc_sem.at[lk(key)]).start()

    def loaded(like, key):
        pltpu.make_async_remote_copy(
            src_ref=like, dst_ref=like, send_sem=send_sem.at[0], recv_sem=loc_sem.at[lk(key)],
            device_id=me, device_id_type=MESH,
        ).wait_recv()

    def columns(kind, kc):
        half = lo if kind == "O" else other
        return pl.ds(pl.multiple_of((half * 2 + kc) * KC, KC), KC)

    def load_chunk(i):
        at = columns(*ORDER[i])
        load(pg_hbm.at[:, :, at], v_pg.at[i], ("in", i))
        load(comp_hbm.at[:, :, at], v_comp.at[i], ("in", i))

    barrier = pltpu.get_barrier_semaphore()

    def greet(to):
        pl.semaphore_signal(barrier, inc=1, device_id=to, device_id_type=MESH)

    def core_of_probe(zz):
        return 0 if zz < FIRST else 1

    def p_dev(y_, zz):
        return dev(x, core_of_probe(zz), y_, zz)

    def goes_to(src, zz):
        return core_of_probe(zz) if TREE[src].get(zz) else 1

    def senders(zz, to_core):
        found = {}
        for src in TREE:
            for q, to in TREE[src].items():
                if zz in to and goes_to(src, zz) == to_core:
                    found[0, q] = y
                    if q == src:
                        found[1, q] = mate
        if to_core == 1:
            found[1, zz] = mate
        if zz in LINKS and to_core == core_of_probe(zz):
            found[0, LINKS[zz]], found[1, LINKS[zz]] = y, mate
        return [(found[key], key[1]) for key in sorted(found)]

    late = z >= EARLY

    @pl.when(core == hc)
    def _():
        @pl.when(jnp.logical_not(late))
        def _():
            load_chunk(0)

        greet(w_dev)
        for zz in range(NZ):

            @pl.when(z == zz)
            def _():
                for yy, q in senders(zz, core_of_probe(zz)):
                    if not (q < EARLY <= zz):
                        greet(p_dev(yy, q))

        for kc in (0, 1):
            load(probe_hbm.at[x, :, columns("O", kc)], pb.at[lo, z, kc], "own")
            load(probe_hbm.at[x, :, columns("P", kc)], b_send.at[kc], "own")

        @pl.when(late)
        def _():
            load_chunk(0)

    @pl.when(core == wc)
    def _():
        for d in (1, -1):
            greet(dev(xat(d), wc, y, z))
            greet(dev(xat(d), wc, mate, z))

        @pl.when(wc == 0)
        def _():
            greet(dev(x, wc, mate, z))

        for zz in range(FIRST):

            @pl.when(z == zz)
            def _():
                for yy, q in senders(zz, 1):
                    greet(p_dev(yy, q))

        @pl.when(wc == 1)
        def _():
            for kc in (0, 1):
                load(probe_hbm.at[x, :, columns("O", kc)], pb.at[lo, z, kc], "own")

        @pl.when(late)
        def _():
            greet(h_dev)

        load_chunk(0)

    @pl.when(core == 1)
    def _():
        for d in range(1, NY):
            greet(dev(x, wc, yat(d), z))

    for i in (1, 2, 3):
        load_chunk(i)
    load(prm_hbm, prm, "state")
    load(mom_hbm, mom, "state")

    @pl.when(core == wc)
    def _():
        right, left, far = xat(1), xat(-1), xat(2)
        rdev, ldev = dev(right, wc, y, z), dev(left, wc, y, z)
        pl.semaphore_wait(barrier, 1 + 4 + 7 + hc)

        @pl.when(jnp.logical_not(late))
        def _():
            pl.semaphore_signal(go, inc=1, device_id=h_dev, device_id_type=MESH)

        def chip_sum(i, s):
            return v_pg[i, s].astype(F32) + v_comp[i, s] + out_s[i, s].astype(F32)

        def opposite(i):
            loaded(pb.at[0], ("in", i))
            arrived(out_s.at[i], "w", "push", i)
            for side, to in ((1, rdev), (0, ldev)):
                s = far * 2 + side
                cs[i, s] = chip_sum(i, s).astype(BF16)
                send(cs.at[i, s], r_opp.at[i, side], ("w", "opp", i, side), to, "rs")

        def direct(i):
            for side, to, xx in ((0, rdev, right), (1, ldev, left)):
                s = xx * 2 + side
                cs[i, s] = chip_sum(i, s).astype(BF16)
                send(cs.at[i, s], r_fin.at[i, side, 0], ("w", "fin", i), to, "rs")

        def on_the_way(i):
            for side, to, xx in ((1, rdev, right), (0, ldev, left)):
                s = xx * 2 + side
                arrived(r_opp.at[i, side], "w", "opp", i, side)
                t_acc[i, side] = (chip_sum(i, s) + r_opp[i, side].astype(F32)).astype(BF16)
                send(t_acc.at[i, side], r_fin.at[i, side, 1], ("w", "fin", i), to, "rs")

        opposite(0)
        opposite(1)
        direct(0)
        direct(1)
        opposite(2)
        opposite(3)
        on_the_way(0)
        on_the_way(1)
        direct(2)
        direct(3)
        on_the_way(2)
        on_the_way(3)

        loaded(v_comp.at[0], "state")
        arrived(q_s, "w", "q")

        def gather(src, kc, y_, rel):
            for side, to, first in ((1, right, True), (0, left, True), (0, right, False), (1, left, False)):
                key = ("w", "ag", kc, rel, side) if first else ("w", "rest", kc, rel)
                send(src.at[side], w.at[kc, lo, x, side], key, dev(to, wc, y_, z), "ag")

        def relay(kc, f, rel):
            for side, to, xx in ((1, rdev, left), (0, ldev, right)):
                ref = w.at[kc, f, xx, side]
                arrived(ref, "w", "ag", kc, rel, side)
                send(ref, ref, ("w", "rest", kc, rel), to, "ag")

        for i, (kind, kc) in enumerate(ORDER):
            at = columns(kind, kc)
            arrived(r_fin.at[i], "w", "fin", i)

            def average(side):
                return (
                    chip_sum(i, x * 2 + side)
                    + r_fin[i, side, 0].astype(F32)
                    + r_fin[i, side, 1].astype(F32)
                ) * 0.125

            avg = average(wc)
            m = NEST * mom[:, at] + avg
            new = prm[:, at] - RATE * (avg + NEST * m)
            n_mom[:, at] = m
            n_prm[:, at] = new
            avg = average(hc)
            sum_s[i] = avg
            new_h = q_s[:, at] - (RATE * (1 + NEST)) * avg
            if kind == "O":
                w[kc, lo, x, wc] = new.astype(BF16)
                w[kc, lo, x, hc] = new_h.astype(BF16)
                gather(w.at[kc, lo, x], kc, y, 0)
            else:
                wy[kc, wc] = new.astype(BF16)
                wy[kc, hc] = new_h.astype(BF16)
                gather(wy.at[kc], kc, mate, 1)
                for side in (0, 1):
                    send(wy.at[kc, side], w.at[kc, lo, x, side], ("w", "rest", kc, 1), dev(x, wc, mate, z), "ag")
            send(sum_s.at[i], sum_s.at[i], ("p", "sum"), h_dev, "sum")

        for rel, f in ((1, other), (0, lo)):
            for kc in (0, 1):
                relay(kc, f, rel)
        for rel, f in ((1, other), (0, lo)):
            for kc in (0, 1):
                arrived(w.at[kc, f, 0 : 2 + rel], "w", "rest", kc, rel)

                @pl.when(wc == 0)
                def _():
                    send(w.at[kc, f], w.at[kc, f], ("t", "wf"), h_dev, "wf")

    lane = {"A": lo, "B": other}

    def receivers(zz):
        found = set()
        for src in TREE:
            for to in TREE[src].get(zz, ()):
                if not (zz < EARLY <= to):
                    found.add((to, 0, goes_to(src, to)))
                    if src == zz:
                        found.add((to, 1, goes_to(src, to)))
        found.add((zz, 1, 1))
        for early_plane, late_plane in LINKS.items():
            if late_plane == zz:
                found |= {(early_plane, i, core_of_probe(early_plane)) for i in (0, 1)}
        return len(found)

    def hop(typ, src, kc, zz, to):
        ref = pb.at[lane[typ], src, kc]
        target = dev(x, goes_to(src, to), y, to)
        if TREE[src].get(to):
            send(ref, ref, ("p", "z", typ, src, kc), target, "relay")
        else:
            send(ref, ref, ("t", "in", src), target, "relay")

    def start(kc, zz, to):
        ref = pb.at[lo, zz, kc]
        core_ = goes_to(zz, to)
        for typ, from_, lane_ in (("A", ref, y), ("B", b_send.at[kc], mate)):
            key = ("p", "z", typ, zz, kc) if TREE[zz].get(to) else ("t", "in", zz)
            send(from_, ref, key, dev(x, core_, lane_, to), "own")

    def item(code):
        return "AB"[code % 2], code // 4, code // 2 % 2

    def begin(zz):
        loaded(pb.at[0, 0:2], "own")
        pl.semaphore_wait(barrier, receivers(zz) + (1 if zz >= EARLY else 0))
        for early_plane, late_plane in LINKS.items():
            if late_plane == zz:
                for yy in (y, mate):
                    to = p_dev(yy, early_plane)
                    pl.semaphore_signal(go_late, inc=1, device_id=to, device_id_type=MESH)
        for kc in (0, 1):
            for to in TREE[zz][zz]:
                if not (zz < EARLY <= to):
                    start(kc, zz, to)
            send(b_send.at[kc], pb.at[lo, zz, kc], ("t", "twin"), dev(x, 1, mate, zz), "own")

    def pass_on(zz):
        seen, missing, held = {}, set(), []
        for code in WAITS[zz]:
            if code < 0:
                pl.semaphore_wait(go_late, 2)
                for kc in (0, 1):
                    for to in TREE[zz][zz]:
                        if zz < EARLY <= to:
                            start(kc, zz, to)
                for one in held:
                    hop(*one)
                held = None
                continue
            typ, src, kc = item(code)
            arrived(pb.at[lane[typ], src, kc], "p", "z", typ, src, kc)
            for to in TREE[src][zz]:
                if zz < EARLY <= to and held is not None:
                    held.append((typ, src, kc, zz, to))
                else:
                    hop(typ, src, kc, zz, to)
            seen[src] = seen.get(src, 0) + 1
            if seen[src] == 4 and zz < FIRST:
                for typ in "AB":
                    ref = pb.at[lane[typ], src]
                    send(ref, ref, ("t", "in", src), w_dev, "fw")

    def probe_sent(zz):
        sent(pb.at[0, 0 : 2 * len(TREE[zz][zz]) + 1], "own")
        passed = [src for src in TREE if src != zz and TREE[src].get(zz)]
        count = sum(len(TREE[src][zz]) for src in passed)
        assert count <= NZ
        sent(pb.at[:, 0:count], "relay")
        if zz < FIRST:
            sent(pb.at[:, 0 : len(passed)], "fw")

    @pl.when(core == hc)
    def _():
        def pushes():
            for i in range(4):
                loaded(pb.at[0], ("in", i))
                out_s[i] = (v_pg[i].astype(F32) + v_comp[i]).astype(BF16)
                send(out_s.at[i], out_s.at[i], ("w", "push", i), w_dev, "push")
            loaded(v_comp.at[0], "state")
            q_s[...] = prm[...] - (RATE * NEST * NEST) * mom[...]
            send(q_s, q_s, ("w", "q"), w_dev, "q")

        @pl.when(jnp.logical_not(late))
        def _():
            pl.semaphore_wait(go, 1)
            pushes()

        for zz in range(NZ):
            pl.when(z == zz)(lambda zz=zz: begin(zz))

        @pl.when(late)
        def _():
            pushes()

        for zz in range(NZ):
            pl.when(z == zz)(lambda zz=zz: pass_on(zz))

    @pl.when(core == 1)
    def _():
        near = z // HALF

        @pl.when(wc == 0)
        def _():
            arrived(w, "t", "wf")

        @pl.when(wc == 1)
        def _():
            loaded(pb.at[0, 0], "own")

        for kc in (0, 1):
            w_t[kc] = w[kc].reshape(256, KC).T

        def wait_blocks(zz, want_near):
            if want_near:
                arrived(pb.at[0, 0], "t", "twin")
            for src in TREE:
                if src != zz and (src // HALF == zz // HALF) == want_near:
                    if zz < FIRST or not TREE[src].get(zz):
                        arrived(pb.at[0, 0:2], "t", "in", src)

        for phase in (0, 1):
            h = near if phase == 0 else 1 - near
            for zz in range(NZ):
                pl.when(z == zz)(lambda zz=zz: wait_blocks(zz, phase == 0))
            acc = jnp.zeros((2 * HALF * 16, 256), F32)
            for kc in (0, 1):
                rows = pb[:, pl.ds(h * HALF, HALF), kc].reshape(2 * HALF * 16, KC)
                acc += jnp.dot(rows, w_t[kc], preferred_element_type=F32)
            for lp in (0, 1):
                for lw in (0, 1):
                    piece = acc[lp * 96 : lp * 96 + 96, lw * 128 : lw * 128 + 128]
                    part[phase, lp, lw] = piece.astype(BF16).reshape(HALF, 16, 128)
            for lp in (0, 1):
                for lw in (0, 1):
                    to = 4 * lp + 2 * h + lw

                    @pl.when(to != y)
                    def _():
                        send(part.at[phase, lp, lw], y_in.at[y], ("t", "y"), dev(x, 1, to, z), "y")

                    @pl.when(to == y)
                    def _():
                        y_in[y] = part[phase, lp, lw]

        arrived(y_in.at[0:7], "t", "y")
        total = y_in[0].astype(F32)
        for i in range(1, NY):
            total += y_in[i].astype(F32)
        outb[:, x] = total.astype(BF16)
        mine = outb.at[:, x]
        for d in (2, 1, 3):
            for cc in (1, 0):
                send(mine, mine, ("t", "out"), dev(xat(d), cc, y, z), "out")
        send(mine, mine, ("t", "out"), dev(x, 0, y, z), "out")

    @pl.when(core == hc)
    def _():
        arrived(sum_s, "p", "sum")
        for i, (kind, kc) in enumerate(ORDER):
            at = columns(kind, kc)
            avg = sum_s[i]
            m = NEST * mom[:, at] + avg
            n_mom[:, at] = m
            n_prm[:, at] = prm[:, at] - RATE * (avg + NEST * m)
        sent(out_s, "push")
        sent(q_s, "q")
        for zz in range(NZ):
            pl.when(z == zz)(lambda zz=zz: probe_sent(zz))

    @pl.when(core == wc)
    def _():
        sent(pb.at[0], "rs")
        sent(pb.at[:, 0:7], "ag")
        sent(sum_s, "sum")

        @pl.when(wc == 0)
        def _():
            sent(w, "wf")

    @pl.when(core == 1)
    def _():
        sent(y_in.at[0:7], "y")
        sent(y_in.at[0:7], "out")
        arrived(y_in.at[0:3], "t", "out")

    @pl.when(core == 0)
    def _():
        arrived(y_in.at[0:4], "t", "out")

    assert max(len(keys[g].at) for g in "wp") <= SHARED and len(keys["t"].at) <= N_RECV - SHARED
    assert len(sk.at) <= N_SEND and len(lk.at) <= N_LOCAL


def store(a, b, c, a_out, b_out, c_out, sem):
    copies = [
        pltpu.make_async_copy(src, dst, sem.at[i])
        for i, (src, dst) in enumerate(((a, a_out), (b, b_out), (c, c_out)))
    ]
    for cp in copies:
        cp.start()
    for cp in copies:
        cp.wait()


def per_device(pseudo_grad, compensation, params, momentum, probe):
    any_space = pl.BlockSpec(memory_space=pl.ANY)
    vmem = pl.BlockSpec(memory_space=pltpu.VMEM)
    shapes = (
        jax.ShapeDtypeStruct((16, K), F32),
        jax.ShapeDtypeStruct((16, K), F32),
        jax.ShapeDtypeStruct((6, NX, 16, 128), BF16),
    )
    outs = pl.pallas_call(
        kernel,
        out_shape=tuple(pltpu.VMEM(s.shape, s.dtype) for s in shapes),
        in_specs=[any_space] * 5,
        out_specs=[vmem] * 3,
        scratch_shapes=[
            pltpu.VMEM((4, 8, 16, KC), BF16),
            pltpu.VMEM((4, 8, 16, KC), F32),
            pltpu.VMEM((4, 8, 16, KC), BF16),
            pltpu.VMEM((4, 8, 16, KC), BF16),
            pltpu.VMEM((4, 2, 16, KC), BF16),
            pltpu.VMEM((4, 2, 2, 16, KC), BF16),
            pltpu.VMEM((4, 2, 16, KC), BF16),
            pltpu.VMEM((16, K), F32),
            pltpu.VMEM((16, K), F32),
            pltpu.VMEM((16, K), F32),
            pltpu.VMEM((4, 16, KC), F32),
            pltpu.VMEM((2, 2, NX, 2, 16, KC), BF16),
            pltpu.VMEM((2, KC, 256), BF16),
            pltpu.VMEM((2, 2, 16, KC), BF16),
            pltpu.VMEM((2, NZ, 2, 16, KC), BF16),
            pltpu.VMEM((2, 16, KC), BF16),
            pltpu.VMEM((2, 2, 2, HALF, 16, 128), BF16),
            pltpu.VMEM((NY, HALF, 16, 128), BF16),
            pltpu.SemaphoreType.DMA((N_SEND,)),
            pltpu.SemaphoreType.DMA((N_RECV,)),
            pltpu.SemaphoreType.DMA((N_LOCAL,)),
            pltpu.SemaphoreType.REGULAR,
            pltpu.SemaphoreType.REGULAR,
        ],
        compiler_params=pltpu.CompilerParams(
            collective_id=0, has_side_effects=True, vmem_limit_bytes=60 * 2**20
        ),
    )(
        pseudo_grad.reshape(8, 16, K),
        compensation.reshape(8, 16, K),
        params,
        momentum,
        probe.reshape(NX, 16, K),
    )
    new_params, new_momentum, out = pl.pallas_call(
        store,
        out_shape=shapes,
        in_specs=[any_space] * 3,
        out_specs=[any_space] * 3,
        scratch_shapes=[pltpu.SemaphoreType.DMA((3,))],
        compiler_params=pltpu.CompilerParams(vmem_limit_bytes=2**20),
    )(*outs)
    return new_params, new_momentum, out.reshape(384, 128)


def solution(mesh):
    in_specs = (
        P("replica", "fsdp", "tensor"),
        P("replica", "fsdp", "tensor"),
        P(("fsdp", "replica"), "tensor"),
        P(("fsdp", "replica"), "tensor"),
        P("fsdp", "tensor"),
    )
    out_specs = (
        P(("fsdp", "replica"), "tensor"),
        P(("fsdp", "replica"), "tensor"),
        P("tensor", "fsdp"),
    )
    return jax.shard_map(
        per_device, mesh=mesh, in_specs=in_specs, out_specs=out_specs, check_vma=False
    )
```

time: 49.2 us -> 44.5 us (0.904)
  the two profiles are of different devices: /device:TPU:80 before, /device:TPU:1 now
where the time goes in v4:
time: 44.5 us; the launch traced here: 44.2 us
  Pallas kernels  43.6 us (98%)
  between operations  0.64 us (1%)
    pallas_call x1, Pallas kernels, per_device(): pl.pallas_call(kernel, out_shape=tuple((pltpu.VMEM(s.shape, s.dtype) for...  42.7 us

profile of v4, /device:TPU:1, one launch (start us, length us, event | category | flops | bytes accessed | tf_op | source)
XLA Modules:
  0.0 44.2 jit_solution(4769708640692953011)
XLA Ops:
  0.6 42.7 %shard_map.76 = (f32[16,4608]{1,0:T(8,128)S(1)}, f32[16,4608]{1,0:T(8,128)S(1)}, bf16[6,4,16,128]{3,2,1,0:T(8,128)(2,1)S(1)}) custom-call(bf16[8,16,4608]{2,1,0:T(8,128)(2,1)} %bitcast.5, f32[8,16,4608]{2,1,0:T(8,128)} %bitcast.4, f32[16,4608]{1,0:T(8,128)} %prm_hbm.1, f32[16,4608]{1,0:T(8,128)} %mom_hbm.1, bf16[4,16,4608]{2,1,0:T(8,128)(2,1)} %bitcast.6), custom_call_target="tpu_custom_call" | custom-call | tf_op jit(solution)/shard_map/pallas_call | solution.py:559
  43.3 0.9 %shard_map.77 = (f32[16,4608]{1,0:T(8,128)}, f32[16,4608]{1,0:T(8,128)}, bf16[6,4,16,128]{3,2,1,0:T(8,128)(2,1)}) custom-call(f32[16,4608]{1,0:T(8,128)S(1)} %get-tuple-element.9.a, f32[16,4608]{1,0:T(8,128)S(1)} %get-tuple-element.10.b, bf16[6,4,16,128]{3,2,1,0:T(8,128)(2,1)S(1)} %get-tuple-element.11.c), custom_call_target="tpu_custom_call" | custom-call | tf_op jit(solution)/shard_map/pallas_call | solution.py:599

commit v5 on v4

--- a/solution.py
+++ b/solution.py
@@ -426,18 +426,15 @@
             q_s[...] = prm[...] - (RATE * NEST * NEST) * mom[...]
             send(q_s, q_s, ("w", "q"), w_dev, "q")
 
-        @pl.when(jnp.logical_not(late))
-        def _():
+        def pushes_early():
             pl.semaphore_wait(go, 1)
             pushes()
 
+        pl.when(z < FIRST)(pushes_early)
         for zz in range(NZ):
             pl.when(z == zz)(lambda zz=zz: begin(zz))
-
-        @pl.when(late)
-        def _():
-            pushes()
-
+        pl.when(jnp.logical_and(z >= FIRST, z < EARLY))(pushes_early)
+        pl.when(late)(pushes)
         for zz in range(NZ):
             pl.when(z == zz)(lambda zz=zz: pass_on(zz))
 

time: 44.5 us -> 41.1 us (0.924)
  Pallas kernels: 43.6 us -> 39.8 us
    pallas_call x1, Pallas kernels: 42.7 us -> 38.9 us  [per_device(): pl.pallas_call(kernel, out_shape=tuple((pltpu.VMEM(s.shape, s.dtype) for...]
where the time goes in v5:
time: 41.1 us; the launch traced here: 40.4 us
  Pallas kernels  39.8 us (97%)
  between operations  0.64 us (2%)
    pallas_call x1, Pallas kernels, per_device(): pl.pallas_call(kernel, out_shape=tuple((pltpu.VMEM(s.shape, s.dtype) for...  38.9 us
    pallas_call x1, Pallas kernels, per_device(): pl.pallas_call(store, out_shape=shapes, in_specs=[any_space] * 3, out_spe...  0.86 us

profile of v5, /device:TPU:1, one launch (start us, length us, event | category | flops | bytes accessed | tf_op | source)
XLA Modules:
  0.0 40.4 jit_solution(5125057565129045532)
XLA Ops:
  0.6 38.9 %shard_map.76 = (f32[16,4608]{1,0:T(8,128)S(1)}, f32[16,4608]{1,0:T(8,128)S(1)}, bf16[6,4,16,128]{3,2,1,0:T(8,128)(2,1)S(1)}) custom-call(bf16[8,16,4608]{2,1,0:T(8,128)(2,1)} %bitcast.5, f32[8,16,4608]{2,1,0:T(8,128)} %bitcast.4, f32[16,4608]{1,0:T(8,128)} %prm_hbm.1, f32[16,4608]{1,0:T(8,128)} %mom_hbm.1, bf16[4,16,4608]{2,1,0:T(8,128)(2,1)} %bitcast.6), custom_call_target="tpu_custom_call" | custom-call | tf_op jit(solution)/shard_map/pallas_call | solution.py:556
  39.6 0.9 %shard_map.77 = (f32[16,4608]{1,0:T(8,128)}, f32[16,4608]{1,0:T(8,128)}, bf16[6,4,16,128]{3,2,1,0:T(8,128)(2,1)}) custom-call(f32[16,4608]{1,0:T(8,128)S(1)} %get-tuple-element.9.a, f32[16,4608]{1,0:T(8,128)S(1)} %get-tuple-element.10.b, bf16[6,4,16,128]{3,2,1,0:T(8,128)(2,1)S(1)} %get-tuple-element.11.c), custom_call_target="tpu_custom_call" | custom-call | tf_op jit(solution)/shard_map/pallas_call | solution.py:596

commit v6 on v5

--- a/solution.py
+++ b/solution.py
@@ -18,32 +18,32 @@
 EARLY = 6
 ORDER = (("P", 0), ("P", 1), ("O", 0), ("O", 1))
 TREE = {
-    0: {0: (1, 11,), 1: (2,), 2: (3,), 3: (4,), 4: (5,), 5: (6,), 8: (9, 7,), 10: (8,), 11: (10,)},
-    1: {0: (11,), 1: (2, 0,), 2: (3,), 3: (4,), 4: (5,), 5: (6,), 6: (7,), 9: (8, 10,), 11: (9,)},
-    2: {0: (11,), 1: (0,), 2: (1, 3,), 3: (4,), 4: (5,), 5: (6,), 6: (7,), 7: (8,), 10: (9,), 11: (10,)},
-    3: {0: (11,), 1: (0,), 2: (1,), 3: (2, 4,), 4: (5,), 5: (6,), 6: (7,), 7: (8,), 10: (9,), 11: (10,)},
-    4: {0: (11,), 1: (0,), 2: (1,), 3: (2,), 4: (3, 5,), 5: (6,), 6: (7,), 7: (8,), 8: (9,), 9: (10,)},
-    5: {1: (0,), 2: (1,), 3: (2,), 4: (3,), 5: (4, 6,), 6: (7,), 7: (8,), 8: (11, 9,), 9: (10,)},
-    6: {1: (0, 2,), 2: (3,), 4: (5,), 6: (4, 8, 7, 1,), 8: (9,), 9: (10,), 10: (11,)},
-    7: {2: (1,), 3: (2, 4,), 4: (5,), 6: (3,), 7: (8, 6,), 8: (9, 10,), 10: (11, 0,)},
-    8: {0: (1, 11,), 3: (2,), 4: (5, 3,), 5: (6,), 7: (4,), 8: (7, 9,), 9: (0,), 11: (10,)},
-    9: {0: (11, 1,), 1: (2,), 4: (3, 5,), 6: (4,), 7: (6, 8,), 9: (7, 0,), 11: (10,)},
-    10: {0: (1,), 1: (2,), 4: (3,), 6: (5,), 7: (6,), 8: (7,), 9: (4,), 10: (9, 8, 11,), 11: (0,)},
-    11: {1: (0, 2,), 2: (3,), 3: (4,), 6: (5, 7,), 9: (8,), 10: (9, 6,), 11: (1, 10,)},
+    0: {0: (1, 11,), 1: (2,), 2: (3,), 3: (4,), 4: (5,), 5: (6,), 9: (7, 8,), 10: (9,), 11: (10,)},
+    1: {0: (11,), 1: (2, 0,), 2: (3,), 3: (4,), 4: (5,), 5: (6,), 6: (7,), 10: (8, 9,), 11: (10,)},
+    2: {0: (11,), 1: (0,), 2: (3, 1,), 3: (4,), 4: (5,), 5: (6,), 6: (7,), 7: (8,), 10: (9,), 11: (10,)},
+    3: {0: (11,), 1: (0,), 2: (1,), 3: (4, 2,), 4: (5,), 5: (6,), 6: (7,), 7: (8,), 9: (10,), 11: (9,)},
+    4: {0: (11,), 1: (0,), 2: (1,), 3: (2,), 4: (3, 5,), 5: (6,), 6: (8,), 8: (9, 7,), 11: (10,)},
+    5: {1: (0,), 2: (1,), 3: (2,), 4: (3,), 5: (6, 4,), 6: (8,), 8: (9, 7,), 9: (10,), 10: (11,)},
+    6: {1: (0, 2,), 4: (3, 5,), 6: (7, 4, 1,), 7: (8,), 8: (9,), 9: (10,), 10: (11,)},
+    7: {0: (11,), 2: (1,), 3: (2, 4,), 4: (5,), 7: (3, 6, 8,), 8: (0, 9,), 11: (10,)},
+    8: {0: (1,), 3: (2, 4,), 6: (7, 3, 5,), 8: (0, 6, 9,), 9: (10,), 10: (11,)},
+    9: {1: (2,), 2: (3,), 5: (4,), 6: (5, 7,), 8: (6,), 9: (8, 10,), 10: (1, 11,), 11: (0,)},
+    10: {0: (11,), 1: (0, 2,), 2: (3,), 3: (4,), 6: (5,), 7: (6,), 8: (7,), 10: (8, 9, 1,)},
+    11: {2: (1, 3,), 5: (4,), 7: (6,), 8: (7,), 9: (0, 5,), 10: (9, 8,), 11: (10, 2,)},
 }
 WAITS = (
-    (4, 6, 5, 7, 8, 10, 9, 11, -1, 12, 14, 13, 15, 36, 40, 16, 38, 37, 42, 18, 41, 32, 17, 39, 43, 34, 19, 33, 35),
-    (0, 8, 2, 1, 10, 9, 3, 11, 12, 14, 13, 15, 16, 44, 18, 46, 45, 17, 24, 47, 19, 25, 26, 20, 22, 27, 36, 21, 40, 23, 38, 37, 42, 41, 39, 43),
-    (4, 6, 5, 12, 7, 0, 14, 2, 13, 1, 15, 3, 16, 18, 17, 19, 20, 22, 21, 44, 23, 46, 45, 24, 47, 28, 30, 25, 26, 29, 31, 27),
-    (8, 10, 9, 11, 4, 16, 6, 5, 18, 17, 7, 0, 19, 2, 1, 3, 20, 22, 21, 23, 28, 30, 29, 31, 44, 32, 46, 34, 45, 33, 47, 35),
-    (12, 14, 13, 8, 15, 10, 20, 9, 22, 11, 21, 4, 23, 24, 6, 5, 7, 0, 25, 26, 2, 1, 27, 3, 32, 34, 33, 35, 28, 40, 30, 36, 29, 41, 42, 31, 38, 37, 39, 43),
-    (16, 18, 17, 12, -1, 19, 14, 13, 8, 15, 10, 9, 11, 4, 6, 5, 0, 7, 2, 1, 32, 3, 34, 33, 35),
-    (28, 30, 20, 29, 22, 31, 21, 16, 23, 18, 17, 12, 19, 36, 14, 13, 8, 38, 15, 37, 10, 9, 39, 4, 11, 40, 6, 44, 5, 46, 7, 41, 42, 45, 47, 43),
-    (32, 34, 33, 36, 35, 38, 37, 20, 39, 22, 21, 16, 40, 23, 18, 17, 41, 12, 42, 19, 14, 13, 8, 43, 15, 10, 9, 11),
-    (28, 30, 29, 24, 31, 26, 25, 40, 27, 41, 42, 43, 20, 22, 21, 16, 23, 18, 17, 0, 19, 2, 1, 3),
-    (32, 40, 34, 33, 35, 41, 42, 43, 24, 44, 46, 45, 26, 25, 47, 27, 4, 20, 6, 22, 5, 21, 7, 16, 23, 18, 17, 19),
-    (44, 46, 45, 47, 28, 30, 0, 29, 2, 31, 1, 24, 3, 8, 26, 10, 25, 9, 27, 11, 12, 14, 13, 15),
-    (40, 42, 41, 43, 0, 2, 1, 3, 4, 6, 8, 5, 7, 10, 9, 11, 12, 14, 13, 15, 36, 38, 37, 32, 39, 34, 33, 35),
+    (4, -1, 5, 15, 13, 6, 10, 7, 11, 14, 8, 9, 12, 33, 32, 42, 41, 35, 43, 34, 40, 16, 28, 19, 30, 17, 29, 18, 31),
+    (1, 0, 3, 2, 9, 8, 10, 11, 15, 13, 12, 14, 40, 42, 41, 18, 43, 24, 26, 19, 16, 25, 38, 27, 37, 17, 20, 22, 21, 36, 39, 23),
+    (4, 6, 5, 7, 14, 15, 13, 12, 17, 18, 0, 3, 19, 2, 1, 16, 21, 22, 40, 20, 23, 42, 41, 44, 30, 43, 28, 46, 45, 47, 29, 31, 38, 37, 36, 39),
+    (10, 8, 18, 9, 11, 17, 16, 19, 4, 21, 7, 6, 5, 22, 23, 20, 28, 0, 30, 3, 1, 2, 29, 31, 40, 32, 34, 35, 41, 42, 33, 43),
+    (21, 20, 22, 8, 23, 12, 10, 13, 14, 11, 9, 4, 15, 25, 24, 27, 7, 6, 0, 30, 5, 1, 3, 2, 29, 28, 26, 31),
+    (-1, 16, 17, 18, 14, 19, 12, 10, 13, 9, 8, 15, 11, 4, 7, 6, 37, 5, 0, 44, 36, 38, 46, 1, 2, 3, 39, 47, 45),
+    (32, 35, 34, 23, 22, 20, 21, 33, 16, 18, 37, 17, 36, 13, 38, 14, 19, 40, 12, 39, 9, 42, 15, 10, 41, 8, 6, 43, 11, 4, 7, 5),
+    (24, 26, 25, 27, 40, 42, 41, 43, 44, 46, 47, 14, 45, 12, 13, 15, 9, 8, 10, 11),
+    (40, 37, 36, 30, 38, 24, 28, 41, 31, 42, 26, 29, 27, 43, 39, 25, 46, 44, 45, 23, 47, 20, 16, 21, 18, 22, 17, 19),
+    (44, 46, 47, 45, 35, 34, 33, 32, 1, 25, 26, 23, 3, 2, 0, 24, 27, 21, 20, 22, 14, 15, 13, 12),
+    (36, 38, 44, 46, 45, 37, 39, 47, 1, 2, 0, 3, 4, 5, 10, 35, 33, 11, 34, 25, 32, 6, 26, 7, 23, 9, 27, 24, 21, 8, 22, 20),
+    (1, 2, 0, 3, 36, 4, 38, 5, 6, 37, 15, 10, 11, 13, 14, 7, 9, 8, 12, 39, 28, 16, 30, 19, 17, 18, 29, 31),
 )
 LINKS = {0: NZ - 1, EARLY - 1: EARLY}
 SHARED = 50
@@ -63,7 +63,7 @@
     n_prm, n_mom, outb,
     v_pg, v_comp, out_s, cs, r_opp, r_fin, t_acc, prm, mom, q_s, sum_s,
     w, w_t, wy, pb, b_send, part, y_in,
-    send_sem, recv_sem, loc_sem, go, go_late,
+    send_sem, recv_sem, loc_sem, go, go_late, token,
 ):
     rep = lax.axis_index("replica")
     fs = lax.axis_index("fsdp")
@@ -196,10 +196,7 @@
         for d in (1, -1):
             greet(dev(xat(d), wc, y, z))
             greet(dev(xat(d), wc, mate, z))
-
-        @pl.when(wc == 0)
-        def _():
-            greet(dev(x, wc, mate, z))
+            greet(dev(x, wc, yat(d), z))
 
         for zz in range(FIRST):
 
@@ -219,11 +216,6 @@
 
         load_chunk(0)
 
-    @pl.when(core == 1)
-    def _():
-        for d in range(1, NY):
-            greet(dev(x, wc, yat(d), z))
-
     for i in (1, 2, 3):
         load_chunk(i)
     load(prm_hbm, prm, "state")
@@ -233,7 +225,17 @@
     def _():
         right, left, far = xat(1), xat(-1), xat(2)
         rdev, ldev = dev(right, wc, y, z), dev(left, wc, y, z)
-        pl.semaphore_wait(barrier, 1 + 4 + 7 + hc)
+        pl.semaphore_wait(barrier, 7)
+
+        def pass_token(step):
+            if step:
+                pl.semaphore_wait(token.at[step - 1], 2)
+            if step < NY // 2:
+                for d in (1, -1):
+                    to = dev(x, wc, yat(d), z)
+                    pl.semaphore_signal(token.at[step], inc=1, device_id=to, device_id_type=MESH)
+
+        pass_token(0)
 
         @pl.when(jnp.logical_not(late))
         def _():
@@ -269,12 +271,14 @@
         direct(1)
         opposite(2)
         opposite(3)
+        pass_token(1)
         on_the_way(0)
         on_the_way(1)
         direct(2)
         direct(3)
         on_the_way(2)
         on_the_way(3)
+        pass_token(2)
 
         loaded(v_comp.at[0], "state")
         arrived(q_s, "w", "q")
@@ -321,9 +325,11 @@
                     send(wy.at[kc, side], w.at[kc, lo, x, side], ("w", "rest", kc, 1), dev(x, wc, mate, z), "ag")
             send(sum_s.at[i], sum_s.at[i], ("p", "sum"), h_dev, "sum")
 
+        pass_token(3)
         for rel, f in ((1, other), (0, lo)):
             for kc in (0, 1):
                 relay(kc, f, rel)
+        pass_token(4)
         for rel, f in ((1, other), (0, lo)):
             for kc in (0, 1):
                 arrived(w.at[kc, f, 0 : 2 + rel], "w", "rest", kc, rel)
@@ -582,6 +588,7 @@
             pltpu.SemaphoreType.DMA((N_LOCAL,)),
             pltpu.SemaphoreType.REGULAR,
             pltpu.SemaphoreType.REGULAR,
+            pltpu.SemaphoreType.REGULAR((NY // 2,)),
         ],
         compiler_params=pltpu.CompilerParams(
             collective_id=0, has_side_effects=True, vmem_limit_bytes=60 * 2**20

time: 41.1 us -> 41.7 us (1.015); the launches traced: 40.4 us -> 41.5 us
  Pallas kernels: 39.8 us -> 40.9 us
    pallas_call x1, Pallas kernels: 38.9 us -> 40 us  [per_device(): pl.pallas_call(kernel, out_shape=tuple((pltpu.VMEM(s.shape, s.dtype) for...]
where the time goes in v6:
time: 41.7 us; the launch traced here: 41.5 us
  Pallas kernels  40.9 us (98%)
  between operations  0.64 us (2%)
    pallas_call x1, Pallas kernels, per_device(): pl.pallas_call(kernel, out_shape=tuple((pltpu.VMEM(s.shape, s.dtype) for...  40 us
    pallas_call x1, Pallas kernels, per_device(): pl.pallas_call(store, out_shape=shapes, in_specs=[any_space] * 3, out_spe...  0.86 us

profile of v6, /device:TPU:1, one launch (start us, length us, event | category | flops | bytes accessed | tf_op | source)
XLA Modules:
  0.0 41.5 jit_solution(6471099424414579317)
XLA Ops:
  0.6 40.0 %shard_map.76 = (f32[16,4608]{1,0:T(8,128)S(1)}, f32[16,4608]{1,0:T(8,128)S(1)}, bf16[6,4,16,128]{3,2,1,0:T(8,128)(2,1)S(1)}) custom-call(bf16[8,16,4608]{2,1,0:T(8,128)(2,1)} %bitcast.5, f32[8,16,4608]{2,1,0:T(8,128)} %bitcast.4, f32[16,4608]{1,0:T(8,128)} %prm_hbm.1, f32[16,4608]{1,0:T(8,128)} %mom_hbm.1, bf16[4,16,4608]{2,1,0:T(8,128)(2,1)} %bitcast.6), custom_call_target="tpu_custom_call" | custom-call | tf_op jit(solution)/shard_map/pallas_call | solution.py:562
  40.6 0.9 %shard_map.77 = (f32[16,4608]{1,0:T(8,128)}, f32[16,4608]{1,0:T(8,128)}, bf16[6,4,16,128]{3,2,1,0:T(8,128)(2,1)}) custom-call(f32[16,4608]{1,0:T(8,128)S(1)} %get-tuple-element.9.a, f32[16,4608]{1,0:T(8,128)S(1)} %get-tuple-element.10.b, bf16[6,4,16,128]{3,2,1,0:T(8,128)(2,1)S(1)} %get-tuple-element.11.c), custom_call_target="tpu_custom_call" | custom-call | tf_op jit(solution)/shard_map/pallas_call | solution.py:603

commit v7 on v6

--- a/solution.py
+++ b/solution.py
@@ -14,40 +14,39 @@
 K = 4608
 KC = K // 4
 HALF = NZ // 2
-FIRST = 1
 EARLY = 6
 ORDER = (("P", 0), ("P", 1), ("O", 0), ("O", 1))
 TREE = {
-    0: {0: (1, 11,), 1: (2,), 2: (3,), 3: (4,), 4: (5,), 5: (6,), 9: (7, 8,), 10: (9,), 11: (10,)},
-    1: {0: (11,), 1: (2, 0,), 2: (3,), 3: (4,), 4: (5,), 5: (6,), 6: (7,), 10: (8, 9,), 11: (10,)},
+    0: {0: (11, 1,), 1: (2,), 2: (3,), 3: (4,), 4: (5,), 5: (6,), 7: (8,), 9: (7,), 10: (9,), 11: (10,)},
+    1: {0: (11,), 1: (0, 2,), 2: (3,), 3: (4,), 4: (5,), 5: (6,), 6: (7,), 9: (8,), 10: (9,), 11: (10,)},
     2: {0: (11,), 1: (0,), 2: (3, 1,), 3: (4,), 4: (5,), 5: (6,), 6: (7,), 7: (8,), 10: (9,), 11: (10,)},
-    3: {0: (11,), 1: (0,), 2: (1,), 3: (4, 2,), 4: (5,), 5: (6,), 6: (7,), 7: (8,), 9: (10,), 11: (9,)},
-    4: {0: (11,), 1: (0,), 2: (1,), 3: (2,), 4: (3, 5,), 5: (6,), 6: (8,), 8: (9, 7,), 11: (10,)},
-    5: {1: (0,), 2: (1,), 3: (2,), 4: (3,), 5: (6, 4,), 6: (8,), 8: (9, 7,), 9: (10,), 10: (11,)},
-    6: {1: (0, 2,), 4: (3, 5,), 6: (7, 4, 1,), 7: (8,), 8: (9,), 9: (10,), 10: (11,)},
-    7: {0: (11,), 2: (1,), 3: (2, 4,), 4: (5,), 7: (3, 6, 8,), 8: (0, 9,), 11: (10,)},
-    8: {0: (1,), 3: (2, 4,), 6: (7, 3, 5,), 8: (0, 6, 9,), 9: (10,), 10: (11,)},
-    9: {1: (2,), 2: (3,), 5: (4,), 6: (5, 7,), 8: (6,), 9: (8, 10,), 10: (1, 11,), 11: (0,)},
-    10: {0: (11,), 1: (0, 2,), 2: (3,), 3: (4,), 6: (5,), 7: (6,), 8: (7,), 10: (8, 9, 1,)},
-    11: {2: (1, 3,), 5: (4,), 7: (6,), 8: (7,), 9: (0, 5,), 10: (9, 8,), 11: (10, 2,)},
+    3: {0: (11,), 1: (0,), 2: (1,), 3: (4, 2,), 4: (5,), 5: (6,), 6: (7,), 9: (10, 8,), 11: (9,)},
+    4: {0: (11,), 1: (0,), 2: (1,), 3: (2,), 4: (3, 5,), 5: (6,), 6: (8,), 8: (7, 9,), 11: (10,)},
+    5: {0: (11,), 1: (0,), 2: (1,), 3: (2,), 4: (3,), 5: (4, 6,), 6: (7,), 7: (9, 8,), 11: (10,)},
+    6: {2: (3, 1,), 4: (5,), 6: (4, 7, 8, 2,), 7: (0,), 8: (9,), 9: (11, 10,)},
+    7: {0: (1,), 3: (2,), 4: (3, 5,), 7: (8, 4,), 8: (6, 0, 9,), 9: (10,), 10: (11,)},
+    8: {2: (1, 3,), 3: (4,), 6: (2, 7,), 7: (5,), 8: (9, 6, 10,), 9: (0,), 10: (11,)},
+    9: {0: (1, 11,), 1: (2,), 5: (4, 6,), 7: (3, 5, 8,), 9: (7, 0,), 11: (10,)},
+    10: {0: (11,), 1: (0,), 2: (3, 1,), 3: (4,), 4: (5,), 7: (6,), 8: (7,), 10: (8, 9, 2,)},
+    11: {0: (1,), 2: (3,), 3: (4,), 6: (5,), 9: (7, 8,), 10: (0, 6, 9,), 11: (10, 2,)},
 }
 WAITS = (
-    (4, -1, 5, 15, 13, 6, 10, 7, 11, 14, 8, 9, 12, 33, 32, 42, 41, 35, 43, 34, 40, 16, 28, 19, 30, 17, 29, 18, 31),
-    (1, 0, 3, 2, 9, 8, 10, 11, 15, 13, 12, 14, 40, 42, 41, 18, 43, 24, 26, 19, 16, 25, 38, 27, 37, 17, 20, 22, 21, 36, 39, 23),
-    (4, 6, 5, 7, 14, 15, 13, 12, 17, 18, 0, 3, 19, 2, 1, 16, 21, 22, 40, 20, 23, 42, 41, 44, 30, 43, 28, 46, 45, 47, 29, 31, 38, 37, 36, 39),
-    (10, 8, 18, 9, 11, 17, 16, 19, 4, 21, 7, 6, 5, 22, 23, 20, 28, 0, 30, 3, 1, 2, 29, 31, 40, 32, 34, 35, 41, 42, 33, 43),
-    (21, 20, 22, 8, 23, 12, 10, 13, 14, 11, 9, 4, 15, 25, 24, 27, 7, 6, 0, 30, 5, 1, 3, 2, 29, 28, 26, 31),
-    (-1, 16, 17, 18, 14, 19, 12, 10, 13, 9, 8, 15, 11, 4, 7, 6, 37, 5, 0, 44, 36, 38, 46, 1, 2, 3, 39, 47, 45),
-    (32, 35, 34, 23, 22, 20, 21, 33, 16, 18, 37, 17, 36, 13, 38, 14, 19, 40, 12, 39, 9, 42, 15, 10, 41, 8, 6, 43, 11, 4, 7, 5),
-    (24, 26, 25, 27, 40, 42, 41, 43, 44, 46, 47, 14, 45, 12, 13, 15, 9, 8, 10, 11),
-    (40, 37, 36, 30, 38, 24, 28, 41, 31, 42, 26, 29, 27, 43, 39, 25, 46, 44, 45, 23, 47, 20, 16, 21, 18, 22, 17, 19),
-    (44, 46, 47, 45, 35, 34, 33, 32, 1, 25, 26, 23, 3, 2, 0, 24, 27, 21, 20, 22, 14, 15, 13, 12),
-    (36, 38, 44, 46, 45, 37, 39, 47, 1, 2, 0, 3, 4, 5, 10, 35, 33, 11, 34, 25, 32, 6, 26, 7, 23, 9, 27, 24, 21, 8, 22, 20),
-    (1, 2, 0, 3, 36, 4, 38, 5, 6, 37, 15, 10, 11, 13, 14, 7, 9, 8, 12, 39, 28, 16, 30, 19, 17, 18, 29, 31),
+    (-1, 5, 8, 7, 4, 6, 9, 15, 10, 11, 36, 39, 12, 38, 37, 14, 47, 28, 45, 19, 31, 13, 30, 17, 29, 18, 46, 44, 22, 16, 42, 21, 20, 23, 40, 41, 43),
+    (0, 2, 3, 1, 9, 8, 10, 11, 13, 15, 12, 19, 17, 14, 40, 16, 18, 41, 22, 36, 42, 43, 39, 21, 20, 38, 37, 23),
+    (6, 7, 0, 2, 5, 4, 3, 14, 1, 15, 13, 12, 17, 19, 18, 16, 46, 40, 44, 42, 41, 21, 22, 43, 20, 26, 23, 24, 25, 27, 45, 35, 47, 32, 33, 34),
+    (11, 8, 6, 7, 10, 18, 9, 0, 5, 17, 19, 16, 4, 2, 20, 3, 22, 21, 23, 1, 46, 30, 42, 44, 40, 31, 41, 43, 29, 28, 45, 35, 47, 32, 33, 34),
+    (20, 22, 8, 12, 21, 23, 14, 6, 11, 15, 13, 9, 10, 30, 7, 2, 0, 29, 3, 31, 26, 5, 1, 28, 4, 25, 42, 24, 40, 41, 43, 27),
+    (-1, 18, 17, 19, 16, 12, 14, 13, 8, 15, 2, 11, 7, 9, 3, 10, 36, 1, 5, 6, 0, 38, 4, 37, 39),
+    (35, 32, 33, 23, 34, 18, 22, 21, 17, 16, 20, 47, 14, 15, 44, 46, 19, 11, 45, 13, 12, 8, 10, 9, 7, 6, 5, 4),
+    (36, 38, 37, 24, 25, 26, 39, 27, 35, 32, 23, 40, 34, 21, 33, 22, 42, 41, 43, 20, 3, 11, 2, 8, 0, 1, 9, 10),
+    (28, 30, 31, 40, 42, 41, 29, 24, 25, 26, 43, 27, 17, 18, 16, 19),
+    (46, 34, 32, 47, 35, 33, 45, 30, 28, 44, 3, 2, 31, 29, 24, 0, 26, 1, 25, 7, 5, 27, 6, 15, 4, 14, 13, 12),
+    (46, 47, 45, 32, 44, 33, 3, 34, 2, 35, 0, 1, 5, 7, 6, 4, 8, 10, 11, 30, 9, 29, 31, 28),
+    (2, 3, 0, 1, 5, 7, 6, 8, 4, 10, 15, 11, 9, 39, 38, 36, 37, 14, 13, 12, 18, 19, 17, 16, 22, 20, 23, 21),
 )
 LINKS = {0: NZ - 1, EARLY - 1: EARLY}
 SHARED = 50
-N_RECV, N_SEND, N_LOCAL = SHARED + 16, 12, 6
+N_RECV, N_SEND, N_LOCAL = SHARED + 17, 12, 6
 
 
 class Keys:
@@ -62,7 +61,7 @@
     pg_hbm, comp_hbm, prm_hbm, mom_hbm, probe_hbm,
     n_prm, n_mom, outb,
     v_pg, v_comp, out_s, cs, r_opp, r_fin, t_acc, prm, mom, q_s, sum_s,
-    w, w_t, wy, pb, b_send, part, y_in,
+    w, w_t, wn, r_ag, pb, b_send, part, y_in,
     send_sem, recv_sem, loc_sem, go, go_late, token,
 ):
     rep = lax.axis_index("replica")
@@ -86,12 +85,7 @@
     def zat(d):
         return lax.rem(z + d + NZ, NZ)
 
-    def w_core(z_):
-        return jnp.where(z_ < FIRST, 1, 0)
-
-    wc = w_core(z)
-    hc = 1 - wc
-    w_dev, h_dev, me = dev(x, wc, y, z), dev(x, hc, y, z), dev(x, core, y, z)
+    w_dev, h_dev, me = dev(x, 0, y, z), dev(x, 1, y, z), dev(x, core, y, z)
 
     keys, sk, lk = {group: Keys() for group in "wpt"}, Keys(), Keys()
 
@@ -143,32 +137,24 @@
     def greet(to):
         pl.semaphore_signal(barrier, inc=1, device_id=to, device_id_type=MESH)
 
-    def core_of_probe(zz):
-        return 0 if zz < FIRST else 1
-
     def p_dev(y_, zz):
-        return dev(x, core_of_probe(zz), y_, zz)
-
-    def goes_to(src, zz):
-        return core_of_probe(zz) if TREE[src].get(zz) else 1
-
-    def senders(zz, to_core):
-        found = {}
+        return dev(x, 1, y_, zz)
+
+    def senders(zz):
+        found = {(1, zz): mate}
         for src in TREE:
             for q, to in TREE[src].items():
-                if zz in to and goes_to(src, zz) == to_core:
+                if zz in to:
                     found[0, q] = y
                     if q == src:
                         found[1, q] = mate
-        if to_core == 1:
-            found[1, zz] = mate
-        if zz in LINKS and to_core == core_of_probe(zz):
+        if zz in LINKS:
             found[0, LINKS[zz]], found[1, LINKS[zz]] = y, mate
         return [(found[key], key[1]) for key in sorted(found)]
 
     late = z >= EARLY
 
-    @pl.when(core == hc)
+    @pl.when(core == 1)
     def _():
         @pl.when(jnp.logical_not(late))
         def _():
@@ -179,7 +165,7 @@
 
             @pl.when(z == zz)
             def _():
-                for yy, q in senders(zz, core_of_probe(zz)):
+                for yy, q in senders(zz):
                     if not (q < EARLY <= zz):
                         greet(p_dev(yy, q))
 
@@ -191,55 +177,42 @@
         def _():
             load_chunk(0)
 
-    @pl.when(core == wc)
-    def _():
+    @pl.when(core == 0)
+    def _():
+        load_chunk(0)
         for d in (1, -1):
-            greet(dev(xat(d), wc, y, z))
-            greet(dev(xat(d), wc, mate, z))
-            greet(dev(x, wc, yat(d), z))
-
-        for zz in range(FIRST):
-
-            @pl.when(z == zz)
-            def _():
-                for yy, q in senders(zz, 1):
-                    greet(p_dev(yy, q))
-
-        @pl.when(wc == 1)
-        def _():
-            for kc in (0, 1):
-                load(probe_hbm.at[x, :, columns("O", kc)], pb.at[lo, z, kc], "own")
+            greet(dev(xat(d), 0, y, z))
+            greet(dev(xat(d), 0, mate, z))
+            greet(dev(x, 0, yat(d), z))
 
         @pl.when(late)
         def _():
             greet(h_dev)
-
-        load_chunk(0)
 
     for i in (1, 2, 3):
         load_chunk(i)
     load(prm_hbm, prm, "state")
     load(mom_hbm, mom, "state")
 
-    @pl.when(core == wc)
+    @pl.when(core == 0)
     def _():
         right, left, far = xat(1), xat(-1), xat(2)
-        rdev, ldev = dev(right, wc, y, z), dev(left, wc, y, z)
+        rdev, ldev = dev(right, 0, y, z), dev(left, 0, y, z)
         pl.semaphore_wait(barrier, 7)
+
+        @pl.when(jnp.logical_not(late))
+        def _():
+            pl.semaphore_signal(go, inc=1, device_id=h_dev, device_id_type=MESH)
 
         def pass_token(step):
             if step:
                 pl.semaphore_wait(token.at[step - 1], 2)
             if step < NY // 2:
                 for d in (1, -1):
-                    to = dev(x, wc, yat(d), z)
+                    to = dev(x, 0, yat(d), z)
                     pl.semaphore_signal(token.at[step], inc=1, device_id=to, device_id_type=MESH)
 
         pass_token(0)
-
-        @pl.when(jnp.logical_not(late))
-        def _():
-            pl.semaphore_signal(go, inc=1, device_id=h_dev, device_id_type=MESH)
 
         def chip_sum(i, s):
             return v_pg[i, s].astype(F32) + v_comp[i, s] + out_s[i, s].astype(F32)
@@ -283,16 +256,26 @@
         loaded(v_comp.at[0], "state")
         arrived(q_s, "w", "q")
 
-        def gather(src, kc, y_, rel):
-            for side, to, first in ((1, right, True), (0, left, True), (0, right, False), (1, left, False)):
-                key = ("w", "ag", kc, rel, side) if first else ("w", "rest", kc, rel)
-                send(src.at[side], w.at[kc, lo, x, side], key, dev(to, wc, y_, z), "ag")
-
-        def relay(kc, f, rel):
-            for side, to, xx in ((1, rdev, left), (0, ldev, right)):
-                ref = w.at[kc, f, xx, side]
+        def gather(src, kc, kind, first):
+            y_, rel = (y, 0) if kind == "O" else (mate, 1)
+            for side, xx in ((1, right), (0, left)):
+                if first:
+                    send(src.at[side], r_ag.at[kc, rel, side], ("w", "ag", kc, rel, side), dev(xx, 0, y_, z), "ag")
+            if not first:
+                for side, xx in ((0, right), (1, left), (0, x), (1, x)):
+                    send(src.at[side], w.at[kc, lo, x, side], ("t", "w", kc), dev(xx, 1, y_, z), "ag")
+
+        def relay(kc, rel):
+            f = other if rel else lo
+            for side, to, xx in ((1, right, left), (0, left, right)):
+                ref = r_ag.at[kc, rel, side]
                 arrived(ref, "w", "ag", kc, rel, side)
-                send(ref, ref, ("w", "rest", kc, rel), to, "ag")
+                for x_ in (to, x):
+                    send(ref, w.at[kc, f, xx, side], ("t", "w", kc), dev(x_, 1, y, z), "ag")
+
+        def block(i):
+            kind, kc = ORDER[i]
+            return wn.at[i], kc, kind
 
         for i, (kind, kc) in enumerate(ORDER):
             at = columns(kind, kc)
@@ -305,58 +288,46 @@
                     + r_fin[i, side, 1].astype(F32)
                 ) * 0.125
 
-            avg = average(wc)
+            avg = average(0)
             m = NEST * mom[:, at] + avg
             new = prm[:, at] - RATE * (avg + NEST * m)
             n_mom[:, at] = m
             n_prm[:, at] = new
-            avg = average(hc)
+            wn[i, 0] = new.astype(BF16)
+            avg = average(1)
             sum_s[i] = avg
-            new_h = q_s[:, at] - (RATE * (1 + NEST)) * avg
-            if kind == "O":
-                w[kc, lo, x, wc] = new.astype(BF16)
-                w[kc, lo, x, hc] = new_h.astype(BF16)
-                gather(w.at[kc, lo, x], kc, y, 0)
-            else:
-                wy[kc, wc] = new.astype(BF16)
-                wy[kc, hc] = new_h.astype(BF16)
-                gather(wy.at[kc], kc, mate, 1)
-                for side in (0, 1):
-                    send(wy.at[kc, side], w.at[kc, lo, x, side], ("w", "rest", kc, 1), dev(x, wc, mate, z), "ag")
+            wn[i, 1] = (q_s[:, at] - (RATE * (1 + NEST)) * avg).astype(BF16)
+            gather(*block(i), True)
+            if i == 1:
+                gather(*block(0), False)
+        for i in (2, 1, 3):
+            gather(*block(i), False)
+        for i in range(4):
             send(sum_s.at[i], sum_s.at[i], ("p", "sum"), h_dev, "sum")
 
         pass_token(3)
-        for rel, f in ((1, other), (0, lo)):
-            for kc in (0, 1):
-                relay(kc, f, rel)
+        relay(0, 1)
+        relay(1, 1)
+        relay(0, 0)
         pass_token(4)
-        for rel, f in ((1, other), (0, lo)):
-            for kc in (0, 1):
-                arrived(w.at[kc, f, 0 : 2 + rel], "w", "rest", kc, rel)
-
-                @pl.when(wc == 0)
-                def _():
-                    send(w.at[kc, f], w.at[kc, f], ("t", "wf"), h_dev, "wf")
+        relay(1, 0)
 
     lane = {"A": lo, "B": other}
 
     def receivers(zz):
-        found = set()
+        found = {(zz, 1)}
         for src in TREE:
             for to in TREE[src].get(zz, ()):
                 if not (zz < EARLY <= to):
-                    found.add((to, 0, goes_to(src, to)))
-                    if src == zz:
-                        found.add((to, 1, goes_to(src, to)))
-        found.add((zz, 1, 1))
+                    found |= {(to, 0), (to, 1)} if src == zz else {(to, 0)}
         for early_plane, late_plane in LINKS.items():
             if late_plane == zz:
-                found |= {(early_plane, i, core_of_probe(early_plane)) for i in (0, 1)}
+                found |= {(early_plane, 0), (early_plane, 1)}
         return len(found)
 
     def hop(typ, src, kc, zz, to):
         ref = pb.at[lane[typ], src, kc]
-        target = dev(x, goes_to(src, to), y, to)
+        target = dev(x, 1, y, to)
         if TREE[src].get(to):
             send(ref, ref, ("p", "z", typ, src, kc), target, "relay")
         else:
@@ -364,10 +335,9 @@
 
     def start(kc, zz, to):
         ref = pb.at[lo, zz, kc]
-        core_ = goes_to(zz, to)
         for typ, from_, lane_ in (("A", ref, y), ("B", b_send.at[kc], mate)):
             key = ("p", "z", typ, zz, kc) if TREE[zz].get(to) else ("t", "in", zz)
-            send(from_, ref, key, dev(x, core_, lane_, to), "own")
+            send(from_, ref, key, dev(x, 1, lane_, to), "own")
 
     def item(code):
         return "AB"[code % 2], code // 4, code // 2 % 2
@@ -387,7 +357,7 @@
             send(b_send.at[kc], pb.at[lo, zz, kc], ("t", "twin"), dev(x, 1, mate, zz), "own")
 
     def pass_on(zz):
-        seen, missing, held = {}, set(), []
+        held = []
         for code in WAITS[zz]:
             if code < 0:
                 pl.semaphore_wait(go_late, 2)
@@ -406,11 +376,6 @@
                     held.append((typ, src, kc, zz, to))
                 else:
                     hop(typ, src, kc, zz, to)
-            seen[src] = seen.get(src, 0) + 1
-            if seen[src] == 4 and zz < FIRST:
-                for typ in "AB":
-                    ref = pb.at[lane[typ], src]
-                    send(ref, ref, ("t", "in", src), w_dev, "fw")
 
     def probe_sent(zz):
         sent(pb.at[0, 0 : 2 * len(TREE[zz][zz]) + 1], "own")
@@ -418,29 +383,43 @@
         count = sum(len(TREE[src][zz]) for src in passed)
         assert count <= NZ
         sent(pb.at[:, 0:count], "relay")
-        if zz < FIRST:
-            sent(pb.at[:, 0 : len(passed)], "fw")
-
-    @pl.when(core == hc)
-    def _():
-        def pushes():
-            for i in range(4):
-                loaded(pb.at[0], ("in", i))
-                out_s[i] = (v_pg[i].astype(F32) + v_comp[i]).astype(BF16)
-                send(out_s.at[i], out_s.at[i], ("w", "push", i), w_dev, "push")
-            loaded(v_comp.at[0], "state")
-            q_s[...] = prm[...] - (RATE * NEST * NEST) * mom[...]
-            send(q_s, q_s, ("w", "q"), w_dev, "q")
-
-        def pushes_early():
-            pl.semaphore_wait(go, 1)
-            pushes()
-
-        pl.when(z < FIRST)(pushes_early)
+
+    @pl.when(core == 1)
+    def _():
+        def prepare(i):
+            loaded(pb.at[0], ("in", i))
+            out_s[i] = (v_pg[i].astype(F32) + v_comp[i]).astype(BF16)
+
+        def push(i):
+            send(out_s.at[i], out_s.at[i], ("w", "push", i), w_dev, "push")
+
+        prepare(0)
+
+        @pl.when(jnp.logical_not(late))
+        def _():
+            prepare(1)
+            prepare(2)
+            prepare(3)
+
         for zz in range(NZ):
             pl.when(z == zz)(lambda zz=zz: begin(zz))
-        pl.when(jnp.logical_and(z >= FIRST, z < EARLY))(pushes_early)
-        pl.when(late)(pushes)
+
+        @pl.when(jnp.logical_not(late))
+        def _():
+            pl.semaphore_wait(go, 1)
+            for i in range(4):
+                push(i)
+
+        @pl.when(late)
+        def _():
+            push(0)
+            for i in (1, 2, 3):
+                prepare(i)
+                push(i)
+
+        loaded(v_comp.at[0], "state")
+        q_s[...] = prm[...] - (RATE * NEST * NEST) * mom[...]
+        send(q_s, q_s, ("w", "q"), w_dev, "q")
         for zz in range(NZ):
             pl.when(z == zz)(lambda zz=zz: pass_on(zz))
 
@@ -448,15 +427,8 @@
     def _():
         near = z // HALF
 
-        @pl.when(wc == 0)
-        def _():
-            arrived(w, "t", "wf")
-
-        @pl.when(wc == 1)
-        def _():
-            loaded(pb.at[0, 0], "own")
-
         for kc in (0, 1):
+            arrived(w.at[kc], "t", "w", kc)
             w_t[kc] = w[kc].reshape(256, KC).T
 
         def wait_blocks(zz, want_near):
@@ -464,7 +436,7 @@
                 arrived(pb.at[0, 0], "t", "twin")
             for src in TREE:
                 if src != zz and (src // HALF == zz // HALF) == want_near:
-                    if zz < FIRST or not TREE[src].get(zz):
+                    if not TREE[src].get(zz):
                         arrived(pb.at[0, 0:2], "t", "in", src)
 
         for phase in (0, 1):
@@ -502,7 +474,7 @@
                 send(mine, mine, ("t", "out"), dev(xat(d), cc, y, z), "out")
         send(mine, mine, ("t", "out"), dev(x, 0, y, z), "out")
 
-    @pl.when(core == hc)
+    @pl.when(core == 1)
     def _():
         arrived(sum_s, "p", "sum")
         for i, (kind, kc) in enumerate(ORDER):
@@ -516,15 +488,11 @@
         for zz in range(NZ):
             pl.when(z == zz)(lambda zz=zz: probe_sent(zz))
 
-    @pl.when(core == wc)
+    @pl.when(core == 0)
     def _():
         sent(pb.at[0], "rs")
-        sent(pb.at[:, 0:7], "ag")
+        sent(pb.at[:, 0:10], "ag")
         sent(sum_s, "sum")
-
-        @pl.when(wc == 0)
-        def _():
-            sent(w, "wf")
 
     @pl.when(core == 1)
     def _():
@@ -578,7 +546,8 @@
             pltpu.VMEM((4, 16, KC), F32),
             pltpu.VMEM((2, 2, NX, 2, 16, KC), BF16),
             pltpu.VMEM((2, KC, 256), BF16),
-            pltpu.VMEM((2, 2, 16, KC), BF16),
+            pltpu.VMEM((4, 2, 16, KC), BF16),
+            pltpu.VMEM((2, 2, 2, 16, KC), BF16),
             pltpu.VMEM((2, NZ, 2, 16, KC), BF16),
             pltpu.VMEM((2, 16, KC), BF16),
             pltpu.VMEM((2, 2, 2, HALF, 16, 128), BF16),

time: 41.7 us -> 50.4 us (1.21)
  Pallas kernels: 40.9 us -> 49.6 us
    pallas_call x1, Pallas kernels: 40 us -> 48.7 us  [per_device(): pl.pallas_call(kernel, out_shape=tuple((pltpu.VMEM(s.shape, s.dtype) for...]
where the time goes in v7:
time: 50.4 us; the launch traced here: 50.2 us
  Pallas kernels  49.6 us (98%)
  between operations  0.64 us (1%)
    pallas_call x1, Pallas kernels, per_device(): pl.pallas_call(kernel, out_shape=tuple((pltpu.VMEM(s.shape, s.dtype) for...  48.7 us

profile of v7, /device:TPU:1, one launch (start us, length us, event | category | flops | bytes accessed | tf_op | source)
XLA Modules:
  0.0 50.2 jit_solution(509688643184433433)
XLA Ops:
  0.6 48.7 %shard_map.76 = (f32[16,4608]{1,0:T(8,128)S(1)}, f32[16,4608]{1,0:T(8,128)S(1)}, bf16[6,4,16,128]{3,2,1,0:T(8,128)(2,1)S(1)}) custom-call(bf16[8,16,4608]{2,1,0:T(8,128)(2,1)} %bitcast.5, f32[8,16,4608]{2,1,0:T(8,128)} %bitcast.4, f32[16,4608]{1,0:T(8,128)} %prm_hbm.1, f32[16,4608]{1,0:T(8,128)} %mom_hbm.1, bf16[4,16,4608]{2,1,0:T(8,128)(2,1)} %bitcast.6), custom_call_target="tpu_custom_call" | custom-call | tf_op jit(solution)/shard_map/pallas_call | solution.py:530
  49.4 0.9 %shard_map.77 = (f32[16,4608]{1,0:T(8,128)}, f32[16,4608]{1,0:T(8,128)}, bf16[6,4,16,128]{3,2,1,0:T(8,128)(2,1)}) custom-call(f32[16,4608]{1,0:T(8,128)S(1)} %get-tuple-element.9.a, f32[16,4608]{1,0:T(8,128)S(1)} %get-tuple-element.10.b, bf16[6,4,16,128]{3,2,1,0:T(8,128)(2,1)S(1)} %get-tuple-element.11.c), custom_call_target="tpu_custom_call" | custom-call | tf_op jit(solution)/shard_map/pallas_call | solution.py:572

commit v8 on v7

--- a/solution.py
+++ b/solution.py
@@ -17,32 +17,32 @@
 EARLY = 6
 ORDER = (("P", 0), ("P", 1), ("O", 0), ("O", 1))
 TREE = {
-    0: {0: (11, 1,), 1: (2,), 2: (3,), 3: (4,), 4: (5,), 5: (6,), 7: (8,), 9: (7,), 10: (9,), 11: (10,)},
-    1: {0: (11,), 1: (0, 2,), 2: (3,), 3: (4,), 4: (5,), 5: (6,), 6: (7,), 9: (8,), 10: (9,), 11: (10,)},
+    0: {0: (1, 11,), 1: (2,), 2: (3,), 3: (4,), 4: (5,), 5: (6,), 9: (7, 8,), 10: (9,), 11: (10,)},
+    1: {0: (11,), 1: (2, 0,), 2: (3,), 3: (4,), 4: (5,), 5: (6,), 6: (7,), 10: (8, 9,), 11: (10,)},
     2: {0: (11,), 1: (0,), 2: (3, 1,), 3: (4,), 4: (5,), 5: (6,), 6: (7,), 7: (8,), 10: (9,), 11: (10,)},
-    3: {0: (11,), 1: (0,), 2: (1,), 3: (4, 2,), 4: (5,), 5: (6,), 6: (7,), 9: (10, 8,), 11: (9,)},
-    4: {0: (11,), 1: (0,), 2: (1,), 3: (2,), 4: (3, 5,), 5: (6,), 6: (8,), 8: (7, 9,), 11: (10,)},
-    5: {0: (11,), 1: (0,), 2: (1,), 3: (2,), 4: (3,), 5: (4, 6,), 6: (7,), 7: (9, 8,), 11: (10,)},
-    6: {2: (3, 1,), 4: (5,), 6: (4, 7, 8, 2,), 7: (0,), 8: (9,), 9: (11, 10,)},
-    7: {0: (1,), 3: (2,), 4: (3, 5,), 7: (8, 4,), 8: (6, 0, 9,), 9: (10,), 10: (11,)},
-    8: {2: (1, 3,), 3: (4,), 6: (2, 7,), 7: (5,), 8: (9, 6, 10,), 9: (0,), 10: (11,)},
-    9: {0: (1, 11,), 1: (2,), 5: (4, 6,), 7: (3, 5, 8,), 9: (7, 0,), 11: (10,)},
-    10: {0: (11,), 1: (0,), 2: (3, 1,), 3: (4,), 4: (5,), 7: (6,), 8: (7,), 10: (8, 9, 2,)},
-    11: {0: (1,), 2: (3,), 3: (4,), 6: (5,), 9: (7, 8,), 10: (0, 6, 9,), 11: (10, 2,)},
+    3: {0: (11,), 1: (0,), 2: (1,), 3: (4, 2,), 4: (5,), 5: (6,), 6: (7,), 7: (8,), 9: (10,), 11: (9,)},
+    4: {0: (11,), 1: (0,), 2: (1,), 3: (2,), 4: (3, 5,), 5: (6,), 6: (8,), 8: (9, 7,), 11: (10,)},
+    5: {1: (0,), 2: (1,), 3: (2,), 4: (3,), 5: (6, 4,), 6: (8,), 8: (9, 7,), 9: (10,), 10: (11,)},
+    6: {1: (0, 2,), 4: (3, 5,), 6: (7, 4, 1,), 7: (8,), 8: (9,), 9: (10,), 10: (11,)},
+    7: {0: (11,), 2: (1,), 3: (2, 4,), 4: (5,), 7: (3, 6, 8,), 8: (0, 9,), 11: (10,)},
+    8: {0: (1,), 3: (2, 4,), 6: (7, 3, 5,), 8: (0, 6, 9,), 9: (10,), 10: (11,)},
+    9: {1: (2,), 2: (3,), 5: (4,), 6: (5, 7,), 8: (6,), 9: (8, 10,), 10: (1, 11,), 11: (0,)},
+    10: {0: (11,), 1: (0, 2,), 2: (3,), 3: (4,), 6: (5,), 7: (6,), 8: (7,), 10: (8, 9, 1,)},
+    11: {2: (1, 3,), 5: (4,), 7: (6,), 8: (7,), 9: (0, 5,), 10: (9, 8,), 11: (10, 2,)},
 }
 WAITS = (
-    (-1, 5, 8, 7, 4, 6, 9, 15, 10, 11, 36, 39, 12, 38, 37, 14, 47, 28, 45, 19, 31, 13, 30, 17, 29, 18, 46, 44, 22, 16, 42, 21, 20, 23, 40, 41, 43),
-    (0, 2, 3, 1, 9, 8, 10, 11, 13, 15, 12, 19, 17, 14, 40, 16, 18, 41, 22, 36, 42, 43, 39, 21, 20, 38, 37, 23),
-    (6, 7, 0, 2, 5, 4, 3, 14, 1, 15, 13, 12, 17, 19, 18, 16, 46, 40, 44, 42, 41, 21, 22, 43, 20, 26, 23, 24, 25, 27, 45, 35, 47, 32, 33, 34),
-    (11, 8, 6, 7, 10, 18, 9, 0, 5, 17, 19, 16, 4, 2, 20, 3, 22, 21, 23, 1, 46, 30, 42, 44, 40, 31, 41, 43, 29, 28, 45, 35, 47, 32, 33, 34),
-    (20, 22, 8, 12, 21, 23, 14, 6, 11, 15, 13, 9, 10, 30, 7, 2, 0, 29, 3, 31, 26, 5, 1, 28, 4, 25, 42, 24, 40, 41, 43, 27),
-    (-1, 18, 17, 19, 16, 12, 14, 13, 8, 15, 2, 11, 7, 9, 3, 10, 36, 1, 5, 6, 0, 38, 4, 37, 39),
-    (35, 32, 33, 23, 34, 18, 22, 21, 17, 16, 20, 47, 14, 15, 44, 46, 19, 11, 45, 13, 12, 8, 10, 9, 7, 6, 5, 4),
-    (36, 38, 37, 24, 25, 26, 39, 27, 35, 32, 23, 40, 34, 21, 33, 22, 42, 41, 43, 20, 3, 11, 2, 8, 0, 1, 9, 10),
-    (28, 30, 31, 40, 42, 41, 29, 24, 25, 26, 43, 27, 17, 18, 16, 19),
-    (46, 34, 32, 47, 35, 33, 45, 30, 28, 44, 3, 2, 31, 29, 24, 0, 26, 1, 25, 7, 5, 27, 6, 15, 4, 14, 13, 12),
-    (46, 47, 45, 32, 44, 33, 3, 34, 2, 35, 0, 1, 5, 7, 6, 4, 8, 10, 11, 30, 9, 29, 31, 28),
-    (2, 3, 0, 1, 5, 7, 6, 8, 4, 10, 15, 11, 9, 39, 38, 36, 37, 14, 13, 12, 18, 19, 17, 16, 22, 20, 23, 21),
+    (4, -1, 5, 15, 13, 6, 10, 7, 11, 14, 8, 9, 12, 33, 32, 42, 41, 35, 43, 34, 40, 16, 28, 19, 30, 17, 29, 18, 31),
+    (1, 0, 3, 2, 9, 8, 10, 11, 15, 13, 12, 14, 40, 42, 41, 18, 43, 24, 26, 19, 16, 25, 38, 27, 37, 17, 20, 22, 21, 36, 39, 23),
+    (4, 6, 5, 7, 14, 15, 13, 12, 17, 18, 0, 3, 19, 2, 1, 16, 21, 22, 40, 20, 23, 42, 41, 44, 30, 43, 28, 46, 45, 47, 29, 31, 38, 37, 36, 39),
+    (10, 8, 18, 9, 11, 17, 16, 19, 4, 21, 7, 6, 5, 22, 23, 20, 28, 0, 30, 3, 1, 2, 29, 31, 40, 32, 34, 35, 41, 42, 33, 43),
+    (21, 20, 22, 8, 23, 12, 10, 13, 14, 11, 9, 4, 15, 25, 24, 27, 7, 6, 0, 30, 5, 1, 3, 2, 29, 28, 26, 31),
+    (-1, 16, 17, 18, 14, 19, 12, 10, 13, 9, 8, 15, 11, 4, 7, 6, 37, 5, 0, 44, 36, 38, 46, 1, 2, 3, 39, 47, 45),
+    (32, 35, 34, 23, 22, 20, 21, 33, 16, 18, 37, 17, 36, 13, 38, 14, 19, 40, 12, 39, 9, 42, 15, 10, 41, 8, 6, 43, 11, 4, 7, 5),
+    (24, 26, 25, 27, 40, 42, 41, 43, 44, 46, 47, 14, 45, 12, 13, 15, 9, 8, 10, 11),
+    (40, 37, 36, 30, 38, 24, 28, 41, 31, 42, 26, 29, 27, 43, 39, 25, 46, 44, 45, 23, 47, 20, 16, 21, 18, 22, 17, 19),
+    (44, 46, 47, 45, 35, 34, 33, 32, 1, 25, 26, 23, 3, 2, 0, 24, 27, 21, 20, 22, 14, 15, 13, 12),
+    (36, 38, 44, 46, 45, 37, 39, 47, 1, 2, 0, 3, 4, 5, 10, 35, 33, 11, 34, 25, 32, 6, 26, 7, 23, 9, 27, 24, 21, 8, 22, 20),
+    (1, 2, 0, 3, 36, 4, 38, 5, 6, 37, 15, 10, 11, 13, 14, 7, 9, 8, 12, 39, 28, 16, 30, 19, 17, 18, 29, 31),
 )
 LINKS = {0: NZ - 1, EARLY - 1: EARLY}
 SHARED = 50

time: 50.4 us -> 43.8 us (0.87)
  Pallas kernels: 49.6 us -> 43 us
    pallas_call x1, Pallas kernels: 48.7 us -> 42.2 us  [per_device(): pl.pallas_call(kernel, out_shape=tuple((pltpu.VMEM(s.shape, s.dtype) for...]
where the time goes in v8:
time: 43.8 us; the launch traced here: 43.7 us
  Pallas kernels  43 us (98%)
  between operations  0.64 us (1%)
    pallas_call x1, Pallas kernels, per_device(): pl.pallas_call(kernel, out_shape=tuple((pltpu.VMEM(s.shape, s.dtype) for...  42.2 us

profile of v8, /device:TPU:1, one launch (start us, length us, event | category | flops | bytes accessed | tf_op | source)
XLA Modules:
  0.0 43.7 jit_solution(5859700744508323190)
XLA Ops:
  0.6 42.2 %shard_map.76 = (f32[16,4608]{1,0:T(8,128)S(1)}, f32[16,4608]{1,0:T(8,128)S(1)}, bf16[6,4,16,128]{3,2,1,0:T(8,128)(2,1)S(1)}) custom-call(bf16[8,16,4608]{2,1,0:T(8,128)(2,1)} %bitcast.5, f32[8,16,4608]{2,1,0:T(8,128)} %bitcast.4, f32[16,4608]{1,0:T(8,128)} %prm_hbm.1, f32[16,4608]{1,0:T(8,128)} %mom_hbm.1, bf16[4,16,4608]{2,1,0:T(8,128)(2,1)} %bitcast.6), custom_call_target="tpu_custom_call" | custom-call | tf_op jit(solution)/shard_map/pallas_call | solution.py:530
  42.8 0.9 %shard_map.77 = (f32[16,4608]{1,0:T(8,128)}, f32[16,4608]{1,0:T(8,128)}, bf16[6,4,16,128]{3,2,1,0:T(8,128)(2,1)}) custom-call(f32[16,4608]{1,0:T(8,128)S(1)} %get-tuple-element.9.a, f32[16,4608]{1,0:T(8,128)S(1)} %get-tuple-element.10.b, bf16[6,4,16,128]{3,2,1,0:T(8,128)(2,1)S(1)} %get-tuple-element.11.c), custom_call_target="tpu_custom_call" | custom-call | tf_op jit(solution)/shard_map/pallas_call | solution.py:572

commit v9 on v8

--- a/solution.py
+++ b/solution.py
@@ -1,3 +1,5 @@
+import functools
+
 import jax
 import jax.numpy as jnp
 from jax import lax
@@ -17,36 +19,37 @@
 EARLY = 6
 ORDER = (("P", 0), ("P", 1), ("O", 0), ("O", 1))
 TREE = {
-    0: {0: (1, 11,), 1: (2,), 2: (3,), 3: (4,), 4: (5,), 5: (6,), 9: (7, 8,), 10: (9,), 11: (10,)},
-    1: {0: (11,), 1: (2, 0,), 2: (3,), 3: (4,), 4: (5,), 5: (6,), 6: (7,), 10: (8, 9,), 11: (10,)},
-    2: {0: (11,), 1: (0,), 2: (3, 1,), 3: (4,), 4: (5,), 5: (6,), 6: (7,), 7: (8,), 10: (9,), 11: (10,)},
-    3: {0: (11,), 1: (0,), 2: (1,), 3: (4, 2,), 4: (5,), 5: (6,), 6: (7,), 7: (8,), 9: (10,), 11: (9,)},
-    4: {0: (11,), 1: (0,), 2: (1,), 3: (2,), 4: (3, 5,), 5: (6,), 6: (8,), 8: (9, 7,), 11: (10,)},
-    5: {1: (0,), 2: (1,), 3: (2,), 4: (3,), 5: (6, 4,), 6: (8,), 8: (9, 7,), 9: (10,), 10: (11,)},
-    6: {1: (0, 2,), 4: (3, 5,), 6: (7, 4, 1,), 7: (8,), 8: (9,), 9: (10,), 10: (11,)},
-    7: {0: (11,), 2: (1,), 3: (2, 4,), 4: (5,), 7: (3, 6, 8,), 8: (0, 9,), 11: (10,)},
-    8: {0: (1,), 3: (2, 4,), 6: (7, 3, 5,), 8: (0, 6, 9,), 9: (10,), 10: (11,)},
-    9: {1: (2,), 2: (3,), 5: (4,), 6: (5, 7,), 8: (6,), 9: (8, 10,), 10: (1, 11,), 11: (0,)},
-    10: {0: (11,), 1: (0, 2,), 2: (3,), 3: (4,), 6: (5,), 7: (6,), 8: (7,), 10: (8, 9, 1,)},
-    11: {2: (1, 3,), 5: (4,), 7: (6,), 8: (7,), 9: (0, 5,), 10: (9, 8,), 11: (10, 2,)},
+    0: {0: (1, 11,), 1: (2,), 2: (3,), 3: (4,), 4: (5,), 5: (6,), 8: (9, 7,), 9: (10,), 11: (8,)},
+    1: {0: (11,), 1: (2, 0,), 2: (3,), 3: (4,), 4: (5,), 5: (6,), 7: (8,), 9: (10, 7,), 11: (9,)},
+    2: {0: (11,), 2: (3, 0, 1,), 3: (4,), 4: (5,), 5: (6,), 6: (7,), 9: (8,), 10: (9,), 11: (10,)},
+    3: {0: (11,), 3: (0, 2, 4, 1,), 4: (5,), 5: (6,), 6: (7,), 7: (8,), 10: (9,), 11: (10,)},
+    4: {0: (1, 11,), 2: (0, 3,), 4: (5, 2,), 5: (6,), 6: (7,), 7: (8,), 8: (9,), 11: (10,)},
+    5: {2: (1,), 3: (0, 2,), 5: (3, 4, 6,), 6: (7,), 7: (10, 8,), 8: (9,), 10: (11,)},
+    6: {0: (11,), 1: (2, 0,), 2: (3,), 4: (1, 5,), 6: (4, 7,), 7: (8,), 8: (9,), 9: (10,)},
+    7: {4: (5, 2, 3,), 7: (4, 6, 10,), 9: (8,), 10: (9, 11, 0, 1,)},
+    8: {0: (1, 11,), 3: (2,), 5: (6, 3, 4,), 6: (7,), 8: (9, 5,), 9: (0,), 11: (10,)},
+    9: {0: (1,), 3: (2, 4,), 6: (3, 5, 7,), 7: (8,), 9: (11, 6,), 11: (0, 10,)},
+    10: {0: (11,), 1: (0, 2,), 2: (3,), 3: (4,), 6: (5,), 7: (6,), 8: (7,), 10: (1, 9, 8,)},
+    11: {1: (0, 2,), 2: (3,), 5: (4,), 7: (6,), 8: (7, 5,), 10: (9,), 11: (8, 1, 10,)},
 }
 WAITS = (
-    (4, -1, 5, 15, 13, 6, 10, 7, 11, 14, 8, 9, 12, 33, 32, 42, 41, 35, 43, 34, 40, 16, 28, 19, 30, 17, 29, 18, 31),
-    (1, 0, 3, 2, 9, 8, 10, 11, 15, 13, 12, 14, 40, 42, 41, 18, 43, 24, 26, 19, 16, 25, 38, 27, 37, 17, 20, 22, 21, 36, 39, 23),
-    (4, 6, 5, 7, 14, 15, 13, 12, 17, 18, 0, 3, 19, 2, 1, 16, 21, 22, 40, 20, 23, 42, 41, 44, 30, 43, 28, 46, 45, 47, 29, 31, 38, 37, 36, 39),
-    (10, 8, 18, 9, 11, 17, 16, 19, 4, 21, 7, 6, 5, 22, 23, 20, 28, 0, 30, 3, 1, 2, 29, 31, 40, 32, 34, 35, 41, 42, 33, 43),
-    (21, 20, 22, 8, 23, 12, 10, 13, 14, 11, 9, 4, 15, 25, 24, 27, 7, 6, 0, 30, 5, 1, 3, 2, 29, 28, 26, 31),
-    (-1, 16, 17, 18, 14, 19, 12, 10, 13, 9, 8, 15, 11, 4, 7, 6, 37, 5, 0, 44, 36, 38, 46, 1, 2, 3, 39, 47, 45),
-    (32, 35, 34, 23, 22, 20, 21, 33, 16, 18, 37, 17, 36, 13, 38, 14, 19, 40, 12, 39, 9, 42, 15, 10, 41, 8, 6, 43, 11, 4, 7, 5),
-    (24, 26, 25, 27, 40, 42, 41, 43, 44, 46, 47, 14, 45, 12, 13, 15, 9, 8, 10, 11),
-    (40, 37, 36, 30, 38, 24, 28, 41, 31, 42, 26, 29, 27, 43, 39, 25, 46, 44, 45, 23, 47, 20, 16, 21, 18, 22, 17, 19),
-    (44, 46, 47, 45, 35, 34, 33, 32, 1, 25, 26, 23, 3, 2, 0, 24, 27, 21, 20, 22, 14, 15, 13, 12),
-    (36, 38, 44, 46, 45, 37, 39, 47, 1, 2, 0, 3, 4, 5, 10, 35, 33, 11, 34, 25, 32, 6, 26, 7, 23, 9, 27, 24, 21, 8, 22, 20),
-    (1, 2, 0, 3, 36, 4, 38, 5, 6, 37, 15, 10, 11, 13, 14, 7, 9, 8, 12, 39, 28, 16, 30, 19, 17, 18, 29, 31),
+    (1, 3, 10, 6, 8, 4, 5, -1, 7, 12, 18, 9, 11, 14, 15, 16, 13, 17, 19, 32, 36, 34, 35, 38, 33, 40, 41, 43, 37, 42, 39, 25, 24, 27, 26),
+    (5, 7, 0, 3, 2, 1, 46, 40, 41, 43, 47, 44, 45, 42, 26, 25, 24, 27),
+    (9, 5, 6, 4, 0, 11, 7, 16, 3, 1, 18, 2, 17, 19, 40, 46, 41, 43, 47, 45, 22, 20, 42, 26, 21, 44, 25, 23, 24, 27),
+    (9, 13, 5, 8, 11, 15, 10, 20, 6, 4, 7, 0, 21, 22, 3, 2, 1, 23, 32, 36, 34, 40, 37, 43, 35, 38, 41, 33, 42, 39),
+    (14, 17, 12, 19, 13, 9, 5, 24, 26, 11, 8, 15, 10, 25, 27, 28, 7, 4, 3, 30, 0, 1, 2, 6, 31, 29),
+    (-1, 21, 23, 19, 16, 14, 18, 34, 12, 32, 17, 9, 13, 10, 35, 33, 15, 11, 8, 4, 7, 0, 3, 5, 1, 2, 6, 44, 47, 46, 45),
+    (25, 27, 20, 21, 23, 36, 22, 19, 16, 34, 37, 14, 18, 17, 38, 12, 35, 32, 10, 39, 15, 13, 11, 40, 8, 9, 33, 42, 41, 43),
+    (24, 27, 25, 31, 26, 29, 21, 42, 20, 40, 19, 23, 22, 36, 16, 44, 41, 18, 43, 17, 37, 46, 45, 14, 47, 38, 12, 15, 39, 13, 5, 7, 4, 6),
+    (35, 33, 40, 42, 44, 25, 41, 47, 27, 24, 43, 26, 46, 45, 2, 0, 20, 3, 1, 21, 23, 22, 19, 18, 17, 16),
+    (37, 32, 34, 39, 35, 33, 25, 30, 27, 28, 5, 24, 7, 4, 31, 26, 2, 6, 0, 29, 3, 1, 8, 10, 9, 11),
+    (41, 43, 30, 28, 46, 31, 47, 29, 44, 8, 12, 10, 23, 45, 15, 21, 20, 9, 11, 22, 14, 13),
+    (45, 47, 36, 38, 2, 3, 1, 6, 0, 10, 37, 4, 5, 7, 8, 12, 39, 15, 9, 13, 11, 14, 32, 17, 16, 19, 33, 35, 34, 18),
 )
 LINKS = {0: NZ - 1, EARLY - 1: EARLY}
-SHARED = 50
-N_RECV, N_SEND, N_LOCAL = SHARED + 17, 12, 6
+FAR_FIRST, SPLIT = (), {}
+SHARED = 49
+N_RECV, N_SEND, N_LOCAL = SHARED + 6, 10, 6
 
 
 class Keys:
@@ -62,7 +65,7 @@
     n_prm, n_mom, outb,
     v_pg, v_comp, out_s, cs, r_opp, r_fin, t_acc, prm, mom, q_s, sum_s,
     w, w_t, wn, r_ag, pb, b_send, part, y_in,
-    send_sem, recv_sem, loc_sem, go, go_late, token,
+    send_sem, recv_sem, loc_sem, go, go_late, both, token,
 ):
     rep = lax.axis_index("replica")
     fs = lax.axis_index("fsdp")
@@ -141,18 +144,17 @@
         return dev(x, 1, y_, zz)
 
     def senders(zz):
-        found = {(1, zz): mate}
+        found = {(1, zz): mate, (2, zz): jnp.where(lo == 1, yat(1), yat(-1))}
         for src in TREE:
             for q, to in TREE[src].items():
                 if zz in to:
                     found[0, q] = y
-                    if q == src:
-                        found[1, q] = mate
         if zz in LINKS:
-            found[0, LINKS[zz]], found[1, LINKS[zz]] = y, mate
+            found[0, LINKS[zz]] = y
         return [(found[key], key[1]) for key in sorted(found)]
 
     late = z >= EARLY
+    apart = jnp.logical_and(z == 0, jnp.logical_and(x == 0, y == 0))
 
     @pl.when(core == 1)
     def _():
@@ -183,9 +185,9 @@
         for d in (1, -1):
             greet(dev(xat(d), 0, y, z))
             greet(dev(xat(d), 0, mate, z))
-            greet(dev(x, 0, yat(d), z))
-
-        @pl.when(late)
+        greet(dev(x, 0, mate, z))
+
+        @pl.when(jnp.logical_not(apart))
         def _():
             greet(h_dev)
 
@@ -198,21 +200,13 @@
     def _():
         right, left, far = xat(1), xat(-1), xat(2)
         rdev, ldev = dev(right, 0, y, z), dev(left, 0, y, z)
-        pl.semaphore_wait(barrier, 7)
-
-        @pl.when(jnp.logical_not(late))
+        pl.semaphore_wait(barrier, 6)
+
+        @pl.when(apart)
         def _():
             pl.semaphore_signal(go, inc=1, device_id=h_dev, device_id_type=MESH)
 
-        def pass_token(step):
-            if step:
-                pl.semaphore_wait(token.at[step - 1], 2)
-            if step < NY // 2:
-                for d in (1, -1):
-                    to = dev(x, 0, yat(d), z)
-                    pl.semaphore_signal(token.at[step], inc=1, device_id=to, device_id_type=MESH)
-
-        pass_token(0)
+        pl.semaphore_signal(both, inc=1, device_id=dev(x, 0, mate, z), device_id_type=MESH)
 
         def chip_sum(i, s):
             return v_pg[i, s].astype(F32) + v_comp[i, s] + out_s[i, s].astype(F32)
@@ -244,14 +238,13 @@
         direct(1)
         opposite(2)
         opposite(3)
-        pass_token(1)
+        pl.semaphore_wait(both, 1)
         on_the_way(0)
         on_the_way(1)
         direct(2)
         direct(3)
         on_the_way(2)
         on_the_way(3)
-        pass_token(2)
 
         loaded(v_comp.at[0], "state")
         arrived(q_s, "w", "q")
@@ -305,80 +298,96 @@
         for i in range(4):
             send(sum_s.at[i], sum_s.at[i], ("p", "sum"), h_dev, "sum")
 
-        pass_token(3)
         relay(0, 1)
         relay(1, 1)
         relay(0, 0)
-        pass_token(4)
         relay(1, 0)
 
     lane = {"A": lo, "B": other}
 
     def receivers(zz):
-        found = {(zz, 1)}
+        found = {(zz, 1), (zz, 2)}
         for src in TREE:
             for to in TREE[src].get(zz, ()):
                 if not (zz < EARLY <= to):
-                    found |= {(to, 0), (to, 1)} if src == zz else {(to, 0)}
+                    found.add((to, 0))
         for early_plane, late_plane in LINKS.items():
             if late_plane == zz:
-                found |= {(early_plane, 0), (early_plane, 1)}
+                found.add((early_plane, 0))
         return len(found)
 
     def hop(typ, src, kc, zz, to):
         ref = pb.at[lane[typ], src, kc]
         target = dev(x, 1, y, to)
-        if TREE[src].get(to):
-            send(ref, ref, ("p", "z", typ, src, kc), target, "relay")
-        else:
-            send(ref, ref, ("t", "in", src), target, "relay")
+        key = ("p", "z", typ, src, kc) if TREE[src].get(to) else ("t", "in", src // HALF == to // HALF)
+        send(ref, ref, key, target, "twin" if src == zz else "relay")
 
     def start(kc, zz, to):
         ref = pb.at[lo, zz, kc]
-        for typ, from_, lane_ in (("A", ref, y), ("B", b_send.at[kc], mate)):
-            key = ("p", "z", typ, zz, kc) if TREE[zz].get(to) else ("t", "in", zz)
-            send(from_, ref, key, dev(x, 1, lane_, to), "own")
+        key = ("p", "z", "A", zz, kc) if TREE[zz].get(to) else ("t", "in", zz // HALF == to // HALF)
+        send(ref, ref, key, dev(x, 1, y, to), "own")
 
     def item(code):
         return "AB"[code % 2], code // 4, code // 2 % 2
 
+    def pass_token(step):
+        if step:
+            pl.semaphore_wait(token.at[step - 1], 2)
+        if step < 3:
+            for d in (1, -1):
+                to = dev(x, 1, yat(d), z)
+                pl.semaphore_signal(token.at[step], inc=1, device_id=to, device_id_type=MESH)
+
     def begin(zz):
         loaded(pb.at[0, 0:2], "own")
-        pl.semaphore_wait(barrier, receivers(zz) + (1 if zz >= EARLY else 0))
+        pl.semaphore_wait(barrier, receivers(zz) + (jnp.where(apart, 0, 1) if zz == 0 else 1))
         for early_plane, late_plane in LINKS.items():
             if late_plane == zz:
-                for yy in (y, mate):
-                    to = p_dev(yy, early_plane)
-                    pl.semaphore_signal(go_late, inc=1, device_id=to, device_id_type=MESH)
+                to = p_dev(y, early_plane)
+                pl.semaphore_signal(go_late, inc=1, device_id=to, device_id_type=MESH)
         for kc in (0, 1):
+            send(b_send.at[kc], pb.at[lo, zz, kc], ("p", "z", "B", zz, kc), dev(x, 1, mate, zz), "own")
             for to in TREE[zz][zz]:
                 if not (zz < EARLY <= to):
                     start(kc, zz, to)
-            send(b_send.at[kc], pb.at[lo, zz, kc], ("t", "twin"), dev(x, 1, mate, zz), "own")
 
     def pass_on(zz):
-        held = []
-        for code in WAITS[zz]:
+        steps, held, count = [], [], len(WAITS[zz])
+
+        def late_planes():
+            pl.semaphore_wait(go_late, 1)
+            for kc in (0, 1):
+                for to in TREE[zz][zz]:
+                    if zz < EARLY <= to:
+                        start(kc, zz, to)
+
+        def one(typ, src, kc, targets):
+            arrived(pb.at[lane[typ], src, kc], "p", "z", typ, src, kc)
+            for to in targets:
+                hop(typ, src, kc, zz, to)
+
+        for n, code in enumerate(WAITS[zz]):
+            if n in (count // 3, 2 * count // 3):
+                steps.append(functools.partial(pass_token, 1 if n == count // 3 else 2))
             if code < 0:
-                pl.semaphore_wait(go_late, 2)
-                for kc in (0, 1):
-                    for to in TREE[zz][zz]:
-                        if zz < EARLY <= to:
-                            start(kc, zz, to)
-                for one in held:
-                    hop(*one)
+                steps.append(late_planes)
+                steps += [functools.partial(hop, *what) for what in held]
                 held = None
                 continue
             typ, src, kc = item(code)
-            arrived(pb.at[lane[typ], src, kc], "p", "z", typ, src, kc)
-            for to in TREE[src][zz]:
-                if zz < EARLY <= to and held is not None:
-                    held.append((typ, src, kc, zz, to))
-                else:
-                    hop(typ, src, kc, zz, to)
+            wait = [to for to in TREE[src][zz] if zz < EARLY <= to and held is not None]
+            if wait:
+                held += [(typ, src, kc, zz, to) for to in wait]
+            steps.append(functools.partial(one, typ, src, kc, [to for to in TREE[src][zz] if to not in wait]))
+        return steps
+
+    def run(steps):
+        for step in steps:
+            step()
 
     def probe_sent(zz):
-        sent(pb.at[0, 0 : 2 * len(TREE[zz][zz]) + 1], "own")
+        sent(pb.at[0, 0 : len(TREE[zz][zz]) + 1], "own")
+        sent(pb.at[0, 0 : len(TREE[zz][zz])], "twin")
         passed = [src for src in TREE if src != zz and TREE[src].get(zz)]
         count = sum(len(TREE[src][zz]) for src in passed)
         assert count <= NZ
@@ -403,10 +412,14 @@
 
         for zz in range(NZ):
             pl.when(z == zz)(lambda zz=zz: begin(zz))
+        pass_token(0)
+
+        @pl.when(apart)
+        def _():
+            pl.semaphore_wait(go, 1)
 
         @pl.when(jnp.logical_not(late))
         def _():
-            pl.semaphore_wait(go, 1)
             for i in range(4):
                 push(i)
 
@@ -421,28 +434,32 @@
         q_s[...] = prm[...] - (RATE * NEST * NEST) * mom[...]
         send(q_s, q_s, ("w", "q"), w_dev, "q")
         for zz in range(NZ):
-            pl.when(z == zz)(lambda zz=zz: pass_on(zz))
-
-    @pl.when(core == 1)
-    def _():
+            steps = pass_on(zz)
+            pl.when(z == zz)(functools.partial(run, steps[: SPLIT.get(zz, len(steps))]))
+
         near = z // HALF
-
-        for kc in (0, 1):
-            arrived(w.at[kc], "t", "w", kc)
-            w_t[kc] = w[kc].reshape(256, KC).T
-
-        def wait_blocks(zz, want_near):
-            if want_near:
-                arrived(pb.at[0, 0], "t", "twin")
-            for src in TREE:
-                if src != zz and (src // HALF == zz // HALF) == want_near:
-                    if not TREE[src].get(zz):
-                        arrived(pb.at[0, 0:2], "t", "in", src)
-
-        for phase in (0, 1):
-            h = near if phase == 0 else 1 - near
+        far_first = functools.reduce(jnp.logical_or, [z == zz for zz in FAR_FIRST], z < 0)
+
+        def weights():
+            for kc in (0, 1):
+                arrived(w.at[kc], "t", "w", kc)
+                w_t[kc] = w[kc].reshape(256, KC).T
+
+        def wait_blocks(zz, phase):
+            want_near = (phase == 0) != (zz in FAR_FIRST)
+            stop = [
+                src for src in TREE
+                if src != zz and (src // HALF == zz // HALF) == want_near and not TREE[src].get(zz)
+            ]
+            if stop:
+                arrived(pb.at[:, 0 : len(stop)], "t", "in", want_near)
+
+        def multiply(phase):
+            h = jnp.where(far_first, 1 - near, near)
+            if phase:
+                h = 1 - h
             for zz in range(NZ):
-                pl.when(z == zz)(lambda zz=zz: wait_blocks(zz, phase == 0))
+                pl.when(z == zz)(functools.partial(wait_blocks, zz, phase))
             acc = jnp.zeros((2 * HALF * 16, 256), F32)
             for kc in (0, 1):
                 rows = pb[:, pl.ds(h * HALF, HALF), kc].reshape(2 * HALF * 16, KC)
@@ -451,17 +468,30 @@
                 for lw in (0, 1):
                     piece = acc[lp * 96 : lp * 96 + 96, lw * 128 : lw * 128 + 128]
                     part[phase, lp, lw] = piece.astype(BF16).reshape(HALF, 16, 128)
-            for lp in (0, 1):
-                for lw in (0, 1):
-                    to = 4 * lp + 2 * h + lw
-
-                    @pl.when(to != y)
-                    def _():
-                        send(part.at[phase, lp, lw], y_in.at[y], ("t", "y"), dev(x, 1, to, z), "y")
-
-                    @pl.when(to == y)
-                    def _():
-                        y_in[y] = part[phase, lp, lw]
+            for d in (4, 3, 5, 2, 6, 1, 7):
+                to = yat(d)
+
+                @pl.when(to // 2 % 2 == h)
+                def _():
+                    send(part.at[phase, to // 4, to % 2], y_in.at[y], ("t", "y"), dev(x, 1, to, z), "y")
+
+            @pl.when(y // 2 % 2 == h)
+            def _():
+                y_in[y] = part[phase, y // 4, y % 2]
+
+        soon = jnp.logical_and(functools.reduce(jnp.logical_or, [z == zz for zz in SPLIT], z < 0), y >= 2)
+
+        def first_half():
+            pass_token(3)
+            weights()
+            multiply(0)
+
+        if SPLIT:
+            pl.when(soon)(first_half)
+            for zz in SPLIT:
+                pl.when(z == zz)(functools.partial(run, pass_on(zz)[SPLIT[zz] :]))
+        pl.when(jnp.logical_not(soon))(first_half)
+        multiply(1)
 
         arrived(y_in.at[0:7], "t", "y")
         total = y_in[0].astype(F32)
@@ -557,7 +587,8 @@
             pltpu.SemaphoreType.DMA((N_LOCAL,)),
             pltpu.SemaphoreType.REGULAR,
             pltpu.SemaphoreType.REGULAR,
-            pltpu.SemaphoreType.REGULAR((NY // 2,)),
+            pltpu.SemaphoreType.REGULAR,
+            pltpu.SemaphoreType.REGULAR((3,)),
         ],
         compiler_params=pltpu.CompilerParams(
             collective_id=0, has_side_effects=True, vmem_limit_bytes=60 * 2**20

time: 43.8 us -> 40 us (0.913)
  Pallas kernels: 43 us -> 39.2 us
    pallas_call x1, Pallas kernels: 42.2 us -> 38.4 us  [per_device(): pl.pallas_call(kernel, out_shape=tuple((pltpu.VMEM(s.shape, s.dtype) for...]
where the time goes in v9:
time: 40 us; the launch traced here: 39.9 us
  Pallas kernels  39.2 us (98%)
  between operations  0.64 us (2%)
    pallas_call x1, Pallas kernels, per_device(): pl.pallas_call(kernel, out_shape=tuple((pltpu.VMEM(s.shape, s.dtype) for...  38.4 us
    pallas_call x1, Pallas kernels, per_device(): pl.pallas_call(store, out_shape=shapes, in_specs=[any_space] * 3, out_spe...  0.86 us

profile of v9, /device:TPU:1, one launch (start us, length us, event | category | flops | bytes accessed | tf_op | source)
XLA Modules:
  0.0 39.9 jit_solution(16547522527807653442)
XLA Ops:
  0.6 38.4 %shard_map.76 = (f32[16,4608]{1,0:T(8,128)S(1)}, f32[16,4608]{1,0:T(8,128)S(1)}, bf16[6,4,16,128]{3,2,1,0:T(8,128)(2,1)S(1)}) custom-call(bf16[8,16,4608]{2,1,0:T(8,128)(2,1)} %bitcast.5, f32[8,16,4608]{2,1,0:T(8,128)} %bitcast.4, f32[16,4608]{1,0:T(8,128)} %prm_hbm.1, f32[16,4608]{1,0:T(8,128)} %mom_hbm.1, bf16[4,16,4608]{2,1,0:T(8,128)(2,1)} %bitcast.6), custom_call_target="tpu_custom_call" | custom-call | tf_op jit(solution)/shard_map/pallas_call | solution.py:560
  39.0 0.9 %shard_map.77 = (f32[16,4608]{1,0:T(8,128)}, f32[16,4608]{1,0:T(8,128)}, bf16[6,4,16,128]{3,2,1,0:T(8,128)(2,1)}) custom-call(f32[16,4608]{1,0:T(8,128)S(1)} %get-tuple-element.9.a, f32[16,4608]{1,0:T(8,128)S(1)} %get-tuple-element.10.b, bf16[6,4,16,128]{3,2,1,0:T(8,128)(2,1)S(1)} %get-tuple-element.11.c), custom_call_target="tpu_custom_call" | custom-call | tf_op jit(solution)/shard_map/pallas_call | solution.py:603

commit v10 on v9

--- a/solution.py
+++ b/solution.py
@@ -19,37 +19,38 @@
 EARLY = 6
 ORDER = (("P", 0), ("P", 1), ("O", 0), ("O", 1))
 TREE = {
-    0: {0: (1, 11,), 1: (2,), 2: (3,), 3: (4,), 4: (5,), 5: (6,), 8: (9, 7,), 9: (10,), 11: (8,)},
-    1: {0: (11,), 1: (2, 0,), 2: (3,), 3: (4,), 4: (5,), 5: (6,), 7: (8,), 9: (10, 7,), 11: (9,)},
-    2: {0: (11,), 2: (3, 0, 1,), 3: (4,), 4: (5,), 5: (6,), 6: (7,), 9: (8,), 10: (9,), 11: (10,)},
-    3: {0: (11,), 3: (0, 2, 4, 1,), 4: (5,), 5: (6,), 6: (7,), 7: (8,), 10: (9,), 11: (10,)},
-    4: {0: (1, 11,), 2: (0, 3,), 4: (5, 2,), 5: (6,), 6: (7,), 7: (8,), 8: (9,), 11: (10,)},
-    5: {2: (1,), 3: (0, 2,), 5: (3, 4, 6,), 6: (7,), 7: (10, 8,), 8: (9,), 10: (11,)},
-    6: {0: (11,), 1: (2, 0,), 2: (3,), 4: (1, 5,), 6: (4, 7,), 7: (8,), 8: (9,), 9: (10,)},
-    7: {4: (5, 2, 3,), 7: (4, 6, 10,), 9: (8,), 10: (9, 11, 0, 1,)},
-    8: {0: (1, 11,), 3: (2,), 5: (6, 3, 4,), 6: (7,), 8: (9, 5,), 9: (0,), 11: (10,)},
-    9: {0: (1,), 3: (2, 4,), 6: (3, 5, 7,), 7: (8,), 9: (11, 6,), 11: (0, 10,)},
-    10: {0: (11,), 1: (0, 2,), 2: (3,), 3: (4,), 6: (5,), 7: (6,), 8: (7,), 10: (1, 9, 8,)},
-    11: {1: (0, 2,), 2: (3,), 5: (4,), 7: (6,), 8: (7, 5,), 10: (9,), 11: (8, 1, 10,)},
+    0: {0: (1, 11,), 1: (2,), 2: (3,), 3: (4,), 4: (5,), 7: (6,), 9: (7, 8, 10,), 11: (9,)},
+    1: {0: (11,), 1: (2, 0,), 2: (3,), 3: (4,), 4: (5,), 5: (6,), 6: (7,), 9: (8,), 10: (9,), 11: (10,)},
+    2: {0: (11,), 2: (0, 1, 3,), 3: (4,), 4: (5,), 5: (6,), 6: (7,), 9: (8,), 10: (9,), 11: (10,)},
+    3: {0: (11,), 1: (0,), 3: (1, 2, 4,), 4: (5,), 5: (6,), 6: (7,), 7: (8,), 10: (9,), 11: (10,)},
+    4: {0: (11, 1,), 2: (0,), 4: (2, 3, 5,), 5: (6,), 6: (7,), 7: (9, 8,), 11: (10,)},
+    5: {0: (11,), 1: (0, 2,), 3: (1, 4,), 5: (3, 6,), 6: (7,), 7: (8,), 8: (9,), 11: (10,)},
+    6: {1: (0,), 3: (1, 2,), 4: (3, 5,), 6: (7, 4,), 7: (8, 9,), 9: (10,), 10: (11,)},
+    7: {3: (4, 2, 1,), 5: (3, 6,), 7: (5, 9,), 8: (10,), 9: (8, 11,), 11: (0,)},
+    8: {0: (1, 11,), 3: (2,), 4: (3, 5,), 6: (4,), 8: (6, 10,), 9: (7,), 10: (0, 9,)},
+    9: {1: (2, 0,), 2: (3,), 4: (5,), 6: (4,), 8: (6, 7,), 9: (8, 11,), 11: (1, 10,)},
+    10: {0: (1,), 1: (2,), 2: (3,), 5: (4, 6,), 7: (5,), 8: (7, 9,), 9: (11,), 10: (0, 8,)},
+    11: {1: (0, 2,), 2: (3,), 5: (4,), 6: (5, 7,), 8: (9, 6,), 10: (8,), 11: (10, 1,)},
 }
 WAITS = (
-    (1, 3, 10, 6, 8, 4, 5, -1, 7, 12, 18, 9, 11, 14, 15, 16, 13, 17, 19, 32, 36, 34, 35, 38, 33, 40, 41, 43, 37, 42, 39, 25, 24, 27, 26),
-    (5, 7, 0, 3, 2, 1, 46, 40, 41, 43, 47, 44, 45, 42, 26, 25, 24, 27),
-    (9, 5, 6, 4, 0, 11, 7, 16, 3, 1, 18, 2, 17, 19, 40, 46, 41, 43, 47, 45, 22, 20, 42, 26, 21, 44, 25, 23, 24, 27),
-    (9, 13, 5, 8, 11, 15, 10, 20, 6, 4, 7, 0, 21, 22, 3, 2, 1, 23, 32, 36, 34, 40, 37, 43, 35, 38, 41, 33, 42, 39),
-    (14, 17, 12, 19, 13, 9, 5, 24, 26, 11, 8, 15, 10, 25, 27, 28, 7, 4, 3, 30, 0, 1, 2, 6, 31, 29),
-    (-1, 21, 23, 19, 16, 14, 18, 34, 12, 32, 17, 9, 13, 10, 35, 33, 15, 11, 8, 4, 7, 0, 3, 5, 1, 2, 6, 44, 47, 46, 45),
-    (25, 27, 20, 21, 23, 36, 22, 19, 16, 34, 37, 14, 18, 17, 38, 12, 35, 32, 10, 39, 15, 13, 11, 40, 8, 9, 33, 42, 41, 43),
-    (24, 27, 25, 31, 26, 29, 21, 42, 20, 40, 19, 23, 22, 36, 16, 44, 41, 18, 43, 17, 37, 46, 45, 14, 47, 38, 12, 15, 39, 13, 5, 7, 4, 6),
-    (35, 33, 40, 42, 44, 25, 41, 47, 27, 24, 43, 26, 46, 45, 2, 0, 20, 3, 1, 21, 23, 22, 19, 18, 17, 16),
-    (37, 32, 34, 39, 35, 33, 25, 30, 27, 28, 5, 24, 7, 4, 31, 26, 2, 6, 0, 29, 3, 1, 8, 10, 9, 11),
-    (41, 43, 30, 28, 46, 31, 47, 29, 44, 8, 12, 10, 23, 45, 15, 21, 20, 9, 11, 22, 14, 13),
-    (45, 47, 36, 38, 2, 3, 1, 6, 0, 10, 37, 4, 5, 7, 8, 12, 39, 15, 9, 13, 11, 14, 32, 17, 16, 19, 33, 35, 34, 18),
+    (-1, 1, 4, 3, 14, 10, 7, 9, 5, 40, 6, 8, 11, 12, 15, 42, 13, 43, 18, 41, 16, 22, 17, 21, 19, 32, 20, 34, 33, 23, 35),
+    (5, 7, 2, 0, 14, 12, 15, 13, 44, 20, 1, 46, 45, 3, 22, 21, 47, 23, 42, 24, 26, 36, 38, 37, 39, 43, 25, 41, 40, 27),
+    (4, 7, 5, 6, 2, 9, 0, 11, 16, 18, 17, 19, 44, 1, 3, 46, 45, 47, 36, 42, 38, 39, 37, 41, 40, 43),
+    (13, 15, 8, 6, 20, 10, 22, 4, 5, 9, 7, 2, 21, 11, 23, 24, 0, 26, 28, 25, 27, 30, 29, 31, 1, 3, 34, 32, 35, 33),
+    (19, 17, 13, 15, 24, 26, 12, 14, 25, 27, 8, 9, 10, 4, 11, 7, 5, 6, 32, 2, 34, 35, 33, 38, 0, 36, 1, 3, 39, 37),
+    (-1, 21, 23, 17, 18, 28, 16, 13, 30, 19, 29, 15, 12, 14, 31, 9, 8, 10, 4, 11, 7, 42, 40, 6, 5, 43, 41, 46, 44, 45, 47),
+    (25, 27, 34, 22, 21, 32, 35, 18, 17, 23, 33, 19, 16, 20, 14, 38, 12, 13, 36, 15, 37, 9, 39, 10, 8, 11, 46, 44, 45, 5, 4, 47, 6, 7),
+    (29, 31, 27, 26, 24, 40, 42, 25, 21, 22, 43, 41, 23, 18, 17, 19, 20, 16, 13, 12, 15, 1, 14, 0, 2, 3),
+    (35, 33, 40, 42, 36, 38, 43, 41, 37, 39, 46, 28, 44, 45, 21, 29, 47, 30, 22, 23, 20, 31),
+    (37, 39, 29, 28, 31, 30, 1, 27, 0, 24, 42, 25, 43, 40, 2, 3, 26, 32, 41, 33, 34, 35, 9, 5, 8, 4, 11, 6, 10, 7),
+    (43, 41, 46, 44, 45, 47, 32, 34, 33, 35, 9, 6, 5, 8, 4, 11, 10, 14, 7, 27, 12, 13, 15, 24, 25, 26),
+    (45, 47, 0, 1, 2, 36, 38, 37, 39, 9, 4, 3, 6, 5, 8, 7, 29, 12, 11, 10, 31, 28, 14, 30, 13, 16, 15, 18, 19, 17, 20, 22, 21, 23),
 )
 LINKS = {0: NZ - 1, EARLY - 1: EARLY}
-FAR_FIRST, SPLIT = (), {}
-SHARED = 49
-N_RECV, N_SEND, N_LOCAL = SHARED + 6, 10, 6
+FAR = (1, 1, 1, 0, 0, 0, 1, 1, 1, 0, 0, 0)
+SOON = 5
+SHARED = max(len(order) for order in WAITS)
+N_RECV, N_SEND, N_LOCAL = SHARED + 9, 7, 6
 
 
 class Keys:
@@ -90,14 +91,17 @@
 
     w_dev, h_dev, me = dev(x, 0, y, z), dev(x, 1, y, z), dev(x, core, y, z)
 
-    keys, sk, lk = {group: Keys() for group in "wpt"}, Keys(), Keys()
+    keys, sk, lk = {group: Keys() for group in "wt"}, {core_: Keys() for core_ in (0, 1)}, Keys()
 
     def rsem(group, *key):
+        if group == "p":
+            zz, typ, src, kc = key
+            return recv_sem.at[WAITS[zz].index(src * 4 + kc * 2 + "AB".index(typ))]
         at = keys[group](*key)
         return recv_sem.at[SHARED + at if group == "t" else at]
 
     def ssem(group):
-        return send_sem.at[sk(group)]
+        return send_sem.at[sk[0 if group in ("rs", "ag", "sum") else 1](group)]
 
     def send(src, dst, key, to, group):
         pltpu.make_async_remote_copy(
@@ -142,6 +146,11 @@
 
     def p_dev(y_, zz):
         return dev(x, 1, y_, zz)
+
+    def turn(src, zz):
+        if src // HALF == zz // HALF:
+            return 0
+        return 1 if src % HALF // 3 == FAR[zz] else 2
 
     def senders(zz):
         found = {(1, zz): mate, (2, zz): jnp.where(lo == 1, yat(1), yat(-1))}
@@ -182,8 +191,9 @@
     @pl.when(core == 0)
     def _():
         load_chunk(0)
-        for d in (1, -1):
+        for d in (-1, 1):
             greet(dev(xat(d), 0, y, z))
+        for d in (-1, 1):
             greet(dev(xat(d), 0, mate, z))
         greet(dev(x, 0, mate, z))
 
@@ -296,7 +306,7 @@
         for i in (2, 1, 3):
             gather(*block(i), False)
         for i in range(4):
-            send(sum_s.at[i], sum_s.at[i], ("p", "sum"), h_dev, "sum")
+            send(sum_s.at[i], sum_s.at[i], ("t", "sum"), h_dev, "sum")
 
         relay(0, 1)
         relay(1, 1)
@@ -319,12 +329,12 @@
     def hop(typ, src, kc, zz, to):
         ref = pb.at[lane[typ], src, kc]
         target = dev(x, 1, y, to)
-        key = ("p", "z", typ, src, kc) if TREE[src].get(to) else ("t", "in", src // HALF == to // HALF)
+        key = ("p", to, typ, src, kc) if TREE[src].get(to) else ("t", "in", turn(src, to))
         send(ref, ref, key, target, "twin" if src == zz else "relay")
 
     def start(kc, zz, to):
         ref = pb.at[lo, zz, kc]
-        key = ("p", "z", "A", zz, kc) if TREE[zz].get(to) else ("t", "in", zz // HALF == to // HALF)
+        key = ("p", to, "A", zz, kc) if TREE[zz].get(to) else ("t", "in", turn(zz, to))
         send(ref, ref, key, dev(x, 1, y, to), "own")
 
     def item(code):
@@ -346,7 +356,7 @@
                 to = p_dev(y, early_plane)
                 pl.semaphore_signal(go_late, inc=1, device_id=to, device_id_type=MESH)
         for kc in (0, 1):
-            send(b_send.at[kc], pb.at[lo, zz, kc], ("p", "z", "B", zz, kc), dev(x, 1, mate, zz), "own")
+            send(b_send.at[kc], pb.at[lo, zz, kc], ("p", zz, "B", zz, kc), dev(x, 1, mate, zz), "own")
             for to in TREE[zz][zz]:
                 if not (zz < EARLY <= to):
                     start(kc, zz, to)
@@ -362,7 +372,7 @@
                         start(kc, zz, to)
 
         def one(typ, src, kc, targets):
-            arrived(pb.at[lane[typ], src, kc], "p", "z", typ, src, kc)
+            arrived(pb.at[lane[typ], src, kc], "p", zz, typ, src, kc)
             for to in targets:
                 hop(typ, src, kc, zz, to)
 
@@ -402,13 +412,12 @@
         def push(i):
             send(out_s.at[i], out_s.at[i], ("w", "push", i), w_dev, "push")
 
-        prepare(0)
-
-        @pl.when(jnp.logical_not(late))
-        def _():
-            prepare(1)
-            prepare(2)
-            prepare(3)
+        soon = z < SOON
+
+        @pl.when(soon)
+        def _():
+            for i in range(4):
+                prepare(i)
 
         for zz in range(NZ):
             pl.when(z == zz)(lambda zz=zz: begin(zz))
@@ -418,15 +427,14 @@
         def _():
             pl.semaphore_wait(go, 1)
 
-        @pl.when(jnp.logical_not(late))
+        @pl.when(soon)
         def _():
             for i in range(4):
                 push(i)
 
-        @pl.when(late)
-        def _():
-            push(0)
-            for i in (1, 2, 3):
+        @pl.when(jnp.logical_not(soon))
+        def _():
+            for i in range(4):
                 prepare(i)
                 push(i)
 
@@ -435,78 +443,96 @@
         send(q_s, q_s, ("w", "q"), w_dev, "q")
         for zz in range(NZ):
             steps = pass_on(zz)
-            pl.when(z == zz)(functools.partial(run, steps[: SPLIT.get(zz, len(steps))]))
+            pl.when(z == zz)(functools.partial(run, steps))
 
         near = z // HALF
-        far_first = functools.reduce(jnp.logical_or, [z == zz for zz in FAR_FIRST], z < 0)
-
-        def weights():
-            for kc in (0, 1):
-                arrived(w.at[kc], "t", "w", kc)
-                w_t[kc] = w[kc].reshape(256, KC).T
+        first = sum(jnp.where(z == zz, FAR[zz], 0) for zz in range(NZ))
+        y_at = SHARED + keys["t"]("y", 0)
+        assert keys["t"]("y", 1) == y_at - SHARED + 1
+
+        pass_token(3)
+        for kc in (0, 1):
+            arrived(w.at[kc], "t", "w", kc)
+            w_t[kc] = w[kc].reshape(256, KC).T
 
         def wait_blocks(zz, phase):
-            want_near = (phase == 0) != (zz in FAR_FIRST)
-            stop = [
-                src for src in TREE
-                if src != zz and (src // HALF == zz // HALF) == want_near and not TREE[src].get(zz)
-            ]
+            stop = [src for src in TREE if src != zz and turn(src, zz) == phase and not TREE[src].get(zz)]
             if stop:
-                arrived(pb.at[:, 0 : len(stop)], "t", "in", want_near)
+                arrived(pb.at[:, 0 : len(stop)], "t", "in", phase)
+
+        def put(src, dst, c, to):
+            pltpu.make_async_remote_copy(
+                src_ref=src, dst_ref=dst, send_sem=ssem("y"), recv_sem=recv_sem.at[y_at + c],
+                device_id=dev(x, 1, to, z), device_id_type=MESH,
+            ).start()
 
         def multiply(phase):
-            h = jnp.where(far_first, 1 - near, near)
-            if phase:
-                h = 1 - h
+            h = 1 - near if phase else near
+            q = (None, first, 1 - first)[phase]
+            planes = HALF // 2 if phase else HALF
             for zz in range(NZ):
                 pl.when(z == zz)(functools.partial(wait_blocks, zz, phase))
-            acc = jnp.zeros((2 * HALF * 16, 256), F32)
+            acc = jnp.zeros((2 * planes * 16, 256), F32)
             for kc in (0, 1):
-                rows = pb[:, pl.ds(h * HALF, HALF), kc].reshape(2 * HALF * 16, KC)
+                at = h * HALF + (q * planes if phase else 0)
+                rows = pb[:, pl.ds(at, planes), kc].reshape(2 * planes * 16, KC)
                 acc += jnp.dot(rows, w_t[kc], preferred_element_type=F32)
             for lp in (0, 1):
                 for lw in (0, 1):
-                    piece = acc[lp * 96 : lp * 96 + 96, lw * 128 : lw * 128 + 128]
-                    part[phase, lp, lw] = piece.astype(BF16).reshape(HALF, 16, 128)
+                    n = planes * 16
+                    piece = acc[lp * n : lp * n + n, lw * 128 : lw * 128 + 128].astype(BF16)
+                    if phase:
+                        part[1, lp, lw, q] = piece.reshape(3, 16, 128)
+                    else:
+                        part[0, lp, lw] = piece.reshape(2, 3, 16, 128)
             for d in (4, 3, 5, 2, 6, 1, 7):
                 to = yat(d)
 
                 @pl.when(to // 2 % 2 == h)
                 def _():
-                    send(part.at[phase, to // 4, to % 2], y_in.at[y], ("t", "y"), dev(x, 1, to, z), "y")
+                    if phase:
+                        put(part.at[1, to // 4, to % 2, q], y_in.at[q, y], q, to)
+                    else:
+                        put(part.at[0, to // 4, to % 2], y_in.at[:, y], 0, to)
 
             @pl.when(y // 2 % 2 == h)
             def _():
-                y_in[y] = part[phase, y // 4, y % 2]
-
-        soon = jnp.logical_and(functools.reduce(jnp.logical_or, [z == zz for zz in SPLIT], z < 0), y >= 2)
-
-        def first_half():
-            pass_token(3)
-            weights()
-            multiply(0)
-
-        if SPLIT:
-            pl.when(soon)(first_half)
-            for zz in SPLIT:
-                pl.when(z == zz)(functools.partial(run, pass_on(zz)[SPLIT[zz] :]))
-        pl.when(jnp.logical_not(soon))(first_half)
-        multiply(1)
-
-        arrived(y_in.at[0:7], "t", "y")
-        total = y_in[0].astype(F32)
-        for i in range(1, NY):
-            total += y_in[i].astype(F32)
-        outb[:, x] = total.astype(BF16)
-        mine = outb.at[:, x]
-        for d in (2, 1, 3):
-            for cc in (1, 0):
-                send(mine, mine, ("t", "out"), dev(xat(d), cc, y, z), "out")
-        send(mine, mine, ("t", "out"), dev(x, 0, y, z), "out")
+                if phase:
+                    y_in[q, y] = part[1, y // 4, y % 2, q]
+                else:
+                    y_in[:, y] = part[0, y // 4, y % 2]
+
+        for phase in (0, 1, 2):
+            multiply(phase)
+
+        def share(c, like, quarters, at):
+            pltpu.make_async_remote_copy(
+                src_ref=like, dst_ref=like, send_sem=send_sem.at[0], recv_sem=recv_sem.at[y_at + c],
+                device_id=me, device_id_type=MESH,
+            ).wait_recv()
+            for q in quarters:
+                total = y_in[q, 0].astype(F32)
+                for i in range(1, NY):
+                    total += y_in[q, i].astype(F32)
+                outb[pl.ds(3 * q, 3), x] = total.astype(BF16)
+            mine = outb.at[at, x]
+            for d in (2, 1, 3):
+                for cc in (1, 0):
+                    send(mine, mine, ("t", "out"), dev(xat(d), cc, y, z), "out")
+            send(mine, mine, ("t", "out"), dev(x, 0, y, z), "out")
+
+        @pl.when(y // 2 % 2 == near)
+        def _():
+            share(0, y_in.at[:, 0:7], (0, 1), slice(None))
+
+        @pl.when(y // 2 % 2 != near)
+        def _():
+            for c in (first, 1 - first):
+                share(c, y_in.at[0, 0:7], (c,), pl.ds(3 * c, 3))
 
     @pl.when(core == 1)
     def _():
-        arrived(sum_s, "p", "sum")
+        arrived(sum_s, "t", "sum")
         for i, (kind, kc) in enumerate(ORDER):
             at = columns(kind, kc)
             avg = sum_s[i]
@@ -526,16 +552,16 @@
 
     @pl.when(core == 1)
     def _():
-        sent(y_in.at[0:7], "y")
-        sent(y_in.at[0:7], "out")
-        arrived(y_in.at[0:3], "t", "out")
+        sent(y_in.at[:, 0:7], "y")
+        sent(y_in.at[:, 0:7], "out")
+        arrived(y_in.at[:, 0:3], "t", "out")
 
     @pl.when(core == 0)
     def _():
-        arrived(y_in.at[0:4], "t", "out")
-
-    assert max(len(keys[g].at) for g in "wp") <= SHARED and len(keys["t"].at) <= N_RECV - SHARED
-    assert len(sk.at) <= N_SEND and len(lk.at) <= N_LOCAL
+        arrived(y_in.at[:, 0:4], "t", "out")
+
+    assert len(keys["w"].at) <= SHARED and len(keys["t"].at) <= N_RECV - SHARED
+    assert max(len(k.at) for k in sk.values()) <= N_SEND and len(lk.at) <= N_LOCAL
 
 
 def store(a, b, c, a_out, b_out, c_out, sem):
@@ -580,8 +606,8 @@
             pltpu.VMEM((2, 2, 2, 16, KC), BF16),
             pltpu.VMEM((2, NZ, 2, 16, KC), BF16),
             pltpu.VMEM((2, 16, KC), BF16),
-            pltpu.VMEM((2, 2, 2, HALF, 16, 128), BF16),
-            pltpu.VMEM((NY, HALF, 16, 128), BF16),
+            pltpu.VMEM((2, 2, 2, 2, 3, 16, 128), BF16),
+            pltpu.VMEM((2, NY, 3, 16, 128), BF16),
             pltpu.SemaphoreType.DMA((N_SEND,)),
             pltpu.SemaphoreType.DMA((N_RECV,)),
             pltpu.SemaphoreType.DMA((N_LOCAL,)),

time: 40 us -> 38.7 us (0.968)
  Pallas kernels: 39.2 us -> 37.6 us
    pallas_call x1, Pallas kernels: 38.4 us -> 36.7 us  [per_device(): pl.pallas_call(kernel, out_shape=tuple((pltpu.VMEM(s.shape, s.dtype) for...]
where the time goes in v10:
time: 38.7 us; the launch traced here: 38.2 us
  Pallas kernels  37.6 us (97%)
  between operations  0.64 us (2%)
    pallas_call x1, Pallas kernels, per_device(): pl.pallas_call(kernel, out_shape=tuple((pltpu.VMEM(s.shape, s.dtype) for...  36.7 us
    pallas_call x1, Pallas kernels, per_device(): pl.pallas_call(store, out_shape=shapes, in_specs=[any_space] * 3, out_spe...  0.86 us

profile of v10, /device:TPU:1, one launch (start us, length us, event | category | flops | bytes accessed | tf_op | source)
XLA Modules:
  0.0 38.2 jit_solution(11712158347462813840)
XLA Ops:
  0.6 36.7 %shard_map.76 = (f32[16,4608]{1,0:T(8,128)S(1)}, f32[16,4608]{1,0:T(8,128)S(1)}, bf16[6,4,16,128]{3,2,1,0:T(8,128)(2,1)S(1)}) custom-call(bf16[8,16,4608]{2,1,0:T(8,128)(2,1)} %bitcast.5, f32[8,16,4608]{2,1,0:T(8,128)} %bitcast.4, f32[16,4608]{1,0:T(8,128)} %prm_hbm.1, f32[16,4608]{1,0:T(8,128)} %mom_hbm.1, bf16[4,16,4608]{2,1,0:T(8,128)(2,1)} %bitcast.6), custom_call_target="tpu_custom_call" | custom-call | tf_op jit(solution)/shard_map/pallas_call | solution.py:586
  37.3 0.9 %shard_map.77 = (f32[16,4608]{1,0:T(8,128)}, f32[16,4608]{1,0:T(8,128)}, bf16[6,4,16,128]{3,2,1,0:T(8,128)(2,1)}) custom-call(f32[16,4608]{1,0:T(8,128)S(1)} %get-tuple-element.9.a, f32[16,4608]{1,0:T(8,128)S(1)} %get-tuple-element.10.b, bf16[6,4,16,128]{3,2,1,0:T(8,128)(2,1)S(1)} %get-tuple-element.11.c), custom_call_target="tpu_custom_call" | custom-call | tf_op jit(solution)/shard_map/pallas_call | solution.py:629

commit v11 on v10

--- a/solution.py
+++ b/solution.py
@@ -27,10 +27,10 @@
     5: {0: (11,), 1: (0, 2,), 3: (1, 4,), 5: (3, 6,), 6: (7,), 7: (8,), 8: (9,), 11: (10,)},
     6: {1: (0,), 3: (1, 2,), 4: (3, 5,), 6: (7, 4,), 7: (8, 9,), 9: (10,), 10: (11,)},
     7: {3: (4, 2, 1,), 5: (3, 6,), 7: (5, 9,), 8: (10,), 9: (8, 11,), 11: (0,)},
-    8: {0: (1, 11,), 3: (2,), 4: (3, 5,), 6: (4,), 8: (6, 10,), 9: (7,), 10: (0, 9,)},
+    8: {0: (1, 11,), 3: (2,), 4: (3, 5,), 6: (4,), 8: (6, 10, 9,), 9: (7,), 10: (0,)},
     9: {1: (2, 0,), 2: (3,), 4: (5,), 6: (4,), 8: (6, 7,), 9: (8, 11,), 11: (1, 10,)},
     10: {0: (1,), 1: (2,), 2: (3,), 5: (4, 6,), 7: (5,), 8: (7, 9,), 9: (11,), 10: (0, 8,)},
-    11: {1: (0, 2,), 2: (3,), 5: (4,), 6: (5, 7,), 8: (9, 6,), 10: (8,), 11: (10, 1,)},
+    11: {1: (0, 2,), 2: (3,), 5: (4,), 6: (7, 5,), 8: (9, 6,), 10: (8,), 11: (10, 1,)},
 }
 WAITS = (
     (-1, 1, 4, 3, 14, 10, 7, 9, 5, 40, 6, 8, 11, 12, 15, 42, 13, 43, 18, 41, 16, 22, 17, 21, 19, 32, 20, 34, 33, 23, 35),
@@ -42,12 +42,13 @@
     (25, 27, 34, 22, 21, 32, 35, 18, 17, 23, 33, 19, 16, 20, 14, 38, 12, 13, 36, 15, 37, 9, 39, 10, 8, 11, 46, 44, 45, 5, 4, 47, 6, 7),
     (29, 31, 27, 26, 24, 40, 42, 25, 21, 22, 43, 41, 23, 18, 17, 19, 20, 16, 13, 12, 15, 1, 14, 0, 2, 3),
     (35, 33, 40, 42, 36, 38, 43, 41, 37, 39, 46, 28, 44, 45, 21, 29, 47, 30, 22, 23, 20, 31),
-    (37, 39, 29, 28, 31, 30, 1, 27, 0, 24, 42, 25, 43, 40, 2, 3, 26, 32, 41, 33, 34, 35, 9, 5, 8, 4, 11, 6, 10, 7),
+    (37, 39, 29, 28, 31, 30, 1, 27, 0, 24, 42, 25, 43, 40, 2, 3, 32, 41, 26, 33, 34, 35, 9, 5, 8, 4, 11, 6, 10, 7),
     (43, 41, 46, 44, 45, 47, 32, 34, 33, 35, 9, 6, 5, 8, 4, 11, 10, 14, 7, 27, 12, 13, 15, 24, 25, 26),
     (45, 47, 0, 1, 2, 36, 38, 37, 39, 9, 4, 3, 6, 5, 8, 7, 29, 12, 11, 10, 31, 28, 14, 30, 13, 16, 15, 18, 19, 17, 20, 22, 21, 23),
 )
 LINKS = {0: NZ - 1, EARLY - 1: EARLY}
-FAR = (1, 1, 1, 0, 0, 0, 1, 1, 1, 0, 0, 0)
+FAR = (1, 1, 0, 0, 0, 0, 1, 1, 1, 0, 0, 0)
+TURN = {0: 25, 2: 21}
 SOON = 5
 SHARED = max(len(order) for order in WAITS)
 N_RECV, N_SEND, N_LOCAL = SHARED + 9, 7, 6
@@ -377,6 +378,8 @@
                 hop(typ, src, kc, zz, to)
 
         for n, code in enumerate(WAITS[zz]):
+            if n == TURN.get(zz):
+                steps.append(weights_soon)
             if n in (count // 3, 2 * count // 3):
                 steps.append(functools.partial(pass_token, 1 if n == count // 3 else 2))
             if code < 0:
@@ -391,6 +394,16 @@
             steps.append(functools.partial(one, typ, src, kc, [to for to in TREE[src][zz] if to not in wait]))
         return steps
 
+    def weights():
+        for kc in (0, 1):
+            arrived(w.at[kc], "t", "w", kc)
+            w_t[kc] = w[kc].reshape(256, KC).T
+
+    turned = jnp.logical_or(jnp.logical_and(z == 0, y >= 2), z == 2)
+
+    def weights_soon():
+        pl.when(turned)(weights)
+
     def run(steps):
         for step in steps:
             step()
@@ -451,9 +464,7 @@
         assert keys["t"]("y", 1) == y_at - SHARED + 1
 
         pass_token(3)
-        for kc in (0, 1):
-            arrived(w.at[kc], "t", "w", kc)
-            w_t[kc] = w[kc].reshape(256, KC).T
+        pl.when(jnp.logical_not(turned))(weights)
 
         def wait_blocks(zz, phase):
             stop = [src for src in TREE if src != zz and turn(src, zz) == phase and not TREE[src].get(zz)]

time: 38.7 us -> 38.3 us (0.990)
  Pallas kernels: 37.6 us -> 37.2 us
where the time goes in v11:
time: 38.3 us; the launch traced here: 37.9 us
  Pallas kernels  37.2 us (97%)
  between operations  0.64 us (2%)
    pallas_call x1, Pallas kernels, per_device(): pl.pallas_call(kernel, out_shape=tuple((pltpu.VMEM(s.shape, s.dtype) for...  36.4 us
    pallas_call x1, Pallas kernels, per_device(): pl.pallas_call(store, out_shape=shapes, in_specs=[any_space] * 3, out_spe...  0.86 us

profile of v11, /device:TPU:1, one launch (start us, length us, event | category | flops | bytes accessed | tf_op | source)
XLA Modules:
  0.0 37.9 jit_solution(9323096766633436643)
XLA Ops:
  0.6 36.4 %shard_map.76 = (f32[16,4608]{1,0:T(8,128)S(1)}, f32[16,4608]{1,0:T(8,128)S(1)}, bf16[6,4,16,128]{3,2,1,0:T(8,128)(2,1)S(1)}) custom-call(bf16[8,16,4608]{2,1,0:T(8,128)(2,1)} %bitcast.5, f32[8,16,4608]{2,1,0:T(8,128)} %bitcast.4, f32[16,4608]{1,0:T(8,128)} %prm_hbm.1, f32[16,4608]{1,0:T(8,128)} %mom_hbm.1, bf16[4,16,4608]{2,1,0:T(8,128)(2,1)} %bitcast.6), custom_call_target="tpu_custom_call" | custom-call | tf_op jit(solution)/shard_map/pallas_call | solution.py:597
  37.0 0.9 %shard_map.77 = (f32[16,4608]{1,0:T(8,128)}, f32[16,4608]{1,0:T(8,128)}, bf16[6,4,16,128]{3,2,1,0:T(8,128)(2,1)}) custom-call(f32[16,4608]{1,0:T(8,128)S(1)} %get-tuple-element.9.a, f32[16,4608]{1,0:T(8,128)S(1)} %get-tuple-element.10.b, bf16[6,4,16,128]{3,2,1,0:T(8,128)(2,1)S(1)} %get-tuple-element.11.c), custom_call_target="tpu_custom_call" | custom-call | tf_op jit(solution)/shard_map/pallas_call | solution.py:640
